TPU v7x, 32 devices: a whole 2x2x4 slice. The times are simulated.
32 devices in a mesh: seq: 4 (over y, x), mem: 8 (over z, core).
Axes of the slice: x: 2, y: 2, z: 4, core: 2. Of those that a mesh axis runs over, the one named last changes fastest.
Arguments:
- hidden: bfloat16 [8192, 2048], P(('seq', 'mem')), may hold values from -6 to 6
- routes: int32 [8192, 2], P(('seq', 'mem')), may hold values from 0 to 7, all different within a row; in each aligned block of 256 rows (0 to 255, 256 to 511, ...) at most 64 rows name the same one
- gate_levels: int32 [8192, 2], P(('seq', 'mem')), may hold values from 1 to 255
- query_weight: bfloat16 [2048, 1024], P('seq'), may hold values from -0.125 to 0.125
- key_weight: bfloat16 [8, 2048, 1024], P('mem', 'seq'), may hold values from -0.125 to 0.125
- value_weight: bfloat16 [8, 2048, 1024], P('mem', 'seq'), may hold values from -0.125 to 0.125
Outputs:
- mixed: bfloat16 [8192, 1024], P(('seq', 'mem'))
Inputs may be any that keep to these rules, and one draw needn't show every extreme that they name: `routes`: the two memories of a row differ. In the rows of one device no memory is named by more than 64 rows, a bound that some block reaches.
All inputs are finite; a program needn't handle non-finite values.
Results may differ from a plain program's by a relative error of at most 0.01.
Values may be sent and summed in bfloat16 or wider, within the bound.
No kernel may reach another device: no remote copies, remote signals or barrier semaphores. Data moves between devices by JAX's collectives and lax.ppermute only.
A program may use at most 128 MiB of HBM per device.

v0:
```python
import jax
import jax.numpy as jnp
from jax import lax
from jax.sharding import PartitionSpec as P

HEADS = 8
DK = 128
BLOCK = 512
CAP = 64


def entering(array, axis, join, neutral):
    place = lax.axis_index(axis)
    gathered = lax.all_gather(array.astype(jnp.bfloat16), axis)
    state = jnp.zeros_like(array) + jnp.asarray(neutral, array.dtype)

    def one(step, state):
        return join(state, lax.dynamic_index_in_dim(gathered, step, 0, False).astype(array.dtype))

    return lax.fori_loop(0, place, one, state)


def add_states(earlier, later):
    return earlier + later


def on_device(hidden, routes, gate_levels, query_weight, key_weight, value_weight):
    count = hidden.shape[0]
    model = hidden.shape[1]
    width = query_weight.shape[1]
    mem_local = key_weight.shape[0]
    experts = mem_local * lax.axis_size("mem")
    highest = lax.Precision.HIGHEST
    onehot = (routes[:, :, None] == jnp.arange(experts, dtype=jnp.int32)[None, None, :]).astype(
        jnp.int32
    )
    per_token = jnp.sum(onehot, axis=1)
    before = jnp.cumsum(per_token, axis=0) - per_token
    place = jnp.sum(onehot * before[:, None, :], axis=2)
    slots = (routes * CAP + place).reshape(-1)
    owner_of = jnp.arange(2 * count, dtype=jnp.int32) // 2
    match = jnp.arange(experts * CAP, dtype=jnp.int32)[:, None] == slots[None, :]
    source = jnp.sum(jnp.where(match, owner_of[None, :], 0), axis=1)
    filled = jnp.any(match, axis=1)
    sent_rows = jnp.where(
        filled[:, None], jnp.take(hidden, source, axis=0), jnp.zeros((), hidden.dtype)
    )
    sent_rows = sent_rows.reshape(experts, CAP, model)
    columns = hidden
    queries = jnp.dot(
        columns,
        lax.all_gather(query_weight, "seq", axis=0, tiled=True),
        preferred_element_type=jnp.float32,
    ).astype(jnp.bfloat16)
    sent_queries = jnp.where(
        filled[:, None], jnp.take(queries, source, axis=0), jnp.zeros((), queries.dtype)
    )
    sent_queries = sent_queries.reshape(experts, CAP, width)
    arrived, arrived_queries = (
        lax.all_to_all(sent_rows, "mem", split_axis=0, concat_axis=1, tiled=True),
        lax.all_to_all(sent_queries, "mem", split_axis=0, concat_axis=1, tiled=True),
    )
    length = arrived.shape[1]
    columns = arrived
    key_part = jnp.einsum(
        "mrc,mch->mrh",
        columns,
        lax.all_gather(key_weight, "seq", axis=1, tiled=True),
        preferred_element_type=jnp.float32,
    )
    value_part = jnp.einsum(
        "mrc,mch->mrh",
        columns,
        lax.all_gather(value_weight, "seq", axis=1, tiled=True),
        preferred_element_type=jnp.float32,
    )
    keys = key_part
    values = value_part
    keys = keys.astype(jnp.bfloat16)
    values = values.astype(jnp.bfloat16)
    nblocks = length // BLOCK
    shape5 = (mem_local, nblocks, BLOCK, HEADS, DK)
    q_five = arrived_queries.reshape(shape5)
    k_five = keys.reshape(shape5)
    v_five = values.reshape(shape5)
    block_states = jnp.einsum(
        "mnkhd,mnkhe->mnhde", k_five, v_five, preferred_element_type=jnp.float32
    )
    within = jnp.cumsum(block_states, axis=1) - block_states
    local_total = jnp.sum(block_states, axis=1)
    nothing = jnp.zeros_like(local_total)
    incoming = entering(local_total, "seq", add_states, nothing)
    states = (incoming[:, None] + within).reshape(mem_local * nblocks, HEADS, DK, DK)
    flat = (mem_local * nblocks, BLOCK, HEADS, DK)
    rowids = jnp.arange(BLOCK, dtype=jnp.int32)
    causal = (rowids[:, None] >= rowids[None, :]).astype(jnp.float32)

    def attend(inputs):
        q_block, k_block, v_block, state = inputs
        scores = (
            jnp.einsum("qhd,khd->hqk", q_block, k_block, preferred_element_type=jnp.float32)
            * causal[None]
        )
        local = jnp.einsum("hqk,khd->qhd", scores, v_block.astype(jnp.float32), precision=highest)
        carried = jnp.einsum("qhd,hde->qhe", q_block.astype(jnp.float32), state, precision=highest)
        reads = local + carried
        scale = lax.rsqrt(jnp.mean(reads * reads, axis=-1, keepdims=True) + 1e-06)
        return (reads * scale).astype(jnp.bfloat16)

    normed = lax.map(
        attend, (q_five.reshape(flat), k_five.reshape(flat), v_five.reshape(flat), states)
    )
    normed = normed.reshape(mem_local, length, width)
    returned = lax.all_to_all(normed, "mem", split_axis=1, concat_axis=0, tiled=True)
    returned = returned.reshape(experts * CAP, width)
    picked = jnp.take(returned, slots, axis=0).reshape(count, 2, width)
    levels = gate_levels.astype(jnp.float32)
    gates = levels / jnp.sum(levels, axis=1, keepdims=True)
    mixed = jnp.sum(gates[:, :, None] * picked.astype(jnp.float32), axis=1)
    return mixed.astype(jnp.bfloat16)


def solution(mesh):
    return jax.shard_map(
        on_device,
        mesh=mesh,
        in_specs=(
            P(("seq", "mem"), None),
            P(("seq", "mem"), None),
            P(("seq", "mem"), None),
            P("seq", None),
            P("mem", "seq", None),
            P("mem", "seq", None),
        ),
        out_specs=P(("seq", "mem"), None),
        check_vma=False,
    )
```

profile of v0, /device:TPU:0, one launch (start us, length us, event | category | flops | bytes accessed | tf_op | source)
XLA Modules:
  0.0 289.7 jit_solution(13704537950358973058)
XLA Ops:
  6.5 0.0 copy-start
  6.5 0.0 all-gather.10.cloned.1.call-start
  6.5 0.7 all-gather.10.cloned.1.call-update
  7.3 0.0 all-gather.6.cloned.1.call-start
  7.3 0.7 all-gather.6.cloned.1.call-update
  8.0 0.0 all-gather.8.cloned.1.call-start
  8.1 0.7 all-gather.8.cloned.1.call-update
  8.7 0.0 all-gather.12.cloned.1.call-start
  8.8 0.0 copy-done.5
  8.8 0.6 reduce-window.6
  9.4 0.2 slice_reduce_fusion
  9.7 0.1 bitcast_subtract_fusion
  9.8 0.1 copy.61
  9.9 0.1 reshape.211
  10.1 0.2 fusion.24
  10.3 0.2 select_reduce_fusion
  10.5 0.1 reduce_sum.67
  10.5 0.1 broadcast_in_dim.94
  10.6 0.0 copy-done
  10.6 2.5 gather_fusion
  13.1 0.3 select_select_fusion
  13.5 55.2 %all_to_all.12 = bf16[8,64,2048]{2,1,0:T(8,128)(2,1)S(1)} all-to-all(bf16[8,64,2048]{2,1,0:T(8,128)(2,1)S(1)} %select_select_fusion), channel_id=1, replica_groups=mesh['seq'=4,'mem'=8] {'mem'}, dimensions={0} | all-to-all | bytes 4194304 | tf_op jit(solution)/shard_map/all_to_all | solution.py:60
  68.7 1.4 copy-done.4
  70.0 5.5 %fusion.15 = bf16[512,1024]{1,0:T(8,128)(2,1)} fusion(bf16[512,2048]{1,0:T(8,128)(2,1)S(1)} %bitcast.80, bf16[1,2048,1024]{2,1,0:T(8,128)(2,1)} %all-gather.10.cloned.1.call-done), kind=kOutput, calls=%fused_computation.20 | convolution fusion | flops 2148007936 | bytes 7340032 | tf_op jit(solution)/shard_map/mrc,mch->mrh/dot_general | solution.py:65
  75.5 1.6 copy.74
  77.1 41.9 %all-gather.6.cloned.1.call-done = bf16[1,2048,1024]{2,1,0:T(8,128)(2,1)} async-done(((bf16[1,512,1024]{2,1,0:T(8,128)(2,1)}), bf16[1,2048,1024]{2,1,0:T(8,128)(2,1)}) %all-gather.6.cloned.1.call-update) | async-done | bytes 4194320 | tf_op jit(solution)/shard_map/all_gather | solution.py:74
  119.0 5.2 %fusion.18 = bf16[64,8,8,128]{3,2,1,0:T(8,128)(2,1)S(1)} fusion(bf16[512,2048]{1,0:T(8,128)(2,1)} %bitcast.81, bf16[1,2048,1024]{2,1,0:T(8,128)(2,1)} %all-gather.6.cloned.1.call-done), kind=kOutput, calls=%fused_computation.21 | convolution fusion | flops 2148007936 | bytes 7340032 | tf_op jit(solution)/shard_map/mrc,mch->mrh/dot_general | solution.py:71
  124.2 0.0 copy-start.2
  124.2 1.0 copy-done.2
  125.2 1.2 fusion.36
  126.3 0.0 all-gather.12.cloned.1.call-update
  126.3 47.1 %all-gather.8.cloned.1.call-done = bf16[2048,1024]{1,0:T(8,128)(2,1)} async-done(((bf16[512,1024]{1,0:T(8,128)(2,1)}), bf16[2048,1024]{1,0:T(8,128)(2,1)}) %all-gather.8.cloned.1.call-update) | async-done | bytes 4194320 | tf_op jit(solution)/shard_map/all_gather | solution.py:52
  173.5 3.4 %convolution_convert_fusion = bf16[256,1024]{1,0:T(8,128)(2,1)S(1)} fusion(bf16[256,2048]{1,0:T(8,128)(2,1)S(1)} %copy-done, bf16[2048,1024]{1,0:T(8,128)(2,1)} %all-gather.8.cloned.1.call-done), kind=kOutput, calls=%fused_computation.22 | convolution fusion | flops 1074003968 | bytes 5767168 | tf_op jit(solution)/shard_map/dot_general | solution.py:50
  176.9 2.8 gather_fusion.1
  179.7 2.4 select_select_fusion.1
  182.1 4.6 %all-to-all-start.1 = ((bf16[8,64,1024]{2,1,0:T(8,128)(2,1)}), bf16[8,64,1024]{2,1,0:T(8,128)(2,1)}, u32[]{:S(2)}, u32[]{:S(2)}) async-start(bf16[8,64,1024]{2,1,0:T(8,128)(2,1)} %select_select_fusion.1), calls=%async_computation.1 | async-start | bytes 2097152 | tf_op jit(solution)/shard_map/all_to_all | solution.py:61
  186.7 1.1 fusion.25
  187.8 13.9 %all-gather.12.cloned.1.call-done = bf16[32,128,128]{2,1,0:T(8,128)(2,1)} async-done(((bf16[8,128,128]{2,1,0:T(8,128)(2,1)}), bf16[32,128,128]{2,1,0:T(8,128)(2,1)}) %all-gather.12.cloned.1.call-update) | async-done | bytes 1048592 | tf_op jit(solution)/shard_map/all_gather | solution.py:14
  201.7 0.2 while.2
  201.9 11.5 %all-to-all-done.1 = bf16[8,64,1024]{2,1,0:T(8,128)(2,1)} async-done(((bf16[8,64,1024]{2,1,0:T(8,128)(2,1)}), bf16[8,64,1024]{2,1,0:T(8,128)(2,1)}, u32[]{:S(2)}, u32[]{:S(2)}) %all-to-all-start.1) | async-done | bytes 1048608 | tf_op jit(solution)/shard_map/all_to_all | solution.py:61
  213.4 1.5 copy.76
  214.9 1.2 fusion.30
  216.1 0.0 copy-start.1
  216.2 0.0 copy-start.3
  216.2 1.1 fusion.28
  217.2 0.1 copy-done.1
  217.4 0.3 copy-done.3
  217.7 5.5 %fusion.7 = (f32[512,8]{0,1:T(8,128)S(1)}, f32[8,128,512]{2,1,0:T(8,128)S(1)}) fusion(f32[8,128,512]{2,1,0:T(8,128)S(1)} %fusion.28, f32[8,512,512]{2,1,0:T(8,128)S(1)} %fusion.30, f32[512,512]{1,0:T(8,128)S(1)} %copy-done.1, bf16[64,8,8,128]{3,2,1,0:T(8,128)(2,1)S(1)} %copy-done.3), kind=kOutput, calls=%fused_computation.13 | convolution fusion | flops 3224891392 | bytes 14696448 | tf_op jit(solution)/shard_map/while/body/eval_jaxpr/hqk,khd->qhd/dot_general | solution.py:104
  223.2 1.3 fusion.8
  224.5 4.7 %copy.70 = bf16[1,512,1024]{2,0,1:T(2,128)(2,1)S(1)} copy(bf16[1,512,1024]{1,2,0:T(8,128)(2,1)} %bitcast.78) | data formatting | bytes 2097152 | tf_op jit(solution)/shard_map/reshape | solution.py:113
  229.2 0.5 broadcast.156
  229.8 7.8 %reduce.2 = bf16[512,1024]{1,0:T(8,128)(2,1)} reduce(bf16[512,1,1024]{2,1,0:T(2,128)(2,1)S(1)} %bitcast.77, bf16[]{:T(256)} %broadcast.156), dimensions={1}, to_apply=%bitcast.55.reduce_sub_computation | reduce | bytes 2097154
  237.5 2.6 reshape.245
  240.2 3.6 %all-to-all-start.2 = ((bf16[8,2,32768]{2,1,0:T(2,128)(2,1)}), bf16[8,2,32768]{2,1,0:T(2,128)(2,1)S(1)}, u32[]{:S(2)}, u32[]{:S(2)}) async-start(bf16[8,2,32768]{2,1,0:T(2,128)(2,1)} %reshape.245), calls=%async_computation.2 | async-start | bytes 2097152 | tf_op jit(solution)/shard_map/all_to_all | solution.py:114
  243.7 0.1 reshape.217
  243.9 0.2 copy.60
  244.1 0.0 copy-done.6
  244.1 0.1 copy.59
  244.3 26.0 %all-to-all-done.2 = bf16[8,2,32768]{2,1,0:T(2,128)(2,1)S(1)} async-done(((bf16[8,2,32768]{2,1,0:T(2,128)(2,1)}), bf16[8,2,32768]{2,1,0:T(2,128)(2,1)S(1)}, u32[]{:S(2)}, u32[]{:S(2)}) %all-to-all-start.2) | async-done | bytes 1048608 | tf_op jit(solution)/shard_map/all_to_all | solution.py:114
  270.2 3.5 %reshape.246 = bf16[512,1,1024]{2,1,0:T(2,128)(2,1)} reshape(bf16[8,2,32768]{2,1,0:T(2,128)(2,1)S(1)} %all-to-all-done.2) | data formatting | bytes 2097152
  273.7 2.0 copy.94
  275.6 2.1 gather_fusion.2
  277.7 0.4 gather.23
  278.2 5.0 %multiply_reduce_fusion = bf16[256,1024]{1,0:T(8,128)(2,1)} fusion(bf16[256,2,1024]{2,1,0:T(2,128)(2,1)S(1)} %gather.23, pred[256,2]{1,0:T(8,128)(4,1)S(1)} %copy.60, f32[256,2]{1,0:T(8,128)S(1)} %copy.59), kind=kLoop, calls=%fused_computation.15 | loop fusion | flops 1835008 | bytes 1575424 | tf_op jit(solution)/shard_map/reduce_sum | solution.py:119
  (19 shorter events, 0.2 us)
Async XLA Ops:
  6.5 4.1 %copy-start = (bf16[256,2048]{1,0:T(8,128)(2,1)S(1)}, bf16[256,2048]{1,0:T(8,128)(2,1)}, u32[]{:S(2)}) copy-start(bf16[256,2048]{1,0:T(8,128)(2,1)} %param.8) | copy-start | bytes 3145732
  6.5 2.3 copy-start.5
  6.5 62.1 %all-gather.10.cloned.1.call-start = ((), (), s32[]{:S(2)}) async-start(), calls=%async_computation.5 | async-start | bytes 5242880 | tf_op jit(solution)/shard_map/all_gather | solution.py:68
  7.3 111.8 %all-gather.6.cloned.1.call-start = ((), (), s32[]{:S(2)}) async-start(), calls=%async_computation.3 | async-start | bytes 5242880 | tf_op jit(solution)/shard_map/all_gather | solution.py:74
  8.0 165.5 %all-gather.8.cloned.1.call-start = ((), (), s32[]{:S(2)}) async-start(), calls=%async_computation.4 | async-start | bytes 5242880 | tf_op jit(solution)/shard_map/all_gather | solution.py:52
  8.7 193.0 %all-gather.12.cloned.1.call-start = ((), (), s32[]{:S(2)}) async-start(), calls=%async_computation.6 | async-start | bytes 1310720 | tf_op jit(solution)/shard_map/all_gather | solution.py:14
  68.7 1.4 copy-start.4
  124.2 1.0 copy-start.2
  182.1 31.3 %all-to-all-start.1 = ((bf16[8,64,1024]{2,1,0:T(8,128)(2,1)}), bf16[8,64,1024]{2,1,0:T(8,128)(2,1)}, u32[]{:S(2)}, u32[]{:S(2)}) async-start(bf16[8,64,1024]{2,1,0:T(8,128)(2,1)} %select_select_fusion.1), calls=%async_computation.1 | async-start | bytes 2097152 | tf_op jit(solution)/shard_map/all_to_all | solution.py:61
  216.1 1.2 copy-start.1
  216.2 1.5 copy-start.3
  237.5 6.5 %copy-start.6 = (s32[256,2]{0,1:T(2,128)S(1)}, s32[256,2]{0,1:T(2,128)}, u32[]{:S(2)}) copy-start(s32[256,2]{0,1:T(2,128)} %param.10) | copy-start | bytes 6148
  240.2 30.1 %all-to-all-start.2 = ((bf16[8,2,32768]{2,1,0:T(2,128)(2,1)}), bf16[8,2,32768]{2,1,0:T(2,128)(2,1)S(1)}, u32[]{:S(2)}, u32[]{:S(2)}) async-start(bf16[8,2,32768]{2,1,0:T(2,128)(2,1)} %reshape.245), calls=%async_computation.2 | async-start | bytes 2097152 | tf_op jit(solution)/shard_map/all_to_all | solution.py:114
Sparse Core Ops, SparseCore 0:
  9.2 55.3 all-gather.9
  66.4 52.5 all-gather.5
  120.9 52.5 all-gather.7
  175.2 26.4 all-gather.11
where the time goes:
time: 290 us
  waiting for transfers between devices  142 us (49%)
  blocking collectives  55.2 us (19%)
  local copies, waits for them, and re-layouts  28.1 us (10%)
  matrix products  23 us (8%)
  other arithmetic  19.1 us (7%)
  between operations  13.4 us (5%)
  starting transfers between devices  8.28 us (3%)
    all_to_all x1, blocking collectives, on_device(): lax.all_to_all(sent_rows, 'mem', split_axis=0, concat_axis=1, tiled=True)  55.2 us
    all_gather x1, waiting for transfers between devices, on_device(): lax.all_gather(query_weight, 'seq', axis=0, tiled=True)  47.1 us
    all_gather x1, waiting for transfers between devices, on_device(): lax.all_gather(value_weight, 'seq', axis=1, tiled=True)  41.9 us
    all_to_all x1, waiting for transfers between devices, on_device(): lax.all_to_all(normed, 'mem', split_axis=1, concat_axis=0, tiled=True)  26 us
    all_gather x1, waiting for transfers between devices, entering(): gathered = lax.all_gather(array.astype(jnp.bfloat16), axis)  13.9 us
    unnamed x19, local copies, waits for them, and re-layouts  12.9 us
    all_to_all x1, waiting for transfers between devices, on_device(): lax.all_to_all(sent_queries, 'mem', split_axis=0, concat_axis=1, tiled=True)  11.5 us
    unnamed x1, other arithmetic  7.77 us
  transfers between devices with their start and end apart: 6, of which 5 were waited for; matrix products, arithmetic and copies ran while one was open for 10% of the time, Pallas kernels for 0%

commit v1 on v0

v1 whole, which is shorter than its diff:
```python
import functools

import jax
import jax.numpy as jnp
from jax import lax
from jax.experimental import pallas as pl
from jax.experimental.pallas import tpu as pltpu
from jax.sharding import PartitionSpec as P


DK = 128
CAP = 64
LAST_HEADS = 2
LIMIT = 24 << 20
VMEM = pl.BlockSpec(memory_space=pltpu.VMEM)
SMEM = pl.BlockSpec(memory_space=pltpu.SMEM)
ANY = pl.BlockSpec(memory_space=pl.ANY)
HBM = pl.BlockSpec(memory_space=pltpu.HBM)
shape = jax.ShapeDtypeStruct
bf16 = jnp.bfloat16


def swap(array, axis, mask, forward_only=False):
    size = lax.axis_size(axis)
    pairs = [(i, i ^ mask) for i in range(size) if i < i ^ mask or not forward_only]
    return lax.ppermute(array, axis, pairs)


def contract(left, right, left_dim, right_dim):
    return lax.dot_general(
        left, right, (((left_dim,), (right_dim,)), ((), ())), preferred_element_type=jnp.float32
    )


def dispatch_kernel(here, routes, levels, hidden, table, *sent):
    count = hidden.shape[0]
    experts = len(sent)
    named = [routes[j : j + 1, :] for j in range(2)]
    memory = lax.broadcasted_iota(jnp.int32, (experts, count), 0)
    hits = [(memory == name).astype(jnp.float32) for name in named]
    rows = lax.broadcasted_iota(jnp.int32, (count, count), 0)
    cols = lax.broadcasted_iota(jnp.int32, (count, count), 1)
    earlier = jnp.where(rows < cols, 1.0, 0.0).astype(bf16)
    before = contract((hits[0] + hits[1]).astype(bf16), earlier, 1, 0)
    places = [jnp.sum(h * before, axis=0, keepdims=True).astype(jnp.int32) for h in hits]
    index = lax.broadcasted_iota(jnp.int32, (CAP, count), 0)
    crossed = [(name ^ here[1]) * CAP + place for name, place in zip(named, places)]
    for k in range(experts):
        at = index + k * CAP
        pick = jnp.where((at == crossed[0]) | (at == crossed[1]), 1.0, 0.0).astype(bf16)
        sent[k][...] = contract(pick, hidden[...], 1, 0).astype(bf16)
    slots = [(name * CAP + place).astype(jnp.float32) for name, place in zip(named, places)]
    level = levels[...].astype(jnp.float32)
    gates = level / (level[0:1, :] + level[1:2, :])
    entries = jnp.concatenate(slots + [gates, jnp.zeros((4, count), jnp.float32)], axis=0)
    table[...] = entries.T


def pack_kernel(here, query, key, value, a_out, b_out, sems, *, first, heads, a_heads):
    mine = heads // 2
    width = heads * DK
    start = first * DK
    side = here[1] & 1
    q_at = pl.multiple_of((first + side * mine) * DK, DK)
    copies = [
        pltpu.make_async_copy(key.at[0, :, pl.ds(start, width)], a_out.at[:, pl.ds(0, width)], sems.at[0]),
        pltpu.make_async_copy(value.at[0, :, pl.ds(start, width)], b_out.at[:, pl.ds(0, width)], sems.at[1]),
    ]
    a_cols = a_heads * DK
    b_cols = (mine - a_heads) * DK
    if a_cols:
        copies.append(
            pltpu.make_async_copy(
                query.at[:, pl.ds(q_at, a_cols)], a_out.at[:, pl.ds(width, a_cols)], sems.at[2]
            )
        )
    if b_cols:
        copies.append(
            pltpu.make_async_copy(
                query.at[:, pl.ds(pl.multiple_of(q_at + a_cols, DK), b_cols)],
                b_out.at[:, pl.ds(width, b_cols)],
                sems.at[3],
            )
        )
    for copy in copies:
        copy.start()
    for copy in copies:
        copy.wait()


def join_kernel(here, *refs):
    *pieces, out = refs
    for k, piece in enumerate(pieces):
        out[pl.ds(pl.multiple_of((here[1] ^ k) * CAP, CAP), CAP), :] = piece[...]


def project(x, seq, pieces, masks):
    total = None
    for piece, mask in zip(pieces, masks):
        rows = piece.shape[0]
        at = pl.multiple_of((seq ^ mask) * rows, rows)
        part = contract(x[:, pl.ds(at, rows)], piece[...], 1, 0)
        total = part if total is None else total + part
    return total


def kv_kernel(here, x, *refs, masks, heads, a_heads):
    n = len(masks[0])
    k_out, v_out, q_out, t_out, q_pack = refs[2 * n :]
    width = heads * DK
    seq = here[0]
    q_at = 0
    for pieces, own, out, extra in (
        (refs[:n], masks[0], k_out, a_heads * DK),
        (refs[n : 2 * n], masks[1], v_out, (heads // 2 - a_heads) * DK),
    ):
        part = project(x, seq, pieces, own).astype(bf16)
        out[...] = part[:, :width]
        if extra:
            q_out[:, q_at : q_at + extra] = part[:, width:]
            for piece, mask in zip(pieces, own):
                rows = piece.shape[0]
                at = pl.multiple_of((seq ^ mask) * rows, rows)
                q_pack[pl.ds(at, rows), q_at : q_at + extra] = piece[:, width:]
        q_at += extra
    for h in range(heads):
        cols = slice(h * DK, (h + 1) * DK)
        t_out[h] = contract(k_out[:, cols], v_out[:, cols], 0, 0).astype(bf16)


def attend_kernel(here, x, k, v, q_own, w_other, *refs):
    *states, out = refs
    length = x.shape[0]
    side = here[1] & 1
    mine = q_own.shape[1] // DK
    step = length // 2
    row = lax.broadcasted_iota(jnp.int32, (step, step), 0)
    col = lax.broadcasted_iota(jnp.int32, (step, step), 1)
    causal = row >= col
    q_other = contract(x[...], w_other[...], 1, 0).astype(bf16)
    for queries, group in ((q_own, side), (q_other, 1 - side)):
        for h in range(mine):
            head = group * mine + h
            cols = pl.ds(pl.multiple_of(head * DK, DK), DK)
            state = states[0][head].astype(jnp.float32)
            for other in states[1:]:
                state = state + other[head].astype(jnp.float32)
            high = state.astype(bf16)
            low = (state - high.astype(jnp.float32)).astype(bf16)
            for b in range(2):
                rows = slice(b * step, (b + 1) * step)
                q = queries[rows, h * DK : (h + 1) * DK]
                scores = jnp.where(causal, contract(q, k[rows, cols], 1, 1), 0.0).astype(bf16)
                reads = contract(scores, v[rows, cols], 1, 0)
                for e in range(b):
                    earlier = slice(e * step, (e + 1) * step)
                    scores = contract(q, k[earlier, cols], 1, 1).astype(bf16)
                    reads = reads + contract(scores, v[earlier, cols], 1, 0)
                reads = reads + contract(q, high, 1, 0) + contract(q, low, 1, 0)
                scale = lax.rsqrt(jnp.mean(reads * reads, axis=-1, keepdims=True) + 1e-06)
                out[rows, cols] = (reads * scale).astype(bf16)


def combine_kernel(table, part, *refs):
    out = refs[-1]
    count = table.shape[0]
    index = lax.broadcasted_iota(jnp.int32, (count, part.shape[0]), 1).astype(jnp.float32)
    mixed = None
    for j in range(2):
        pick = jnp.where(index == table[:, j : j + 1], 1.0, 0.0).astype(bf16)
        term = table[:, 2 + j : 3 + j] * contract(pick, part[...], 1, 0)
        mixed = term if mixed is None else mixed + term
    out[...] = mixed.astype(bf16)


def call(kernel, outs, ins, *arrays, flops=1, scratch=()):
    arrays = [
        pltpu.with_memory_space_constraint(a, pltpu.VMEM) if spec is VMEM else a
        for a, spec in zip(arrays, ins)
    ]
    return pl.pallas_call(
        kernel,
        out_shape=jax.tree.map(lambda s: pltpu.VMEM(s.shape, s.dtype), outs),
        in_specs=ins,
        out_specs=jax.tree.map(lambda _: VMEM, outs),
        scratch_shapes=scratch,
        compiler_params=pltpu.CompilerParams(vmem_limit_bytes=LIMIT),
        cost_estimate=pl.CostEstimate(flops=flops, bytes_accessed=1 << 20, transcendentals=0),
    )(*arrays)


def spread(first, bits):
    pieces, masks = [first], [0]
    for bit in bits:
        fresh = []
        for piece in pieces:
            fresh.append(swap(piece, "seq", bit))
        pieces = pieces + fresh
        masks = masks + [m ^ bit for m in masks]
    return pieces, tuple(masks)


def on_device(hidden, routes, gate_levels, query_weight, key_weight, value_weight):
    count, model = hidden.shape
    rows, width = query_weight.shape
    groups, experts = lax.axis_size("seq"), lax.axis_size("mem")
    here = jnp.stack([lax.axis_index("seq"), lax.axis_index("mem")]).astype(jnp.int32)
    bits = [1 << b for b in range(groups.bit_length() - 1)]
    length = experts * CAP
    all_heads = width // DK
    chunks = [(0, all_heads - LAST_HEADS), (all_heads - LAST_HEADS, LAST_HEADS)]

    weights = []
    for c, (first, heads) in enumerate(chunks):
        mine = heads // 2
        a_heads = (mine + 1 - c % 2) // 2
        a_cols, b_cols = (heads + a_heads) * DK, (heads + mine - a_heads) * DK
        a_first, b_first = call(
            functools.partial(pack_kernel, first=first, heads=heads, a_heads=a_heads),
            [shape((rows, a_cols), bf16), shape((rows, b_cols), bf16)],
            [SMEM, HBM, HBM, HBM],
            here,
            query_weight,
            key_weight,
            value_weight,
            scratch=[pltpu.SemaphoreType.DMA((4,))],
        )
        a_pieces, a_masks = spread(a_first, bits)
        b_pieces, b_masks = spread(b_first, bits[::-1])
        weights.append((a_pieces, b_pieces, (a_masks, b_masks), a_heads))

    table, *sent = call(
        dispatch_kernel,
        [shape((count, 8), jnp.float32)] + [shape((CAP, model), bf16)] * experts,
        [SMEM, VMEM, VMEM, VMEM],
        here,
        routes.T,
        gate_levels.T,
        hidden,
        flops=2 * count * length * model,
    )

    def route(array, k):
        return swap(array, "mem", k)

    arrived = call(
        join_kernel,
        shape((length, model), bf16),
        [SMEM] + [VMEM] * experts,
        here,
        sent[0],
        *[route(sent[k], k) for k in range(1, experts)],
    )

    out = None
    for c, (first, heads) in enumerate(chunks):
        a_pieces, b_pieces, masks, a_heads = weights[c]
        mine = heads // 2
        cols = heads * DK
        keys, values, q_own, total, q_pack = call(
            functools.partial(kv_kernel, masks=masks, heads=heads, a_heads=a_heads),
            [
                shape((length, cols), bf16),
                shape((length, cols), bf16),
                shape((length, mine * DK), bf16),
                shape((heads, DK, DK), bf16),
                shape((model, mine * DK), bf16),
            ],
            [SMEM, VMEM] + [VMEM] * (2 * groups),
            here,
            arrived,
            *a_pieces,
            *b_pieces,
            flops=4 * length * model * cols,
        )
        states = []
        for m in range(1, groups):
            states.append(swap(total, "seq", m, forward_only=True))
        w_other = swap(q_pack, "mem", 1)
        normed = call(
            attend_kernel,
            shape((length, cols), bf16),
            [SMEM] + [VMEM] * (5 + len(states)),
            here,
            arrived,
            keys,
            values,
            q_own,
            w_other,
            *states,
            flops=4 * length * model * cols,
        )
        back = lax.all_to_all(
            normed.reshape(experts, CAP, cols), "mem", split_axis=0, concat_axis=0, tiled=True
        )
        back = back.reshape(length, cols)
        prior = [] if out is None else [out]
        out = pl.pallas_call(
            combine_kernel,
            grid=(1,),
            out_shape=shape((count, width), bf16),
            in_specs=[
                pl.BlockSpec((count, 8), lambda i: (0, 0)),
                pl.BlockSpec((length, cols), lambda i: (0, 0)),
            ]
            + [ANY] * len(prior),
            out_specs=pl.BlockSpec((count, cols), lambda i, at=first // heads: (0, at)),
            input_output_aliases={2: 0} if prior else {},
        )(table, back, *prior)
    return out


def solution(mesh):
    return jax.shard_map(
        on_device,
        mesh=mesh,
        in_specs=(
            P(("seq", "mem"), None),
            P(("seq", "mem"), None),
            P(("seq", "mem"), None),
            P("seq", None),
            P("mem", "seq", None),
            P("mem", "seq", None),
        ),
        out_specs=P(("seq", "mem"), None),
        check_vma=False,
    )
```

time: 290 us -> 164 us (0.57)
  waiting for transfers between devices: 142 us -> 84.3 us
  blocking collectives: 55.2 us -> 0 us
  starting transfers between devices: 8.28 us -> 48.5 us
  Pallas kernels: 0 us -> 24.8 us
  local copies, waits for them, and re-layouts: 28.1 us -> 5.07 us
  matrix products: 23 us -> 0 us
  other arithmetic: 19.1 us -> 0.07 us
  between operations: 13.4 us -> 0.23 us
    all_gather x4 -> x0, waiting for transfers between devices: 103 us -> none  [the longest x1 47.1 us: on_device(): lax.all_gather(query_weight, 'seq', axis=0, tiled=True)]
    ppermute x0 -> x27, waiting for transfers between devices: none -> 77.2 us  [swap(): return lax.ppermute(array, axis, pairs)]
    all_to_all x1 -> x0, blocking collectives: 55.2 us -> none  [on_device(): lax.all_to_all(sent_rows, 'mem', split_axis=0, concat_axis=1, tiled=True)]
    ppermute x0 -> x27, starting transfers between devices: none -> 38.9 us  [swap(): return lax.ppermute(array, axis, pairs)]
    all_to_all x2, waiting for transfers between devices: 37.4 us -> 7.12 us  [on_device(): lax.all_to_all(normed.reshape(experts, CAP, cols), 'mem', split_axis=0, c...]
    pallas_call x0 -> x10, Pallas kernels: none -> 24.8 us  [the longest x8 20.2 us: call(): pl.pallas_call(kernel, out_shape=jax.tree.map(lambda s: pltpu.VMEM(s.shap...]
    dot_general x7 -> x0, matrix products: 23 us -> none  [the longest x1 5.5 us: on_device(): jnp.einsum('mrc,mch->mrh', columns, lax.all_gather(key_weight, 'seq', axi...]
    unnamed x19 -> x22, local copies, waits for them, and re-layouts: 12.9 us -> 5.07 us
  transfers between devices with their start and end apart: 6 -> 29, of which waited for: 5 -> 14; matrix products, arithmetic and copies ran while one was open for 10% -> 0% of each run, Pallas kernels for 0% -> 10%
where the time goes in v1:
time: 164 us; the launch traced here: 163 us
  waiting for transfers between devices  84.3 us (51%)
  starting transfers between devices  48.5 us (30%)
  Pallas kernels  24.8 us (15%)
  local copies, waits for them, and re-layouts  5.07 us (3%)
    ppermute x27, waiting for transfers between devices, swap(): return lax.ppermute(array, axis, pairs)  77.2 us
    ppermute x27, starting transfers between devices, swap(): return lax.ppermute(array, axis, pairs)  38.9 us
    pallas_call x8, Pallas kernels, call(): pl.pallas_call(kernel, out_shape=jax.tree.map(lambda s: pltpu.VMEM(s.shap...  20.2 us
    all_to_all x2, starting transfers between devices, on_device(): lax.all_to_all(normed.reshape(experts, CAP, cols), 'mem', split_axis=0, c...  9.58 us
    all_to_all x2, waiting for transfers between devices, on_device(): lax.all_to_all(normed.reshape(experts, CAP, cols), 'mem', split_axis=0, c...  7.12 us
    unnamed x22, local copies, waits for them, and re-layouts  5.07 us
    pallas_call x2, Pallas kernels, on_device(): pl.pallas_call(combine_kernel, grid=(1,), out_shape=shape((count, width),...  4.63 us
  transfers between devices with their start and end apart: 29, of which 14 were waited for; matrix products, arithmetic and copies ran while one was open for 0% of the time, Pallas kernels for 10%

profile of v1, /device:TPU:0, one launch (start us, length us, event | category | flops | bytes accessed | tf_op | source)
XLA Modules:
  0.0 163.0 jit_solution(17777844576702978709)
XLA Ops:
  0.0 0.1 pad_add_fusion.here
  0.1 1.2 copy-done
  1.3 1.2 copy-done.2
  2.5 1.2 copy-done.4
  3.8 0.9 shard_map.69
  4.6 3.0 %collective-permute-start.17 = (bf16[512,1024]{1,0:T(8,128)(2,1)S(1)}, bf16[512,1024]{1,0:T(8,128)(2,1)S(1)}, u32[]{:S(2)}, u32[]{:S(2)}) collective-permute-start(bf16[512,1024]{1,0:T(8,128)(2,1)S(1)} %get-tuple-element.44.refs_0_), channel_id=1, source_target_pairs={{0,8},{8,0},{16,24},{24,16},{1,9},{9,1},{17,25},{25,17},{2,10},{10... | collective-permute-start | bytes 3145736 | tf_op jit(solution)/shard_map/ppermute | solution.py:26
  7.7 1.5 collective-permute-start.20
  9.2 2.3 %shard_map.64 = (f32[256,8]{1,0:T(8,128)S(1)}, bf16[64,2048]{1,0:T(8,128)(2,1)S(1)}, bf16[64,2048]{1,0:T(8,128)(2,1)S(1)}, bf16[64,2048]{1,0:T(8,128)(2,1)S(1)},...) custom-call(s32[2]{0:T(128)S(1)} %pad_add_fusion.here, ...), custom_call_target="tpu_custom_call" | custom-call | flops 536870912 | bytes 1048576 | tf_op jit(solution)/shard_map/pallas_call | solution.py:181
  11.5 0.7 copy-done.6
  12.1 0.0 collective-permute-start
  12.1 1.6 collective-permute-start.1
  13.7 0.3 collective-permute-start.2
  14.0 0.0 collective-permute-done.refs_1_
  14.0 2.6 %collective-permute-start.3 = (bf16[64,2048]{1,0:T(8,128)(2,1)S(1)}, bf16[64,2048]{1,0:T(8,128)(2,1)S(1)}, u32[]{:S(2)}, u32[]{:S(2)}) collective-permute-start(bf16[64,2048]{1,0:T(8,128)(2,1)S(1)} %get-tuple-element.33), channel_id=1, source_target_pairs={{0,4},{1,5},{2,6},{3,7},{4,0},{5,1},{6,2},{7,3},{8,12},{9,13},{10,... | collective-permute-start | bytes 786440 | tf_op jit(solution)/shard_map/ppermute | solution.py:26
  16.6 10.3 %collective-permute-done.1.refs_2_ = bf16[64,2048]{1,0:T(8,128)(2,1)S(1)} collective-permute-done((bf16[64,2048]{1,0:T(8,128)(2,1)S(1)}, bf16[64,2048]{1,0:T(8,128)(2,1)S(1)}, u32[]{:S(2)}, u32[]{:S(2)}) %collective-permute-start.1) | collective-permute-done | bytes 262176 | tf_op jit(solution)/shard_map/ppermute | solution.py:26
  26.9 0.5 collective-permute-start.18
  27.4 3.4 %collective-permute-done.17.refs_1_ = bf16[512,1024]{1,0:T(8,128)(2,1)S(1)} collective-permute-done((bf16[512,1024]{1,0:T(8,128)(2,1)S(1)}, bf16[512,1024]{1,0:T(8,128)(2,1)S(1)}, u32[]{:S(2)}, u32[]{:S(2)}) %collective-permute-start.17) | collective-permute-done | bytes 1048608 | tf_op jit(solution)/shard_map/ppermute | solution.py:26
  30.8 1.8 %collective-permute-start.19 = (bf16[512,1024]{1,0:T(8,128)(2,1)S(1)}, bf16[512,1024]{1,0:T(8,128)(2,1)S(1)}, u32[]{:S(2)}, u32[]{:S(2)}) collective-permute-start(bf16[512,1024]{1,0:T(8,128)(2,1)S(1)} %collective-permute-done.17.refs_1_), channel_id=1, source_target_pairs={{0,16},{8,24},{16,0},{24,8},{1,17},{9,25},{17,1},{25,9},{2,18},{10... | collective-permute-start | bytes 3145736 | tf_op jit(solution)/shard_map/ppermute | solution.py:26
  32.6 0.0 collective-permute-done.2.refs_3_
  32.6 1.5 collective-permute-start.21
  34.1 0.0 collective-permute-done.20.refs_5_
  34.1 0.5 collective-permute-start.22
  34.6 0.3 collective-permute-start.4
  35.0 14.5 %collective-permute-done.4.refs_5_ = bf16[64,2048]{1,0:T(8,128)(2,1)S(1)} collective-permute-done((bf16[64,2048]{1,0:T(8,128)(2,1)S(1)}, bf16[64,2048]{1,0:T(8,128)(2,1)S(1)}, u32[]{:S(2)}, u32[]{:S(2)}) %collective-permute-start.4) | collective-permute-done | bytes 262176 | tf_op jit(solution)/shard_map/ppermute | solution.py:26
  49.5 2.1 %collective-permute-start.5 = (bf16[64,2048]{1,0:T(8,128)(2,1)S(1)}, bf16[64,2048]{1,0:T(8,128)(2,1)S(1)}, u32[]{:S(2)}, u32[]{:S(2)}) collective-permute-start(bf16[64,2048]{1,0:T(8,128)(2,1)S(1)} %get-tuple-element.35), channel_id=1, source_target_pairs={{0,6},{1,7},{2,4},{3,5},{4,2},{5,3},{6,0},{7,1},{8,14},{9,15},{10,... | collective-permute-start | bytes 786440 | tf_op jit(solution)/shard_map/ppermute | solution.py:26
  51.6 8.2 %collective-permute-done.5.refs_6_ = bf16[64,2048]{1,0:T(8,128)(2,1)S(1)} collective-permute-done((bf16[64,2048]{1,0:T(8,128)(2,1)S(1)}, bf16[64,2048]{1,0:T(8,128)(2,1)S(1)}, u32[]{:S(2)}, u32[]{:S(2)}) %collective-permute-start.5) | collective-permute-done | bytes 262176 | tf_op jit(solution)/shard_map/ppermute | solution.py:26
  59.7 0.7 collective-permute-start.6
  60.5 9.2 %collective-permute-done.6.refs_7_ = bf16[64,2048]{1,0:T(8,128)(2,1)S(1)} collective-permute-done((bf16[64,2048]{1,0:T(8,128)(2,1)S(1)}, bf16[64,2048]{1,0:T(8,128)(2,1)S(1)}, u32[]{:S(2)}, u32[]{:S(2)}) %collective-permute-start.6) | collective-permute-done | bytes 262176 | tf_op jit(solution)/shard_map/ppermute | solution.py:26
  69.6 0.7 shard_map.65.x
  70.3 0.0 copy-start.1
  70.3 0.0 copy-start.3
  70.3 0.0 copy-start.5
  70.4 3.8 %collective-permute-done.22.refs_7_ = bf16[512,896]{1,0:T(8,128)(2,1)S(1)} collective-permute-done((bf16[512,896]{1,0:T(8,128)(2,1)S(1)}, bf16[512,896]{1,0:T(8,128)(2,1)S(1)}, u32[]{:S(2)}, u32[]{:S(2)}) %collective-permute-start.22) | collective-permute-done | bytes 917536 | tf_op jit(solution)/shard_map/ppermute | solution.py:26
  74.1 0.3 collective-permute-done.19.refs_3_
  74.4 5.4 %shard_map.70 = (bf16[512,768]{1,0:T(8,128)(2,1)S(1)}, bf16[512,768]{1,0:T(8,128)(2,1)S(1)}, bf16[512,384]{1,0:T(8,128)(2,1)S(1)}, bf16[6,128,128]{2,1,0:T(8,128)(2,1)S(1)}, bf16[2048,384]{1,0:T(8,128)(2,1)S(1)}) custom-call(s32[2]{0:T(128)S(1)} %pad_add_fusion.here, bf16[512,2048]{1,0:T(8,128)(2,1)S(1)} %shard_map.65.x, ...), custom_call_target="tpu_custom_call" | custom-call | flops 3221225472 | bytes 1048576 | tf_op jit(solution)/shard_map/pallas_call | solution.py:181
  79.8 0.1 collective-permute-start.23
  79.9 2.3 %collective-permute-start.24 = (bf16[6,128,128]{2,1,0:T(8,128)(2,1)S(1)}, bf16[6,128,128]{2,1,0:T(8,128)(2,1)S(1)}, u32[]{:S(2)}, u32[]{:S(2)}) collective-permute-start(bf16[6,128,128]{2,1,0:T(8,128)(2,1)S(1)} %get-tuple-element.50), channel_id=1, source_target_pairs={{0,8},{16,24},{1,9},{17,25},{2,10},{18,26},{3,11},{19,27},{4,12},{... | collective-permute-start | bytes 589832 | tf_op jit(solution)/shard_map/ppermute | solution.py:26
  82.2 3.6 %collective-permute-start.25 = (bf16[6,128,128]{2,1,0:T(8,128)(2,1)S(1)}, bf16[6,128,128]{2,1,0:T(8,128)(2,1)S(1)}, u32[]{:S(2)}, u32[]{:S(2)}) collective-permute-start(bf16[6,128,128]{2,1,0:T(8,128)(2,1)S(1)} %get-tuple-element.50), channel_id=1, source_target_pairs={{0,16},{8,24},{1,17},{9,25},{2,18},{10,26},{3,19},{11,27},{4,20},{... | collective-permute-start | bytes 589832 | tf_op jit(solution)/shard_map/ppermute | solution.py:26
  85.8 1.3 collective-permute-start.26
  87.1 0.7 shard_map.66
  87.8 0.1 collective-permute-start.10
  87.9 7.3 %collective-permute-done.25.refs_1_ = bf16[6,128,128]{2,1,0:T(8,128)(2,1)S(1)} collective-permute-done((bf16[6,128,128]{2,1,0:T(8,128)(2,1)S(1)}, bf16[6,128,128]{2,1,0:T(8,128)(2,1)S(1)}, u32[]{:S(2)}, u32[]{:S(2)}) %collective-permute-start.25) | collective-permute-done | bytes 196640 | tf_op jit(solution)/shard_map/ppermute | solution.py:26
  95.3 4.6 %shard_map.71 = bf16[512,768]{1,0:T(8,128)(2,1)} custom-call(s32[2]{0:T(128)S(1)} %pad_add_fusion.here, bf16[512,2048]{1,0:T(8,128)(2,1)S(1)} %shard_map.65.x, bf16[512,768]{1,0:T(8,128)(2,1)S(1)} %get-tuple-element.46.k, bf16[512,768]{1,0:T(8,128)(2,1)S(1)} %get-tuple-element.47.v, bf16[512,384]{1,0:T(8,128)(2,1)S(1)} %get-tuple-element.48.q_own, ...), custom_call_target="tpu_custom_call" | custom-call | flops 3221225472 | bytes 1048576 | tf_op jit(solution)/shard_map/pallas_call | solution.py:181
  99.8 4.9 %all-to-all-start.1 = ((bf16[8,64,768]{2,1,0:T(8,128)(2,1)}), bf16[8,64,768]{2,1,0:T(8,128)(2,1)}, u32[]{:S(2)}, u32[]{:S(2)}) async-start(bf16[8,64,768]{2,1,0:T(8,128)(2,1)} %bitcast.6), calls=%async_computation.1 | async-start | bytes 1572864 | tf_op jit(solution)/shard_map/all_to_all | solution.py:293
  104.7 2.0 %collective-permute-start.11 = (bf16[512,384]{1,0:T(8,128)(2,1)S(1)}, bf16[512,384]{1,0:T(8,128)(2,1)S(1)}, u32[]{:S(2)}, u32[]{:S(2)}) collective-permute-start(bf16[512,384]{1,0:T(8,128)(2,1)S(1)} %get-tuple-element.38.refs_4_), channel_id=1, source_target_pairs={{0,8},{8,0},{16,24},{24,16},{1,9},{9,1},{17,25},{25,17},{2,10},{10... | collective-permute-start | bytes 1179656 | tf_op jit(solution)/shard_map/ppermute | solution.py:26
  106.8 0.1 collective-permute-start.12
  106.8 2.5 %collective-permute-start.8 = (bf16[512,256]{1,0:T(8,128)(2,1)S(1)}, bf16[512,256]{1,0:T(8,128)(2,1)S(1)}, u32[]{:S(2)}, u32[]{:S(2)}) collective-permute-start(bf16[512,256]{1,0:T(8,128)(2,1)S(1)} %get-tuple-element.37.refs_0_), channel_id=1, source_target_pairs={{0,16},{8,24},{16,0},{24,8},{1,17},{9,25},{17,1},{25,9},{2,18},{10... | collective-permute-start | bytes 786440 | tf_op jit(solution)/shard_map/ppermute | solution.py:26
  109.3 4.6 %collective-permute-done.7.refs_1_ = bf16[512,256]{1,0:T(8,128)(2,1)S(1)} collective-permute-done((bf16[512,256]{1,0:T(8,128)(2,1)S(1)}, bf16[512,256]{1,0:T(8,128)(2,1)S(1)}, u32[]{:S(2)}, u32[]{:S(2)}) %collective-permute-start.7) | collective-permute-done | bytes 262176 | tf_op jit(solution)/shard_map/ppermute | solution.py:26
  113.9 2.5 %collective-permute-start.9 = (bf16[512,256]{1,0:T(8,128)(2,1)S(1)}, bf16[512,256]{1,0:T(8,128)(2,1)S(1)}, u32[]{:S(2)}, u32[]{:S(2)}) collective-permute-start(bf16[512,256]{1,0:T(8,128)(2,1)S(1)} %collective-permute-done.7.refs_1_), channel_id=1, source_target_pairs={{0,16},{8,24},{16,0},{24,8},{1,17},{9,25},{17,1},{25,9},{2,18},{10... | collective-permute-start | bytes 786440 | tf_op jit(solution)/shard_map/ppermute | solution.py:26
  116.4 5.9 %collective-permute-done.11.refs_6_ = bf16[512,384]{1,0:T(8,128)(2,1)S(1)} collective-permute-done((bf16[512,384]{1,0:T(8,128)(2,1)S(1)}, bf16[512,384]{1,0:T(8,128)(2,1)S(1)}, u32[]{:S(2)}, u32[]{:S(2)}) %collective-permute-start.11) | collective-permute-done | bytes 393248 | tf_op jit(solution)/shard_map/ppermute | solution.py:26
  122.3 8.0 %collective-permute-done.12.refs_7_ = bf16[512,384]{1,0:T(8,128)(2,1)S(1)} collective-permute-done((bf16[512,384]{1,0:T(8,128)(2,1)S(1)}, bf16[512,384]{1,0:T(8,128)(2,1)S(1)}, u32[]{:S(2)}, u32[]{:S(2)}) %collective-permute-start.12) | collective-permute-done | bytes 393248 | tf_op jit(solution)/shard_map/ppermute | solution.py:26
  130.3 2.5 %shard_map.67 = (bf16[512,256]{1,0:T(8,128)(2,1)S(1)}, bf16[512,256]{1,0:T(8,128)(2,1)S(1)}, bf16[512,128]{1,0:T(8,128)(2,1)S(1)}, bf16[2,128,128]{2,1,0:T(8,128)(2,1)S(1)}, bf16[2048,128]{1,0:T(8,128)(2,1)S(1)}) custom-call(s32[2]{0:T(128)S(1)} %pad_add_fusion.here, bf16[512,2048]{1,0:T(8,128)(2,1)S(1)} %shard_map.65.x, ...), custom_call_target="tpu_custom_call" | custom-call | flops 1073741824 | bytes 1048576 | tf_op jit(solution)/shard_map/pallas_call | solution.py:181
  132.8 0.1 collective-permute-start.13
  132.9 2.2 %collective-permute-start.14 = (bf16[2,128,128]{2,1,0:T(8,128)(2,1)S(1)}, bf16[2,128,128]{2,1,0:T(8,128)(2,1)S(1)}, u32[]{:S(2)}, u32[]{:S(2)}) collective-permute-start(bf16[2,128,128]{2,1,0:T(8,128)(2,1)S(1)} %get-tuple-element.43), channel_id=1, source_target_pairs={{0,8},{16,24},{1,9},{17,25},{2,10},{18,26},{3,11},{19,27},{4,12},{... | collective-permute-start | bytes 196616 | tf_op jit(solution)/shard_map/ppermute | solution.py:26
  135.1 4.4 %collective-permute-start.15 = (bf16[2,128,128]{2,1,0:T(8,128)(2,1)S(1)}, bf16[2,128,128]{2,1,0:T(8,128)(2,1)S(1)}, u32[]{:S(2)}, u32[]{:S(2)}) collective-permute-start(bf16[2,128,128]{2,1,0:T(8,128)(2,1)S(1)} %get-tuple-element.43), channel_id=1, source_target_pairs={{0,16},{8,24},{1,17},{9,25},{2,18},{10,26},{3,19},{11,27},{4,20},{... | collective-permute-start | bytes 196616 | tf_op jit(solution)/shard_map/ppermute | solution.py:26
  139.5 1.5 collective-permute-start.16
  141.0 0.4 collective-permute-done.15.refs_1_
  141.4 1.3 collective-permute-done.16.refs_2_
  142.7 3.2 %shard_map.68 = bf16[512,256]{1,0:T(8,128)(2,1)} custom-call(s32[2]{0:T(128)S(1)} %pad_add_fusion.here, bf16[512,2048]{1,0:T(8,128)(2,1)S(1)} %shard_map.65.x, bf16[512,256]{1,0:T(8,128)(2,1)S(1)} %get-tuple-element.39.k, bf16[512,256]{1,0:T(8,128)(2,1)S(1)} %get-tuple-element.40.v, bf16[512,128]{1,0:T(8,128)(2,1)S(1)} %get-tuple-element.41.q_own, ...), custom_call_target="tpu_custom_call" | custom-call | flops 1073741824 | bytes 1048576 | tf_op jit(solution)/shard_map/pallas_call | solution.py:181
  145.9 4.7 %all-to-all-start = ((bf16[8,64,256]{2,1,0:T(8,128)(2,1)}), bf16[8,64,256]{2,1,0:T(8,128)(2,1)S(1)}, u32[]{:S(2)}, u32[]{:S(2)}) async-start(bf16[8,64,256]{2,1,0:T(8,128)(2,1)} %bitcast.4), calls=%async_computation | async-start | bytes 524288 | tf_op jit(solution)/shard_map/all_to_all | solution.py:293
  150.6 2.6 %shard_map.72.refs_0_ = bf16[256,1024]{1,0:T(8,128)(2,1)} custom-call(f32[256,8]{1,0:T(8,128)} %copy-done.6, bf16[512,768]{1,0:T(8,128)(2,1)} %bitcast.7.part), custom_call_target="tpu_custom_call" | custom-call | tf_op jit(solution)/shard_map/pallas_call | solution.py:298
  153.1 7.1 %all-to-all-done = bf16[8,64,256]{2,1,0:T(8,128)(2,1)S(1)} async-done(((bf16[8,64,256]{2,1,0:T(8,128)(2,1)}), bf16[8,64,256]{2,1,0:T(8,128)(2,1)S(1)}, u32[]{:S(2)}, u32[]{:S(2)}) %all-to-all-start) | async-done | bytes 262176 | tf_op jit(solution)/shard_map/all_to_all | solution.py:293
  160.3 0.7 copy-done.10
  161.0 2.0 %shard_map.73 = bf16[256,1024]{1,0:T(8,128)(2,1)} custom-call(f32[256,8]{1,0:T(8,128)} %copy-done.6, bf16[512,256]{1,0:T(8,128)(2,1)} %bitcast.10, bf16[256,1024]{1,0:T(8,128)(2,1)} %shard_map.72.refs_0_), custom_call_target="tpu_custom_call", output_to_operand_aliasing={{}: (2, {})} | custom-call | tf_op jit(solution)/shard_map/pallas_call | solution.py:298
  (27 shorter events, 0.1 us)
Async XLA Ops:
  0.1 1.2 copy-start
  1.3 1.2 copy-start.2
  2.5 1.2 copy-start.4
  3.8 5.4 %copy-start.7 = (bf16[256,2048]{1,0:T(8,128)(2,1)S(1)}, bf16[256,2048]{1,0:T(8,128)(2,1)}, u32[]{:S(2)}) copy-start(bf16[256,2048]{1,0:T(8,128)(2,1)} %hidden.1) | copy-start | bytes 3145732
  3.8 5.4 %copy-start.8 = (s32[256,2]{0,1:T(2,128)S(1)}, s32[256,2]{0,1:T(2,128)}, u32[]{:S(2)}) copy-start(s32[256,2]{0,1:T(2,128)} %param.7) | copy-start | bytes 6148
  3.8 5.4 %copy-start.9 = (s32[256,2]{0,1:T(2,128)S(1)}, s32[256,2]{0,1:T(2,128)}, u32[]{:S(2)}) copy-start(s32[256,2]{0,1:T(2,128)} %param.8) | copy-start | bytes 6148
  4.6 26.2 %collective-permute-start.17 = (bf16[512,1024]{1,0:T(8,128)(2,1)S(1)}, bf16[512,1024]{1,0:T(8,128)(2,1)S(1)}, u32[]{:S(2)}, u32[]{:S(2)}) collective-permute-start(bf16[512,1024]{1,0:T(8,128)(2,1)S(1)} %get-tuple-element.44.refs_0_), channel_id=1, source_target_pairs={{0,8},{8,0},{16,24},{24,16},{1,9},{9,1},{17,25},{25,17},{2,10},{10... | collective-permute-start | bytes 3145736 | tf_op jit(solution)/shard_map/ppermute | solution.py:26
  7.7 26.4 %collective-permute-start.20 = (bf16[512,896]{1,0:T(8,128)(2,1)S(1)}, bf16[512,896]{1,0:T(8,128)(2,1)S(1)}, u32[]{:S(2)}, u32[]{:S(2)}) collective-permute-start(bf16[512,896]{1,0:T(8,128)(2,1)S(1)} %get-tuple-element.45.refs_4_), channel_id=1, source_target_pairs={{0,16},{8,24},{16,0},{24,8},{1,17},{9,25},{17,1},{25,9},{2,18},{10... | collective-permute-start | bytes 2752520 | tf_op jit(solution)/shard_map/ppermute | solution.py:26
  11.5 0.7 copy-start.6
  12.1 1.9 %collective-permute-start = (bf16[64,2048]{1,0:T(8,128)(2,1)S(1)}, bf16[64,2048]{1,0:T(8,128)(2,1)S(1)}, u32[]{:S(2)}, u32[]{:S(2)}) collective-permute-start(bf16[64,2048]{1,0:T(8,128)(2,1)S(1)} %get-tuple-element.30), channel_id=1, source_target_pairs={{0,1},{1,0},{2,3},{3,2},{4,5},{5,4},{6,7},{7,6},{8,9},{9,8},{10,11... | collective-permute-start | bytes 786440 | tf_op jit(solution)/shard_map/ppermute | solution.py:26
  12.1 14.8 %collective-permute-start.1 = (bf16[64,2048]{1,0:T(8,128)(2,1)S(1)}, bf16[64,2048]{1,0:T(8,128)(2,1)S(1)}, u32[]{:S(2)}, u32[]{:S(2)}) collective-permute-start(bf16[64,2048]{1,0:T(8,128)(2,1)S(1)} %get-tuple-element.31), channel_id=1, source_target_pairs={{0,2},{1,3},{2,0},{3,1},{4,6},{5,7},{6,4},{7,5},{8,10},{9,11},{10,... | collective-permute-start | bytes 786440 | tf_op jit(solution)/shard_map/ppermute | solution.py:26
  13.7 18.9 %collective-permute-start.2 = (bf16[64,2048]{1,0:T(8,128)(2,1)S(1)}, bf16[64,2048]{1,0:T(8,128)(2,1)S(1)}, u32[]{:S(2)}, u32[]{:S(2)}) collective-permute-start(bf16[64,2048]{1,0:T(8,128)(2,1)S(1)} %get-tuple-element.32), channel_id=1, source_target_pairs={{0,3},{1,2},{2,1},{3,0},{4,7},{5,6},{6,5},{7,4},{8,11},{9,10},{10,... | collective-permute-start | bytes 786440 | tf_op jit(solution)/shard_map/ppermute | solution.py:26
  14.0 20.6 %collective-permute-start.3 = (bf16[64,2048]{1,0:T(8,128)(2,1)S(1)}, bf16[64,2048]{1,0:T(8,128)(2,1)S(1)}, u32[]{:S(2)}, u32[]{:S(2)}) collective-permute-start(bf16[64,2048]{1,0:T(8,128)(2,1)S(1)} %get-tuple-element.33), channel_id=1, source_target_pairs={{0,4},{1,5},{2,6},{3,7},{4,0},{5,1},{6,2},{7,3},{8,12},{9,13},{10,... | collective-permute-start | bytes 786440 | tf_op jit(solution)/shard_map/ppermute | solution.py:26
  26.9 43.4 %collective-permute-start.18 = (bf16[512,1024]{1,0:T(8,128)(2,1)S(1)}, bf16[512,1024]{1,0:T(8,128)(2,1)S(1)}, u32[]{:S(2)}, u32[]{:S(2)}) collective-permute-start(bf16[512,1024]{1,0:T(8,128)(2,1)S(1)} %get-tuple-element.44.refs_0_), channel_id=1, source_target_pairs={{0,16},{8,24},{16,0},{24,8},{1,17},{9,25},{17,1},{25,9},{2,18},{10... | collective-permute-start | bytes 3145736 | tf_op jit(solution)/shard_map/ppermute | solution.py:26
  30.8 43.6 %collective-permute-start.19 = (bf16[512,1024]{1,0:T(8,128)(2,1)S(1)}, bf16[512,1024]{1,0:T(8,128)(2,1)S(1)}, u32[]{:S(2)}, u32[]{:S(2)}) collective-permute-start(bf16[512,1024]{1,0:T(8,128)(2,1)S(1)} %collective-permute-done.17.refs_1_), channel_id=1, source_target_pairs={{0,16},{8,24},{16,0},{24,8},{1,17},{9,25},{17,1},{25,9},{2,18},{10... | collective-permute-start | bytes 3145736 | tf_op jit(solution)/shard_map/ppermute | solution.py:26
  32.6 37.8 %collective-permute-start.21 = (bf16[512,896]{1,0:T(8,128)(2,1)S(1)}, bf16[512,896]{1,0:T(8,128)(2,1)S(1)}, u32[]{:S(2)}, u32[]{:S(2)}) collective-permute-start(bf16[512,896]{1,0:T(8,128)(2,1)S(1)} %get-tuple-element.45.refs_4_), channel_id=1, source_target_pairs={{0,8},{8,0},{16,24},{24,16},{1,9},{9,1},{17,25},{25,17},{2,10},{10... | collective-permute-start | bytes 2752520 | tf_op jit(solution)/shard_map/ppermute | solution.py:26
  34.1 40.0 %collective-permute-start.22 = (bf16[512,896]{1,0:T(8,128)(2,1)S(1)}, bf16[512,896]{1,0:T(8,128)(2,1)S(1)}, u32[]{:S(2)}, u32[]{:S(2)}) collective-permute-start(bf16[512,896]{1,0:T(8,128)(2,1)S(1)} %collective-permute-done.20.refs_5_), channel_id=1, source_target_pairs={{0,8},{8,0},{16,24},{24,16},{1,9},{9,1},{17,25},{25,17},{2,10},{10... | collective-permute-start | bytes 2752520 | tf_op jit(solution)/shard_map/ppermute | solution.py:26
  34.6 14.9 %collective-permute-start.4 = (bf16[64,2048]{1,0:T(8,128)(2,1)S(1)}, bf16[64,2048]{1,0:T(8,128)(2,1)S(1)}, u32[]{:S(2)}, u32[]{:S(2)}) collective-permute-start(bf16[64,2048]{1,0:T(8,128)(2,1)S(1)} %get-tuple-element.34), channel_id=1, source_target_pairs={{0,5},{1,4},{2,7},{3,6},{4,1},{5,0},{6,3},{7,2},{8,13},{9,12},{10,... | collective-permute-start | bytes 786440 | tf_op jit(solution)/shard_map/ppermute | solution.py:26
  49.5 10.2 %collective-permute-start.5 = (bf16[64,2048]{1,0:T(8,128)(2,1)S(1)}, bf16[64,2048]{1,0:T(8,128)(2,1)S(1)}, u32[]{:S(2)}, u32[]{:S(2)}) collective-permute-start(bf16[64,2048]{1,0:T(8,128)(2,1)S(1)} %get-tuple-element.35), channel_id=1, source_target_pairs={{0,6},{1,7},{2,4},{3,5},{4,2},{5,3},{6,0},{7,1},{8,14},{9,15},{10,... | collective-permute-start | bytes 786440 | tf_op jit(solution)/shard_map/ppermute | solution.py:26
  59.7 9.9 %collective-permute-start.6 = (bf16[64,2048]{1,0:T(8,128)(2,1)S(1)}, bf16[64,2048]{1,0:T(8,128)(2,1)S(1)}, u32[]{:S(2)}, u32[]{:S(2)}) collective-permute-start(bf16[64,2048]{1,0:T(8,128)(2,1)S(1)} %get-tuple-element.36), channel_id=1, source_target_pairs={{0,7},{1,6},{2,5},{3,4},{4,3},{5,2},{6,1},{7,0},{8,15},{9,14},{10,... | collective-permute-start | bytes 786440 | tf_op jit(solution)/shard_map/ppermute | solution.py:26
  70.3 16.8 %copy-start.1 = (bf16[512,1024]{1,0:T(8,128)(2,1)S(1)}, bf16[512,1024]{1,0:T(8,128)(2,1)}, u32[]{:S(2)}) copy-start(bf16[512,1024]{1,0:T(8,128)(2,1)} %query.3) | copy-start | bytes 3145732
  70.3 16.8 %copy-start.3 = (bf16[1,512,1024]{2,1,0:T(8,128)(2,1)S(1)}, bf16[1,512,1024]{2,1,0:T(8,128)(2,1)}, u32[]{:S(2)}) copy-start(bf16[1,512,1024]{2,1,0:T(8,128)(2,1)} %key.3) | copy-start | bytes 3145732
  70.3 16.8 %copy-start.5 = (bf16[1,512,1024]{2,1,0:T(8,128)(2,1)S(1)}, bf16[1,512,1024]{2,1,0:T(8,128)(2,1)}, u32[]{:S(2)}) copy-start(bf16[1,512,1024]{2,1,0:T(8,128)(2,1)} %value.3) | copy-start | bytes 3145732
  79.8 15.5 %collective-permute-start.23 = (bf16[2048,384]{1,0:T(8,128)(2,1)S(1)}, bf16[2048,384]{1,0:T(8,128)(2,1)S(1)}, u32[]{:S(2)}, u32[]{:S(2)}) collective-permute-start(bf16[2048,384]{1,0:T(8,128)(2,1)S(1)} %get-tuple-element.49), channel_id=1, source_target_pairs={{0,1},{1,0},{2,3},{3,2},{4,5},{5,4},{6,7},{7,6},{8,9},{9,8},{10,11... | collective-permute-start | bytes 4718600 | tf_op jit(solution)/shard_map/ppermute | solution.py:26
  79.9 8.0 %collective-permute-start.24 = (bf16[6,128,128]{2,1,0:T(8,128)(2,1)S(1)}, bf16[6,128,128]{2,1,0:T(8,128)(2,1)S(1)}, u32[]{:S(2)}, u32[]{:S(2)}) collective-permute-start(bf16[6,128,128]{2,1,0:T(8,128)(2,1)S(1)} %get-tuple-element.50), channel_id=1, source_target_pairs={{0,8},{16,24},{1,9},{17,25},{2,10},{18,26},{3,11},{19,27},{4,12},{... | collective-permute-start | bytes 589832 | tf_op jit(solution)/shard_map/ppermute | solution.py:26
  82.2 13.1 %collective-permute-start.25 = (bf16[6,128,128]{2,1,0:T(8,128)(2,1)S(1)}, bf16[6,128,128]{2,1,0:T(8,128)(2,1)S(1)}, u32[]{:S(2)}, u32[]{:S(2)}) collective-permute-start(bf16[6,128,128]{2,1,0:T(8,128)(2,1)S(1)} %get-tuple-element.50), channel_id=1, source_target_pairs={{0,16},{8,24},{1,17},{9,25},{2,18},{10,26},{3,19},{11,27},{4,20},{... | collective-permute-start | bytes 589832 | tf_op jit(solution)/shard_map/ppermute | solution.py:26
  85.8 9.5 %collective-permute-start.26 = (bf16[6,128,128]{2,1,0:T(8,128)(2,1)S(1)}, bf16[6,128,128]{2,1,0:T(8,128)(2,1)S(1)}, u32[]{:S(2)}, u32[]{:S(2)}) collective-permute-start(bf16[6,128,128]{2,1,0:T(8,128)(2,1)S(1)} %get-tuple-element.50), channel_id=1, source_target_pairs={{0,24},{8,16},{1,25},{9,17},{2,26},{10,18},{3,27},{11,19},{4,28},{... | collective-permute-start | bytes 589832 | tf_op jit(solution)/shard_map/ppermute | solution.py:26
  87.8 18.9 %collective-permute-start.10 = (bf16[512,384]{1,0:T(8,128)(2,1)S(1)}, bf16[512,384]{1,0:T(8,128)(2,1)S(1)}, u32[]{:S(2)}, u32[]{:S(2)}) collective-permute-start(bf16[512,384]{1,0:T(8,128)(2,1)S(1)} %get-tuple-element.38.refs_4_), channel_id=1, source_target_pairs={{0,16},{8,24},{16,0},{24,8},{1,17},{9,25},{17,1},{25,9},{2,18},{10... | collective-permute-start | bytes 1179656 | tf_op jit(solution)/shard_map/ppermute | solution.py:26
  99.8 46.0 %all-to-all-start.1 = ((bf16[8,64,768]{2,1,0:T(8,128)(2,1)}), bf16[8,64,768]{2,1,0:T(8,128)(2,1)}, u32[]{:S(2)}, u32[]{:S(2)}) async-start(bf16[8,64,768]{2,1,0:T(8,128)(2,1)} %bitcast.6), calls=%async_computation.1 | async-start | bytes 1572864 | tf_op jit(solution)/shard_map/all_to_all | solution.py:293
  104.7 9.2 %collective-permute-start.7 = (bf16[512,256]{1,0:T(8,128)(2,1)S(1)}, bf16[512,256]{1,0:T(8,128)(2,1)S(1)}, u32[]{:S(2)}, u32[]{:S(2)}) collective-permute-start(bf16[512,256]{1,0:T(8,128)(2,1)S(1)} %get-tuple-element.37.refs_0_), channel_id=1, source_target_pairs={{0,8},{8,0},{16,24},{24,16},{1,9},{9,1},{17,25},{25,17},{2,10},{10... | collective-permute-start | bytes 786440 | tf_op jit(solution)/shard_map/ppermute | solution.py:26
  104.7 17.6 %collective-permute-start.11 = (bf16[512,384]{1,0:T(8,128)(2,1)S(1)}, bf16[512,384]{1,0:T(8,128)(2,1)S(1)}, u32[]{:S(2)}, u32[]{:S(2)}) collective-permute-start(bf16[512,384]{1,0:T(8,128)(2,1)S(1)} %get-tuple-element.38.refs_4_), channel_id=1, source_target_pairs={{0,8},{8,0},{16,24},{24,16},{1,9},{9,1},{17,25},{25,17},{2,10},{10... | collective-permute-start | bytes 1179656 | tf_op jit(solution)/shard_map/ppermute | solution.py:26
  106.8 23.5 %collective-permute-start.12 = (bf16[512,384]{1,0:T(8,128)(2,1)S(1)}, bf16[512,384]{1,0:T(8,128)(2,1)S(1)}, u32[]{:S(2)}, u32[]{:S(2)}) collective-permute-start(bf16[512,384]{1,0:T(8,128)(2,1)S(1)} %collective-permute-done.10.refs_5_), channel_id=1, source_target_pairs={{0,8},{8,0},{16,24},{24,16},{1,9},{9,1},{17,25},{25,17},{2,10},{10... | collective-permute-start | bytes 1179656 | tf_op jit(solution)/shard_map/ppermute | solution.py:26
  106.8 9.6 %collective-permute-start.8 = (bf16[512,256]{1,0:T(8,128)(2,1)S(1)}, bf16[512,256]{1,0:T(8,128)(2,1)S(1)}, u32[]{:S(2)}, u32[]{:S(2)}) collective-permute-start(bf16[512,256]{1,0:T(8,128)(2,1)S(1)} %get-tuple-element.37.refs_0_), channel_id=1, source_target_pairs={{0,16},{8,24},{16,0},{24,8},{1,17},{9,25},{17,1},{25,9},{2,18},{10... | collective-permute-start | bytes 786440 | tf_op jit(solution)/shard_map/ppermute | solution.py:26
  113.9 8.4 %collective-permute-start.9 = (bf16[512,256]{1,0:T(8,128)(2,1)S(1)}, bf16[512,256]{1,0:T(8,128)(2,1)S(1)}, u32[]{:S(2)}, u32[]{:S(2)}) collective-permute-start(bf16[512,256]{1,0:T(8,128)(2,1)S(1)} %collective-permute-done.7.refs_1_), channel_id=1, source_target_pairs={{0,16},{8,24},{16,0},{24,8},{1,17},{9,25},{17,1},{25,9},{2,18},{10... | collective-permute-start | bytes 786440 | tf_op jit(solution)/shard_map/ppermute | solution.py:26
  132.8 9.9 %collective-permute-start.13 = (bf16[2048,128]{1,0:T(8,128)(2,1)S(1)}, bf16[2048,128]{1,0:T(8,128)(2,1)S(1)}, u32[]{:S(2)}, u32[]{:S(2)}) collective-permute-start(bf16[2048,128]{1,0:T(8,128)(2,1)S(1)} %get-tuple-element.42), channel_id=1, source_target_pairs={{0,1},{1,0},{2,3},{3,2},{4,5},{5,4},{6,7},{7,6},{8,9},{9,8},{10,11... | collective-permute-start | bytes 1572872 | tf_op jit(solution)/shard_map/ppermute | solution.py:26
  132.9 8.1 %collective-permute-start.14 = (bf16[2,128,128]{2,1,0:T(8,128)(2,1)S(1)}, bf16[2,128,128]{2,1,0:T(8,128)(2,1)S(1)}, u32[]{:S(2)}, u32[]{:S(2)}) collective-permute-start(bf16[2,128,128]{2,1,0:T(8,128)(2,1)S(1)} %get-tuple-element.43), channel_id=1, source_target_pairs={{0,8},{16,24},{1,9},{17,25},{2,10},{18,26},{3,11},{19,27},{4,12},{... | collective-permute-start | bytes 196616 | tf_op jit(solution)/shard_map/ppermute | solution.py:26
  135.1 6.3 %collective-permute-start.15 = (bf16[2,128,128]{2,1,0:T(8,128)(2,1)S(1)}, bf16[2,128,128]{2,1,0:T(8,128)(2,1)S(1)}, u32[]{:S(2)}, u32[]{:S(2)}) collective-permute-start(bf16[2,128,128]{2,1,0:T(8,128)(2,1)S(1)} %get-tuple-element.43), channel_id=1, source_target_pairs={{0,16},{8,24},{1,17},{9,25},{2,18},{10,26},{3,19},{11,27},{4,20},{... | collective-permute-start | bytes 196616 | tf_op jit(solution)/shard_map/ppermute | solution.py:26
  139.5 3.2 %collective-permute-start.16 = (bf16[2,128,128]{2,1,0:T(8,128)(2,1)S(1)}, bf16[2,128,128]{2,1,0:T(8,128)(2,1)S(1)}, u32[]{:S(2)}, u32[]{:S(2)}) collective-permute-start(bf16[2,128,128]{2,1,0:T(8,128)(2,1)S(1)} %get-tuple-element.43), channel_id=1, source_target_pairs={{0,24},{8,16},{1,25},{9,17},{2,26},{10,18},{3,27},{11,19},{4,28},{... | collective-permute-start | bytes 196616 | tf_op jit(solution)/shard_map/ppermute | solution.py:26
  145.9 14.4 %all-to-all-start = ((bf16[8,64,256]{2,1,0:T(8,128)(2,1)}), bf16[8,64,256]{2,1,0:T(8,128)(2,1)S(1)}, u32[]{:S(2)}, u32[]{:S(2)}) async-start(bf16[8,64,256]{2,1,0:T(8,128)(2,1)} %bitcast.4), calls=%async_computation | async-start | bytes 524288 | tf_op jit(solution)/shard_map/all_to_all | solution.py:293
  160.3 0.7 copy-start.10

commit v2 on v1

v2 whole, which is shorter than its diff:
```python
import functools

import jax
import jax.numpy as jnp
from jax import lax
from jax.experimental import pallas as pl
from jax.experimental.pallas import tpu as pltpu
from jax.sharding import PartitionSpec as P


DK = 128
CAP = 64
LAST_HEADS = 3
LIMIT = 24 << 20
VMEM = pl.BlockSpec(memory_space=pltpu.VMEM)
SMEM = pl.BlockSpec(memory_space=pltpu.SMEM)
ANY = pl.BlockSpec(memory_space=pl.ANY)
HBM = pl.BlockSpec(memory_space=pltpu.HBM)
shape = jax.ShapeDtypeStruct
bf16 = jnp.bfloat16


def swap(array, axis, mask):
    return lax.ppermute(array, axis, [(i, i ^ mask) for i in range(lax.axis_size(axis))])


def contract(left, right, left_dim, right_dim):
    return lax.dot_general(
        left, right, (((left_dim,), (right_dim,)), ((), ())), preferred_element_type=jnp.float32
    )


def dispatch_kernel(here, routes, levels, hidden, table, *sent):
    count = hidden.shape[0]
    experts = len(sent)
    named = [routes[j : j + 1, :] for j in range(2)]
    memory = lax.broadcasted_iota(jnp.int32, (experts, count), 0)
    hits = [(memory == name).astype(jnp.float32) for name in named]
    rows = lax.broadcasted_iota(jnp.int32, (count, count), 0)
    cols = lax.broadcasted_iota(jnp.int32, (count, count), 1)
    earlier = jnp.where(rows < cols, 1.0, 0.0).astype(bf16)
    before = contract((hits[0] + hits[1]).astype(bf16), earlier, 1, 0)
    places = [jnp.sum(h * before, axis=0, keepdims=True).astype(jnp.int32) for h in hits]
    index = lax.broadcasted_iota(jnp.int32, (CAP, count), 0)
    crossed = [(name ^ here[1]) * CAP + place for name, place in zip(named, places)]
    for k in range(experts):
        at = index + k * CAP
        pick = jnp.where((at == crossed[0]) | (at == crossed[1]), 1.0, 0.0).astype(bf16)
        sent[k][...] = contract(pick, hidden[...], 1, 0).astype(bf16)
    slots = [(name * CAP + place).astype(jnp.float32) for name, place in zip(named, places)]
    level = levels[...].astype(jnp.float32)
    gates = level / (level[0:1, :] + level[1:2, :])
    entries = jnp.concatenate(slots + [gates, jnp.zeros((4, count), jnp.float32)], axis=0)
    table[...] = entries.T


def pack_kernel(here, *refs, plan, sources):
    weights, outs, sems = refs[:sources], refs[sources:-1], refs[-1]
    copies = []
    for i, ((source, start, step), out) in enumerate(zip(plan, outs)):
        at = pl.multiple_of(start + (here[1] & 3) * step, DK) if step else start
        cols = pl.ds(at, out.shape[1])
        ref = weights[source]
        view = ref.at[0, :, cols] if len(ref.shape) == 3 else ref.at[:, cols]
        copies.append(pltpu.make_async_copy(view, out, sems.at[i]))
    for copy in copies:
        copy.start()
    for copy in copies:
        copy.wait()


def join_kernel(here, *refs):
    *pieces, out = refs
    for k, piece in enumerate(pieces):
        out[pl.ds(pl.multiple_of((here[1] ^ k) * CAP, CAP), CAP), :] = piece[...]


def project(x, seq, pieces, masks):
    total = None
    for piece, mask in zip(pieces, masks):
        rows = piece.shape[0]
        at = pl.multiple_of((seq ^ mask) * rows, rows)
        part = contract(x[:, pl.ds(at, rows)], piece[...], 1, 0)
        total = part if total is None else total + part
    return total


def kv_kernel(here, x, *refs, masks):
    n = len(masks[0])
    k_out, v_out, t_out = refs[2 * n :]
    k_out[...] = project(x, here[0], refs[:n], masks[0]).astype(bf16)
    v_out[...] = project(x, here[0], refs[n : 2 * n], masks[1]).astype(bf16)
    for h in range(t_out.shape[0]):
        cols = slice(h * DK, (h + 1) * DK)
        t_out[h] = contract(k_out[:, cols], v_out[:, cols], 0, 0).astype(bf16)


def rows_kernel(here, *refs, masks):
    n = len(masks[0])
    out = refs[2 * n]
    at_col = 0
    for pieces, own in ((refs[:n], masks[0]), (refs[n : 2 * n], masks[1])):
        rows, cols = pieces[0].shape
        for piece, mask in zip(pieces, own):
            at = pl.multiple_of((here[0] ^ mask) * rows, rows)
            out[pl.ds(at, rows), at_col : at_col + cols] = piece[...]
        at_col += cols


def query_kernel(here, x, *refs):
    *quarters, out = refs
    for k, quarter in enumerate(quarters):
        cols = quarter.shape[1]
        at = pl.multiple_of(((here[1] & 3) ^ k) * cols, cols)
        out[:, pl.ds(at, cols)] = contract(x[...], quarter[...], 1, 0).astype(bf16)


def attend_kernel(here, q_all, k, v, *refs, first):
    *states, out = refs
    length = k.shape[0]
    step = length // 2
    row = lax.broadcasted_iota(jnp.int32, (step, step), 0)
    col = lax.broadcasted_iota(jnp.int32, (step, step), 1)
    causal = row >= col
    for head in range(states[0].shape[0]):
        cols = slice(head * DK, (head + 1) * DK)
        q_cols = slice((first + head) * DK, (first + head + 1) * DK)
        state = jnp.zeros((DK, DK), jnp.float32)
        for m, other in enumerate(states, 1):
            earlier = (here[0] ^ m) < here[0]
            state = state + jnp.where(earlier, other[head].astype(jnp.float32), 0.0)
        high = state.astype(bf16)
        low = (state - high.astype(jnp.float32)).astype(bf16)
        for b in range(2):
            rows = slice(b * step, (b + 1) * step)
            q = q_all[rows, q_cols]
            scores = jnp.where(causal, contract(q, k[rows, cols], 1, 1), 0.0).astype(bf16)
            reads = contract(scores, v[rows, cols], 1, 0)
            for e in range(b):
                before = slice(e * step, (e + 1) * step)
                scores = contract(q, k[before, cols], 1, 1).astype(bf16)
                reads = reads + contract(scores, v[before, cols], 1, 0)
            reads = reads + contract(q, high, 1, 0) + contract(q, low, 1, 0)
            scale = lax.rsqrt(jnp.mean(reads * reads, axis=-1, keepdims=True) + 1e-06)
            out[rows, cols] = (reads * scale).astype(bf16)


def combine_kernel(table, part, *refs):
    *prior, out = refs
    count = table.shape[0]
    at = 0
    for done in prior:
        out[:, : done.shape[1]] = done[...]
        at = done.shape[1]
    index = lax.broadcasted_iota(jnp.int32, (count, part.shape[0]), 1).astype(jnp.float32)
    mixed = None
    for j in range(2):
        pick = jnp.where(index == table[:, j : j + 1], 1.0, 0.0).astype(bf16)
        term = table[:, 2 + j : 3 + j] * contract(pick, part[...], 1, 0)
        mixed = term if mixed is None else mixed + term
    out[:, at:] = mixed.astype(bf16)


def call(kernel, outs, ins, *arrays, flops=1, scratch=(), last=False):
    arrays = [
        pltpu.with_memory_space_constraint(a, pltpu.VMEM) if spec is VMEM else a
        for a, spec in zip(arrays, ins)
    ]
    return pl.pallas_call(
        kernel,
        out_shape=outs if last else jax.tree.map(lambda s: pltpu.VMEM(s.shape, s.dtype), outs),
        in_specs=ins,
        out_specs=jax.tree.map(lambda _: VMEM, outs),
        scratch_shapes=scratch,
        compiler_params=pltpu.CompilerParams(vmem_limit_bytes=LIMIT),
        cost_estimate=pl.CostEstimate(flops=flops, bytes_accessed=1 << 20, transcendentals=0),
    )(*arrays)


def spread(first, bits):
    pieces, masks = [first], [0]
    for bit in bits:
        fresh = []
        for piece in pieces:
            fresh.append(swap(piece, "seq", bit))
        pieces = pieces + fresh
        masks = masks + [m ^ bit for m in masks]
    return pieces, tuple(masks)


def on_device(hidden, routes, gate_levels, query_weight, key_weight, value_weight):
    count, model = hidden.shape
    rows, width = query_weight.shape
    groups, experts = lax.axis_size("seq"), lax.axis_size("mem")
    here = jnp.stack([lax.axis_index("seq"), lax.axis_index("mem")]).astype(jnp.int32)
    bits = [1 << b for b in range(groups.bit_length() - 1)]
    length = experts * CAP
    all_heads = width // DK
    chunks = [(0, all_heads - LAST_HEADS), (all_heads - LAST_HEADS, LAST_HEADS)]

    def pack(plan):
        arrays = [query_weight, key_weight, value_weight]
        return call(
            functools.partial(pack_kernel, plan=[p[:3] for p in plan], sources=len(arrays)),
            [shape((rows, p[3]), bf16) for p in plan],
            [SMEM] + [HBM] * len(arrays),
            here,
            *[pltpu.with_memory_space_constraint(a, pltpu.HBM) for a in arrays],
            scratch=[pltpu.SemaphoreType.DMA((len(plan),))],
        )

    quarter = width // 4
    part = quarter // 2
    bound = chunks[0][1] * DK
    qa, qb = pack([(0, 0, quarter, part), (0, part, quarter, part)])
    k0, v0 = pack([(1, 0, 0, bound), (2, 0, 0, bound)])
    k1, v1 = pack([(1, bound, 0, width - bound), (2, bound, 0, width - bound)])
    qa_pieces, a_masks = spread(qa, bits)
    qb_pieces, b_masks = spread(qb, bits[::-1])
    masks = (a_masks, b_masks)
    weights = [(spread(k, bits)[0], spread(v, bits[::-1])[0]) for k, v in ((k0, v0), (k1, v1))]

    table, *sent = call(
        dispatch_kernel,
        [shape((count, 8), jnp.float32)] + [shape((CAP, model), bf16)] * experts,
        [SMEM, VMEM, VMEM, VMEM],
        here,
        routes.T,
        gate_levels.T,
        hidden,
        flops=2 * count * length * model,
    )

    def route(array, k):
        return swap(array, "mem", k)

    arrived = call(
        join_kernel,
        shape((length, model), bf16),
        [SMEM] + [VMEM] * experts,
        here,
        sent[0],
        *[route(sent[k], k) for k in range(1, experts)],
    )

    mine = call(
        functools.partial(rows_kernel, masks=masks),
        shape((model, quarter), bf16),
        [SMEM] + [VMEM] * (2 * groups),
        here,
        *qa_pieces,
        *qb_pieces,
    )
    quarter1 = swap(mine, "mem", 1)
    quarter2 = swap(mine, "mem", 2)
    quarter3 = swap(quarter2, "mem", 1)
    queries = call(
        query_kernel,
        shape((length, width), bf16),
        [SMEM] + [VMEM] * 5,
        here,
        arrived,
        mine,
        quarter1,
        quarter2,
        quarter3,
        flops=2 * length * model * width,
    )

    out = None
    for c, (first, heads) in enumerate(chunks):
        cols = heads * DK
        keys, values, total = call(
            functools.partial(kv_kernel, masks=masks),
            [
                shape((length, cols), bf16),
                shape((length, cols), bf16),
                shape((heads, DK, DK), bf16),
            ],
            [SMEM, VMEM] + [VMEM] * (2 * groups),
            here,
            arrived,
            *weights[c][0],
            *weights[c][1],
            flops=4 * length * model * cols,
        )
        states = []
        for m in range(1, groups):
            states.append(swap(total, "seq", m))
        normed = call(
            functools.partial(attend_kernel, first=first),
            shape((length, cols), bf16),
            [SMEM] + [VMEM] * (3 + len(states)),
            here,
            queries,
            keys,
            values,
            *states,
            flops=4 * length * length * cols,
        )
        back = lax.all_to_all(
            normed.reshape(experts, CAP, cols), "mem", split_axis=0, concat_axis=0, tiled=True
        )
        back = back.reshape(length, cols)
        prior = [] if out is None else [out]
        out = call(
            combine_kernel,
            shape((count, first * DK + cols), bf16),
            [VMEM] * (2 + len(prior)),
            table,
            back,
            *prior,
            last=c + 1 == len(chunks),
        )
    return out


def solution(mesh):
    return jax.shard_map(
        on_device,
        mesh=mesh,
        in_specs=(
            P(("seq", "mem"), None),
            P(("seq", "mem"), None),
            P(("seq", "mem"), None),
            P("seq", None),
            P("mem", "seq", None),
            P("mem", "seq", None),
        ),
        out_specs=P(("seq", "mem"), None),
        check_vma=False,
    )
```

time: 164 us -> 204 us (1.24)
  waiting for transfers between devices: 84.3 us -> 118 us
  starting transfers between devices: 48.5 us -> 57.6 us
  local copies, waits for them, and re-layouts: 5.07 us -> 0.02 us
  Pallas kernels: 24.8 us -> 27.2 us
    ppermute x27 -> x34, waiting for transfers between devices: 77.2 us -> 106 us  [swap(): lax.ppermute(array, axis, [(i, i ^ mask) for i in range(lax.axis_size(axi...]
    all_to_all x2, starting transfers between devices: 9.58 us -> 18.8 us  [on_device(): lax.all_to_all(normed.reshape(experts, CAP, cols), 'mem', split_axis=0, c...]
    unnamed x22 -> x10, local copies, waits for them, and re-layouts: 5.07 us -> 0.02 us
    all_to_all x2, waiting for transfers between devices: 7.12 us -> 11.9 us  [on_device(): lax.all_to_all(normed.reshape(experts, CAP, cols), 'mem', split_axis=0, c...]
    pallas_call x10 -> x13, Pallas kernels: 24.8 us -> 27.2 us  [call(): pl.pallas_call(kernel, out_shape=outs if last else jax.tree.map(lambda s:...]
    ppermute x27 -> x34, starting transfers between devices: 38.9 us -> 38.8 us  [swap(): lax.ppermute(array, axis, [(i, i ^ mask) for i in range(lax.axis_size(axi...]
  transfers between devices with their start and end apart: 29 -> 36, of which waited for: 14 -> 21; matrix products, arithmetic and copies ran while one was open for 0% -> 0% of each run, Pallas kernels for 10% -> 10%
where the time goes in v2:
time: 204 us; the launch traced here: 203 us
  waiting for transfers between devices  118 us (58%)
  starting transfers between devices  57.6 us (28%)
  Pallas kernels  27.2 us (13%)
    ppermute x34, waiting for transfers between devices, swap(): lax.ppermute(array, axis, [(i, i ^ mask) for i in range(lax.axis_size(axi...  106 us
    ppermute x34, starting transfers between devices, swap(): lax.ppermute(array, axis, [(i, i ^ mask) for i in range(lax.axis_size(axi...  38.8 us
    pallas_call x13, Pallas kernels, call(): pl.pallas_call(kernel, out_shape=outs if last else jax.tree.map(lambda s:...  27.2 us
    all_to_all x2, starting transfers between devices, on_device(): lax.all_to_all(normed.reshape(experts, CAP, cols), 'mem', split_axis=0, c...  18.8 us
    all_to_all x2, waiting for transfers between devices, on_device(): lax.all_to_all(normed.reshape(experts, CAP, cols), 'mem', split_axis=0, c...  11.9 us
  transfers between devices with their start and end apart: 36, of which 21 were waited for; matrix products, arithmetic and copies ran while one was open for 0% of the time, Pallas kernels for 10%

profile of v2, /device:TPU:0, one launch (start us, length us, event | category | flops | bytes accessed | tf_op | source)
XLA Modules:
  0.0 203.3 jit_solution(14496841501201881864)
XLA Ops:
  0.1 1.5 shard_map.66
  1.6 3.1 %collective-permute-start.10 = (bf16[512,128]{1,0:T(8,128)(2,1)S(1)}, bf16[512,128]{1,0:T(8,128)(2,1)S(1)}, u32[]{:S(2)}, u32[]{:S(2)}) collective-permute-start(bf16[512,128]{1,0:T(8,128)(2,1)S(1)} %get-tuple-element.36.refs_4_), channel_id=1, source_target_pairs={{0,16},{8,24},{16,0},{24,8},{1,17},{9,25},{17,1},{25,9},{2,18},{10... | collective-permute-start | bytes 393224 | tf_op jit(solution)/shard_map/ppermute | solution.py:24
  4.7 1.5 collective-permute-start.7
  6.2 0.5 collective-permute-start.11
  6.8 1.8 collective-permute-done.10.refs_5_
  8.6 1.5 collective-permute-start.12
  10.0 1.0 collective-permute-done.7.refs_1_
  11.1 1.5 collective-permute-start.9
  12.5 1.3 collective-permute-done.11.refs_6_
  13.9 1.4 collective-permute-done.12.refs_7_
  15.3 0.8 collective-permute-done.9.refs_3_
  16.0 0.7 shard_map.67.refs_0_
  16.7 1.6 collective-permute-start.14
  18.4 2.3 %shard_map.64 = (f32[256,8]{1,0:T(8,128)S(1)}, bf16[64,2048]{1,0:T(8,128)(2,1)S(1)}, bf16[64,2048]{1,0:T(8,128)(2,1)S(1)}, bf16[64,2048]{1,0:T(8,128)(2,1)S(1)},...) custom-call(s32[2]{0:T(128)S(1)} %pad_add_fusion.here, ...), custom_call_target="tpu_custom_call" | custom-call | flops 536870912 | bytes 1048576 | tf_op jit(solution)/shard_map/pallas_call | solution.py:169
  20.8 0.5 collective-permute-start.1
  21.3 1.3 collective-permute-start.2
  22.6 2.6 %collective-permute-start.3 = (bf16[64,2048]{1,0:T(8,128)(2,1)S(1)}, bf16[64,2048]{1,0:T(8,128)(2,1)S(1)}, u32[]{:S(2)}, u32[]{:S(2)}) collective-permute-start(bf16[64,2048]{1,0:T(8,128)(2,1)S(1)} %get-tuple-element.31), channel_id=1, source_target_pairs={{0,4},{1,5},{2,6},{3,7},{4,0},{5,1},{6,2},{7,3},{8,12},{9,13},{10,... | collective-permute-start | bytes 786440 | tf_op jit(solution)/shard_map/ppermute | solution.py:24
  25.2 34.3 %collective-permute-done.1.refs_2_ = bf16[64,2048]{1,0:T(8,128)(2,1)S(1)} collective-permute-done((bf16[64,2048]{1,0:T(8,128)(2,1)S(1)}, bf16[64,2048]{1,0:T(8,128)(2,1)S(1)}, u32[]{:S(2)}, u32[]{:S(2)}) %collective-permute-start.1) | collective-permute-done | bytes 262176 | tf_op jit(solution)/shard_map/ppermute | solution.py:24
  59.5 3.9 %collective-permute-start.5 = (bf16[64,2048]{1,0:T(8,128)(2,1)S(1)}, bf16[64,2048]{1,0:T(8,128)(2,1)S(1)}, u32[]{:S(2)}, u32[]{:S(2)}) collective-permute-start(bf16[64,2048]{1,0:T(8,128)(2,1)S(1)} %get-tuple-element.33), channel_id=1, source_target_pairs={{0,6},{1,7},{2,4},{3,5},{4,2},{5,3},{6,0},{7,1},{8,14},{9,15},{10,... | collective-permute-start | bytes 786440 | tf_op jit(solution)/shard_map/ppermute | solution.py:24
  63.4 1.8 shard_map.72
  65.3 1.6 collective-permute-start.25
  66.8 0.5 collective-permute-start.28
  67.4 1.5 collective-permute-start.26
  68.9 1.2 collective-permute-done.5.refs_6_
  70.0 0.8 collective-permute-start.6
  70.8 8.0 %collective-permute-done.6.refs_7_ = bf16[64,2048]{1,0:T(8,128)(2,1)S(1)} collective-permute-done((bf16[64,2048]{1,0:T(8,128)(2,1)S(1)}, bf16[64,2048]{1,0:T(8,128)(2,1)S(1)}, u32[]{:S(2)}, u32[]{:S(2)}) %collective-permute-start.6) | collective-permute-done | bytes 262176 | tf_op jit(solution)/shard_map/ppermute | solution.py:24
  78.9 0.5 collective-permute-start.15
  79.6 1.5 collective-permute-start.29
  81.1 3.3 %collective-permute-done.28.refs_5_ = bf16[512,640]{1,0:T(8,128)(2,1)S(1)} collective-permute-done((bf16[512,640]{1,0:T(8,128)(2,1)S(1)}, bf16[512,640]{1,0:T(8,128)(2,1)S(1)}, u32[]{:S(2)}, u32[]{:S(2)}) %collective-permute-start.28) | collective-permute-done | bytes 655392 | tf_op jit(solution)/shard_map/ppermute | solution.py:24
  84.5 0.5 collective-permute-start.27
  85.0 13.5 %collective-permute-done.26.refs_2_ = bf16[512,640]{1,0:T(8,128)(2,1)S(1)} collective-permute-done((bf16[512,640]{1,0:T(8,128)(2,1)S(1)}, bf16[512,640]{1,0:T(8,128)(2,1)S(1)}, u32[]{:S(2)}, u32[]{:S(2)}) %collective-permute-start.26) | collective-permute-done | bytes 655392 | tf_op jit(solution)/shard_map/ppermute | solution.py:24
  98.5 0.5 collective-permute-start.30
  99.0 0.7 shard_map.65.x
  99.7 9.2 %collective-permute-done.27.refs_3_ = bf16[512,640]{1,0:T(8,128)(2,1)S(1)} collective-permute-done((bf16[512,640]{1,0:T(8,128)(2,1)S(1)}, bf16[512,640]{1,0:T(8,128)(2,1)S(1)}, u32[]{:S(2)}, u32[]{:S(2)}) %collective-permute-start.27) | collective-permute-done | bytes 655392 | tf_op jit(solution)/shard_map/ppermute | solution.py:24
  108.9 1.2 collective-permute-done.30.refs_7_
  110.1 4.6 %shard_map.73 = (bf16[512,640]{1,0:T(8,128)(2,1)S(1)}, bf16[512,640]{1,0:T(8,128)(2,1)S(1)}, bf16[5,128,128]{2,1,0:T(8,128)(2,1)S(1)}) custom-call(s32[2]{0:T(128)S(1)} %pad_add_fusion.here, bf16[512,2048]{1,0:T(8,128)(2,1)S(1)} %shard_map.65.x, bf16[512,640]{1,0:T(8,128)(2,1)S(1)} %get-tuple-element.42.refs_0_, ...), custom_call_target="tpu_custom_call" | custom-call | flops 2684354560 | bytes 1048576 | tf_op jit(solution)/shard_map/pallas_call | solution.py:169
  114.7 1.6 collective-permute-start.31
  116.3 0.5 collective-permute-start.32
  116.8 1.5 collective-permute-start.33
  118.3 3.0 %shard_map.68.q_all = bf16[512,1024]{1,0:T(8,128)(2,1)S(1)} custom-call(s32[2]{0:T(128)S(1)} %pad_add_fusion.here, bf16[512,2048]{1,0:T(8,128)(2,1)S(1)} %shard_map.65.x, bf16[2048,256]{1,0:T(8,128)(2,1)S(1)} %shard_map.67.refs_0_, bf16[2048,256]{1,0:T(8,128)(2,1)S(1)} %collective-permute-done.13.refs_1_, ...), custom_call_target="tpu_custom_call" | custom-call | flops 2147483648 | bytes 1048576 | tf_op jit(solution)/shard_map/pallas_call | solution.py:169
  121.2 2.1 %collective-permute-done.32.refs_1_ = bf16[5,128,128]{2,1,0:T(8,128)(2,1)S(1)} collective-permute-done((bf16[5,128,128]{2,1,0:T(8,128)(2,1)S(1)}, bf16[5,128,128]{2,1,0:T(8,128)(2,1)S(1)}, u32[]{:S(2)}, u32[]{:S(2)}) %collective-permute-start.32) | collective-permute-done | bytes 163872 | tf_op jit(solution)/shard_map/ppermute | solution.py:24
  123.3 3.2 %shard_map.74 = bf16[512,640]{1,0:T(8,128)(2,1)} custom-call(s32[2]{0:T(128)S(1)} %pad_add_fusion.here, bf16[512,1024]{1,0:T(8,128)(2,1)S(1)} %shard_map.68.q_all, bf16[512,640]{1,0:T(8,128)(2,1)S(1)} %get-tuple-element.44.k, bf16[512,640]{1,0:T(8,128)(2,1)S(1)} %get-tuple-element.45.v, bf16[5,128,128]{2,1,0:T(8,128)(2,1)S(1)} %collective-permute-done.31.refs_0_, ...), custom_call_target="tpu_custom_call" | custom-call | flops 671088640 | bytes 1048576 | tf_op jit(solution)/shard_map/pallas_call | solution.py:169
  126.6 14.4 %all-to-all-start.1 = ((bf16[8,64,640]{2,1,0:T(8,128)(2,1)}), bf16[8,64,640]{2,1,0:T(8,128)(2,1)S(1)}, u32[]{:S(2)}, u32[]{:S(2)}) async-start(bf16[8,64,640]{2,1,0:T(8,128)(2,1)} %bitcast.6), calls=%async_computation.1 | async-start | bytes 1310720 | tf_op jit(solution)/shard_map/all_to_all | solution.py:301
  141.0 1.8 shard_map.69
  142.8 0.7 collective-permute-start.16
  143.5 1.1 collective-permute-start.19
  144.6 0.9 collective-permute-start.17
  145.5 1.4 collective-permute-start.20
  146.9 7.9 %collective-permute-done.16.refs_1_ = bf16[512,384]{1,0:T(8,128)(2,1)S(1)} collective-permute-done((bf16[512,384]{1,0:T(8,128)(2,1)S(1)}, bf16[512,384]{1,0:T(8,128)(2,1)S(1)}, u32[]{:S(2)}, u32[]{:S(2)}) %collective-permute-start.16) | collective-permute-done | bytes 393248 | tf_op jit(solution)/shard_map/ppermute | solution.py:24
  154.8 0.5 collective-permute-start.18
  155.5 1.4 collective-permute-start.21
  156.8 7.1 %collective-permute-done.17.refs_2_ = bf16[512,384]{1,0:T(8,128)(2,1)S(1)} collective-permute-done((bf16[512,384]{1,0:T(8,128)(2,1)S(1)}, bf16[512,384]{1,0:T(8,128)(2,1)S(1)}, u32[]{:S(2)}, u32[]{:S(2)}) %collective-permute-start.17) | collective-permute-done | bytes 393248 | tf_op jit(solution)/shard_map/ppermute | solution.py:24
  163.9 7.7 %collective-permute-done.18.refs_3_ = bf16[512,384]{1,0:T(8,128)(2,1)S(1)} collective-permute-done((bf16[512,384]{1,0:T(8,128)(2,1)S(1)}, bf16[512,384]{1,0:T(8,128)(2,1)S(1)}, u32[]{:S(2)}, u32[]{:S(2)}) %collective-permute-start.18) | collective-permute-done | bytes 393248 | tf_op jit(solution)/shard_map/ppermute | solution.py:24
  171.6 3.2 %shard_map.70 = (bf16[512,384]{1,0:T(8,128)(2,1)S(1)}, bf16[512,384]{1,0:T(8,128)(2,1)S(1)}, bf16[3,128,128]{2,1,0:T(8,128)(2,1)S(1)}) custom-call(s32[2]{0:T(128)S(1)} %pad_add_fusion.here, bf16[512,2048]{1,0:T(8,128)(2,1)S(1)} %copy-done.1, bf16[512,384]{1,0:T(8,128)(2,1)S(1)} %get-tuple-element.37.refs_0_, ...), custom_call_target="tpu_custom_call" | custom-call | flops 1610612736 | bytes 1048576 | tf_op jit(solution)/shard_map/pallas_call | solution.py:169
  174.7 1.4 collective-permute-start.22
  176.2 0.5 collective-permute-start.23
  176.7 1.6 collective-permute-start.24
  178.3 1.5 collective-permute-done.22.refs_0_
  179.8 2.8 %collective-permute-done.23.refs_1_ = bf16[3,128,128]{2,1,0:T(8,128)(2,1)S(1)} collective-permute-done((bf16[3,128,128]{2,1,0:T(8,128)(2,1)S(1)}, bf16[3,128,128]{2,1,0:T(8,128)(2,1)S(1)}, u32[]{:S(2)}, u32[]{:S(2)}) %collective-permute-start.23) | collective-permute-done | bytes 98336 | tf_op jit(solution)/shard_map/ppermute | solution.py:24
  182.6 2.6 %shard_map.71 = bf16[512,384]{1,0:T(8,128)(2,1)} custom-call(s32[2]{0:T(128)S(1)} %pad_add_fusion.here, bf16[512,1024]{1,0:T(8,128)(2,1)S(1)} %shard_map.68.q_all, bf16[512,384]{1,0:T(8,128)(2,1)S(1)} %get-tuple-element.39.k, bf16[512,384]{1,0:T(8,128)(2,1)S(1)} %get-tuple-element.40.v, bf16[3,128,128]{2,1,0:T(8,128)(2,1)S(1)} %collective-permute-done.22.refs_0_, ...), custom_call_target="tpu_custom_call" | custom-call | flops 402653184 | bytes 1048576 | tf_op jit(solution)/shard_map/pallas_call | solution.py:169
  185.1 4.4 %all-to-all-start = ((bf16[8,64,384]{2,1,0:T(8,128)(2,1)}), bf16[8,64,384]{2,1,0:T(8,128)(2,1)S(1)}, u32[]{:S(2)}, u32[]{:S(2)}) async-start(bf16[8,64,384]{2,1,0:T(8,128)(2,1)} %bitcast.4), calls=%async_computation | async-start | bytes 786432 | tf_op jit(solution)/shard_map/all_to_all | solution.py:301
  189.5 0.6 shard_map.75.refs_0_
  190.2 11.9 %all-to-all-done = bf16[8,64,384]{2,1,0:T(8,128)(2,1)S(1)} async-done(((bf16[8,64,384]{2,1,0:T(8,128)(2,1)}), bf16[8,64,384]{2,1,0:T(8,128)(2,1)S(1)}, u32[]{:S(2)}, u32[]{:S(2)}) %all-to-all-start) | async-done | bytes 393248 | tf_op jit(solution)/shard_map/all_to_all | solution.py:301
  202.0 1.3 shard_map.76
  (32 shorter events, 0.7 us)
Async XLA Ops:
  0.1 18.3 %copy-start.2 = (bf16[256,2048]{1,0:T(8,128)(2,1)S(1)}, bf16[256,2048]{1,0:T(8,128)(2,1)}, u32[]{:S(2)}) copy-start(bf16[256,2048]{1,0:T(8,128)(2,1)} %hidden.1) | copy-start | bytes 3145732
  0.1 18.3 %copy-start.3 = (s32[256,2]{0,1:T(2,128)S(1)}, s32[256,2]{0,1:T(2,128)}, u32[]{:S(2)}) copy-start(s32[256,2]{0,1:T(2,128)} %param.7) | copy-start | bytes 6148
  0.1 18.3 %copy-start.4 = (s32[256,2]{0,1:T(2,128)S(1)}, s32[256,2]{0,1:T(2,128)}, u32[]{:S(2)}) copy-start(s32[256,2]{0,1:T(2,128)} %param.8) | copy-start | bytes 6148
  1.6 6.9 %collective-permute-start.10 = (bf16[512,128]{1,0:T(8,128)(2,1)S(1)}, bf16[512,128]{1,0:T(8,128)(2,1)S(1)}, u32[]{:S(2)}, u32[]{:S(2)}) collective-permute-start(bf16[512,128]{1,0:T(8,128)(2,1)S(1)} %get-tuple-element.36.refs_4_), channel_id=1, source_target_pairs={{0,16},{8,24},{16,0},{24,8},{1,17},{9,25},{17,1},{25,9},{2,18},{10... | collective-permute-start | bytes 393224 | tf_op jit(solution)/shard_map/ppermute | solution.py:24
  4.7 6.4 %collective-permute-start.7 = (bf16[512,128]{1,0:T(8,128)(2,1)S(1)}, bf16[512,128]{1,0:T(8,128)(2,1)S(1)}, u32[]{:S(2)}, u32[]{:S(2)}) collective-permute-start(bf16[512,128]{1,0:T(8,128)(2,1)S(1)} %get-tuple-element.35.refs_0_), channel_id=1, source_target_pairs={{0,8},{8,0},{16,24},{24,16},{1,9},{9,1},{17,25},{25,17},{2,10},{10... | collective-permute-start | bytes 393224 | tf_op jit(solution)/shard_map/ppermute | solution.py:24
  6.2 7.7 %collective-permute-start.11 = (bf16[512,128]{1,0:T(8,128)(2,1)S(1)}, bf16[512,128]{1,0:T(8,128)(2,1)S(1)}, u32[]{:S(2)}, u32[]{:S(2)}) collective-permute-start(bf16[512,128]{1,0:T(8,128)(2,1)S(1)} %get-tuple-element.36.refs_4_), channel_id=1, source_target_pairs={{0,8},{8,0},{16,24},{24,16},{1,9},{9,1},{17,25},{25,17},{2,10},{10... | collective-permute-start | bytes 393224 | tf_op jit(solution)/shard_map/ppermute | solution.py:24
  6.7 7.1 %collective-permute-start.8 = (bf16[512,128]{1,0:T(8,128)(2,1)S(1)}, bf16[512,128]{1,0:T(8,128)(2,1)S(1)}, u32[]{:S(2)}, u32[]{:S(2)}) collective-permute-start(bf16[512,128]{1,0:T(8,128)(2,1)S(1)} %get-tuple-element.35.refs_0_), channel_id=1, source_target_pairs={{0,16},{8,24},{16,0},{24,8},{1,17},{9,25},{17,1},{25,9},{2,18},{10... | collective-permute-start | bytes 393224 | tf_op jit(solution)/shard_map/ppermute | solution.py:24
  8.6 6.7 %collective-permute-start.12 = (bf16[512,128]{1,0:T(8,128)(2,1)S(1)}, bf16[512,128]{1,0:T(8,128)(2,1)S(1)}, u32[]{:S(2)}, u32[]{:S(2)}) collective-permute-start(bf16[512,128]{1,0:T(8,128)(2,1)S(1)} %collective-permute-done.10.refs_5_), channel_id=1, source_target_pairs={{0,8},{8,0},{16,24},{24,16},{1,9},{9,1},{17,25},{25,17},{2,10},{10... | collective-permute-start | bytes 393224 | tf_op jit(solution)/shard_map/ppermute | solution.py:24
  11.1 5.0 %collective-permute-start.9 = (bf16[512,128]{1,0:T(8,128)(2,1)S(1)}, bf16[512,128]{1,0:T(8,128)(2,1)S(1)}, u32[]{:S(2)}, u32[]{:S(2)}) collective-permute-start(bf16[512,128]{1,0:T(8,128)(2,1)S(1)} %collective-permute-done.7.refs_1_), channel_id=1, source_target_pairs={{0,16},{8,24},{16,0},{24,8},{1,17},{9,25},{17,1},{25,9},{2,18},{10... | collective-permute-start | bytes 393224 | tf_op jit(solution)/shard_map/ppermute | solution.py:24
  16.7 62.1 %collective-permute-start.14 = (bf16[2048,256]{1,0:T(8,128)(2,1)S(1)}, bf16[2048,256]{1,0:T(8,128)(2,1)S(1)}, u32[]{:S(2)}, u32[]{:S(2)}) collective-permute-start(bf16[2048,256]{1,0:T(8,128)(2,1)S(1)} %shard_map.67.refs_0_), channel_id=1, source_target_pairs={{0,2},{1,3},{2,0},{3,1},{4,6},{5,7},{6,4},{7,5},{8,10},{9,11},{10,... | collective-permute-start | bytes 3145736 | tf_op jit(solution)/shard_map/ppermute | solution.py:24
  20.7 4.5 %collective-permute-start = (bf16[64,2048]{1,0:T(8,128)(2,1)S(1)}, bf16[64,2048]{1,0:T(8,128)(2,1)S(1)}, u32[]{:S(2)}, u32[]{:S(2)}) collective-permute-start(bf16[64,2048]{1,0:T(8,128)(2,1)S(1)} %get-tuple-element.28), channel_id=1, source_target_pairs={{0,1},{1,0},{2,3},{3,2},{4,5},{5,4},{6,7},{7,6},{8,9},{9,8},{10,11... | collective-permute-start | bytes 786440 | tf_op jit(solution)/shard_map/ppermute | solution.py:24
  20.8 38.7 %collective-permute-start.1 = (bf16[64,2048]{1,0:T(8,128)(2,1)S(1)}, bf16[64,2048]{1,0:T(8,128)(2,1)S(1)}, u32[]{:S(2)}, u32[]{:S(2)}) collective-permute-start(bf16[64,2048]{1,0:T(8,128)(2,1)S(1)} %get-tuple-element.29), channel_id=1, source_target_pairs={{0,2},{1,3},{2,0},{3,1},{4,6},{5,7},{6,4},{7,5},{8,10},{9,11},{10,... | collective-permute-start | bytes 786440 | tf_op jit(solution)/shard_map/ppermute | solution.py:24
  21.3 44.0 %collective-permute-start.2 = (bf16[64,2048]{1,0:T(8,128)(2,1)S(1)}, bf16[64,2048]{1,0:T(8,128)(2,1)S(1)}, u32[]{:S(2)}, u32[]{:S(2)}) collective-permute-start(bf16[64,2048]{1,0:T(8,128)(2,1)S(1)} %get-tuple-element.30), channel_id=1, source_target_pairs={{0,3},{1,2},{2,1},{3,0},{4,7},{5,6},{6,5},{7,4},{8,11},{9,10},{10,... | collective-permute-start | bytes 786440 | tf_op jit(solution)/shard_map/ppermute | solution.py:24
  22.6 44.2 %collective-permute-start.3 = (bf16[64,2048]{1,0:T(8,128)(2,1)S(1)}, bf16[64,2048]{1,0:T(8,128)(2,1)S(1)}, u32[]{:S(2)}, u32[]{:S(2)}) collective-permute-start(bf16[64,2048]{1,0:T(8,128)(2,1)S(1)} %get-tuple-element.31), channel_id=1, source_target_pairs={{0,4},{1,5},{2,6},{3,7},{4,0},{5,1},{6,2},{7,3},{8,12},{9,13},{10,... | collective-permute-start | bytes 786440 | tf_op jit(solution)/shard_map/ppermute | solution.py:24
  25.2 42.2 %collective-permute-start.4 = (bf16[64,2048]{1,0:T(8,128)(2,1)S(1)}, bf16[64,2048]{1,0:T(8,128)(2,1)S(1)}, u32[]{:S(2)}, u32[]{:S(2)}) collective-permute-start(bf16[64,2048]{1,0:T(8,128)(2,1)S(1)} %get-tuple-element.32), channel_id=1, source_target_pairs={{0,5},{1,4},{2,7},{3,6},{4,1},{5,0},{6,3},{7,2},{8,13},{9,12},{10,... | collective-permute-start | bytes 786440 | tf_op jit(solution)/shard_map/ppermute | solution.py:24
  59.5 10.6 %collective-permute-start.5 = (bf16[64,2048]{1,0:T(8,128)(2,1)S(1)}, bf16[64,2048]{1,0:T(8,128)(2,1)S(1)}, u32[]{:S(2)}, u32[]{:S(2)}) collective-permute-start(bf16[64,2048]{1,0:T(8,128)(2,1)S(1)} %get-tuple-element.33), channel_id=1, source_target_pairs={{0,6},{1,7},{2,4},{3,5},{4,2},{5,3},{6,0},{7,1},{8,14},{9,15},{10,... | collective-permute-start | bytes 786440 | tf_op jit(solution)/shard_map/ppermute | solution.py:24
  65.3 14.4 %collective-permute-start.25 = (bf16[512,640]{1,0:T(8,128)(2,1)S(1)}, bf16[512,640]{1,0:T(8,128)(2,1)S(1)}, u32[]{:S(2)}, u32[]{:S(2)}) collective-permute-start(bf16[512,640]{1,0:T(8,128)(2,1)S(1)} %get-tuple-element.42.refs_0_), channel_id=1, source_target_pairs={{0,8},{8,0},{16,24},{24,16},{1,9},{9,1},{17,25},{25,17},{2,10},{10... | collective-permute-start | bytes 1966088 | tf_op jit(solution)/shard_map/ppermute | solution.py:24
  66.8 17.6 %collective-permute-start.28 = (bf16[512,640]{1,0:T(8,128)(2,1)S(1)}, bf16[512,640]{1,0:T(8,128)(2,1)S(1)}, u32[]{:S(2)}, u32[]{:S(2)}) collective-permute-start(bf16[512,640]{1,0:T(8,128)(2,1)S(1)} %get-tuple-element.43.refs_4_), channel_id=1, source_target_pairs={{0,16},{8,24},{16,0},{24,8},{1,17},{9,25},{17,1},{25,9},{2,18},{10... | collective-permute-start | bytes 1966088 | tf_op jit(solution)/shard_map/ppermute | solution.py:24
  67.4 31.1 %collective-permute-start.26 = (bf16[512,640]{1,0:T(8,128)(2,1)S(1)}, bf16[512,640]{1,0:T(8,128)(2,1)S(1)}, u32[]{:S(2)}, u32[]{:S(2)}) collective-permute-start(bf16[512,640]{1,0:T(8,128)(2,1)S(1)} %get-tuple-element.42.refs_0_), channel_id=1, source_target_pairs={{0,16},{8,24},{16,0},{24,8},{1,17},{9,25},{17,1},{25,9},{2,18},{10... | collective-permute-start | bytes 1966088 | tf_op jit(solution)/shard_map/ppermute | solution.py:24
  70.0 8.8 %collective-permute-start.6 = (bf16[64,2048]{1,0:T(8,128)(2,1)S(1)}, bf16[64,2048]{1,0:T(8,128)(2,1)S(1)}, u32[]{:S(2)}, u32[]{:S(2)}) collective-permute-start(bf16[64,2048]{1,0:T(8,128)(2,1)S(1)} %get-tuple-element.34), channel_id=1, source_target_pairs={{0,7},{1,6},{2,5},{3,4},{4,3},{5,2},{6,1},{7,0},{8,15},{9,14},{10,... | collective-permute-start | bytes 786440 | tf_op jit(solution)/shard_map/ppermute | solution.py:24
  78.9 39.4 %collective-permute-start.13 = (bf16[2048,256]{1,0:T(8,128)(2,1)S(1)}, bf16[2048,256]{1,0:T(8,128)(2,1)S(1)}, u32[]{:S(2)}, u32[]{:S(2)}) collective-permute-start(bf16[2048,256]{1,0:T(8,128)(2,1)S(1)} %shard_map.67.refs_0_), channel_id=1, source_target_pairs={{0,1},{1,0},{2,3},{3,2},{4,5},{5,4},{6,7},{7,6},{8,9},{9,8},{10,11... | collective-permute-start | bytes 3145736 | tf_op jit(solution)/shard_map/ppermute | solution.py:24
  78.9 39.4 %collective-permute-start.15 = (bf16[2048,256]{1,0:T(8,128)(2,1)S(1)}, bf16[2048,256]{1,0:T(8,128)(2,1)S(1)}, u32[]{:S(2)}, u32[]{:S(2)}) collective-permute-start(bf16[2048,256]{1,0:T(8,128)(2,1)S(1)} %collective-permute-done.14.refs_2_), channel_id=1, source_target_pairs={{0,1},{1,0},{2,3},{3,2},{4,5},{5,4},{6,7},{7,6},{8,9},{9,8},{10,11... | collective-permute-start | bytes 3145736 | tf_op jit(solution)/shard_map/ppermute | solution.py:24
  79.6 20.1 %collective-permute-start.29 = (bf16[512,640]{1,0:T(8,128)(2,1)S(1)}, bf16[512,640]{1,0:T(8,128)(2,1)S(1)}, u32[]{:S(2)}, u32[]{:S(2)}) collective-permute-start(bf16[512,640]{1,0:T(8,128)(2,1)S(1)} %get-tuple-element.43.refs_4_), channel_id=1, source_target_pairs={{0,8},{8,0},{16,24},{24,16},{1,9},{9,1},{17,25},{25,17},{2,10},{10... | collective-permute-start | bytes 1966088 | tf_op jit(solution)/shard_map/ppermute | solution.py:24
  84.5 24.5 %collective-permute-start.27 = (bf16[512,640]{1,0:T(8,128)(2,1)S(1)}, bf16[512,640]{1,0:T(8,128)(2,1)S(1)}, u32[]{:S(2)}, u32[]{:S(2)}) collective-permute-start(bf16[512,640]{1,0:T(8,128)(2,1)S(1)} %collective-permute-done.25.refs_1_), channel_id=1, source_target_pairs={{0,16},{8,24},{16,0},{24,8},{1,17},{9,25},{17,1},{25,9},{2,18},{10... | collective-permute-start | bytes 1966088 | tf_op jit(solution)/shard_map/ppermute | solution.py:24
  98.5 11.6 %collective-permute-start.30 = (bf16[512,640]{1,0:T(8,128)(2,1)S(1)}, bf16[512,640]{1,0:T(8,128)(2,1)S(1)}, u32[]{:S(2)}, u32[]{:S(2)}) collective-permute-start(bf16[512,640]{1,0:T(8,128)(2,1)S(1)} %collective-permute-done.28.refs_5_), channel_id=1, source_target_pairs={{0,8},{8,0},{16,24},{24,16},{1,9},{9,1},{17,25},{25,17},{2,10},{10... | collective-permute-start | bytes 1966088 | tf_op jit(solution)/shard_map/ppermute | solution.py:24
  99.7 18.6 %copy-start = (bf16[512,2048]{1,0:T(8,128)(2,1)}, bf16[512,2048]{1,0:T(8,128)(2,1)S(1)}, u32[]{:S(2)}) copy-start(bf16[512,2048]{1,0:T(8,128)(2,1)S(1)} %shard_map.65.x) | copy-start | bytes 6291460
  114.7 6.5 %collective-permute-start.31 = (bf16[5,128,128]{2,1,0:T(8,128)(2,1)S(1)}, bf16[5,128,128]{2,1,0:T(8,128)(2,1)S(1)}, u32[]{:S(2)}, u32[]{:S(2)}) collective-permute-start(bf16[5,128,128]{2,1,0:T(8,128)(2,1)S(1)} %get-tuple-element.46), channel_id=1, source_target_pairs={{0,8},{8,0},{16,24},{24,16},{1,9},{9,1},{17,25},{25,17},{2,10},{10... | collective-permute-start | bytes 491528 | tf_op jit(solution)/shard_map/ppermute | solution.py:24
  116.3 7.1 %collective-permute-start.32 = (bf16[5,128,128]{2,1,0:T(8,128)(2,1)S(1)}, bf16[5,128,128]{2,1,0:T(8,128)(2,1)S(1)}, u32[]{:S(2)}, u32[]{:S(2)}) collective-permute-start(bf16[5,128,128]{2,1,0:T(8,128)(2,1)S(1)} %get-tuple-element.46), channel_id=1, source_target_pairs={{0,16},{8,24},{16,0},{24,8},{1,17},{9,25},{17,1},{25,9},{2,18},{10... | collective-permute-start | bytes 491528 | tf_op jit(solution)/shard_map/ppermute | solution.py:24
  116.8 6.6 %collective-permute-start.33 = (bf16[5,128,128]{2,1,0:T(8,128)(2,1)S(1)}, bf16[5,128,128]{2,1,0:T(8,128)(2,1)S(1)}, u32[]{:S(2)}, u32[]{:S(2)}) collective-permute-start(bf16[5,128,128]{2,1,0:T(8,128)(2,1)S(1)} %get-tuple-element.46), channel_id=1, source_target_pairs={{0,24},{8,16},{16,8},{24,0},{1,25},{9,17},{17,9},{25,1},{2,26},{10... | collective-permute-start | bytes 491528 | tf_op jit(solution)/shard_map/ppermute | solution.py:24
  126.6 58.6 %all-to-all-start.1 = ((bf16[8,64,640]{2,1,0:T(8,128)(2,1)}), bf16[8,64,640]{2,1,0:T(8,128)(2,1)S(1)}, u32[]{:S(2)}, u32[]{:S(2)}) async-start(bf16[8,64,640]{2,1,0:T(8,128)(2,1)} %bitcast.6), calls=%async_computation.1 | async-start | bytes 1310720 | tf_op jit(solution)/shard_map/all_to_all | solution.py:301
  141.0 30.6 %copy-start.1 = (bf16[512,2048]{1,0:T(8,128)(2,1)S(1)}, bf16[512,2048]{1,0:T(8,128)(2,1)}, u32[]{:S(2)}) copy-start(bf16[512,2048]{1,0:T(8,128)(2,1)} %copy-done) | copy-start | bytes 6291460
  142.8 12.1 %collective-permute-start.16 = (bf16[512,384]{1,0:T(8,128)(2,1)S(1)}, bf16[512,384]{1,0:T(8,128)(2,1)S(1)}, u32[]{:S(2)}, u32[]{:S(2)}) collective-permute-start(bf16[512,384]{1,0:T(8,128)(2,1)S(1)} %get-tuple-element.37.refs_0_), channel_id=1, source_target_pairs={{0,8},{8,0},{16,24},{24,16},{1,9},{9,1},{17,25},{25,17},{2,10},{10... | collective-permute-start | bytes 1179656 | tf_op jit(solution)/shard_map/ppermute | solution.py:24
  143.5 12.0 %collective-permute-start.19 = (bf16[512,384]{1,0:T(8,128)(2,1)S(1)}, bf16[512,384]{1,0:T(8,128)(2,1)S(1)}, u32[]{:S(2)}, u32[]{:S(2)}) collective-permute-start(bf16[512,384]{1,0:T(8,128)(2,1)S(1)} %get-tuple-element.38.refs_4_), channel_id=1, source_target_pairs={{0,16},{8,24},{16,0},{24,8},{1,17},{9,25},{17,1},{25,9},{2,18},{10... | collective-permute-start | bytes 1179656 | tf_op jit(solution)/shard_map/ppermute | solution.py:24
  144.6 19.3 %collective-permute-start.17 = (bf16[512,384]{1,0:T(8,128)(2,1)S(1)}, bf16[512,384]{1,0:T(8,128)(2,1)S(1)}, u32[]{:S(2)}, u32[]{:S(2)}) collective-permute-start(bf16[512,384]{1,0:T(8,128)(2,1)S(1)} %get-tuple-element.37.refs_0_), channel_id=1, source_target_pairs={{0,16},{8,24},{16,0},{24,8},{1,17},{9,25},{17,1},{25,9},{2,18},{10... | collective-permute-start | bytes 1179656 | tf_op jit(solution)/shard_map/ppermute | solution.py:24
  145.5 18.4 %collective-permute-start.20 = (bf16[512,384]{1,0:T(8,128)(2,1)S(1)}, bf16[512,384]{1,0:T(8,128)(2,1)S(1)}, u32[]{:S(2)}, u32[]{:S(2)}) collective-permute-start(bf16[512,384]{1,0:T(8,128)(2,1)S(1)} %get-tuple-element.38.refs_4_), channel_id=1, source_target_pairs={{0,8},{8,0},{16,24},{24,16},{1,9},{9,1},{17,25},{25,17},{2,10},{10... | collective-permute-start | bytes 1179656 | tf_op jit(solution)/shard_map/ppermute | solution.py:24
  154.8 16.8 %collective-permute-start.18 = (bf16[512,384]{1,0:T(8,128)(2,1)S(1)}, bf16[512,384]{1,0:T(8,128)(2,1)S(1)}, u32[]{:S(2)}, u32[]{:S(2)}) collective-permute-start(bf16[512,384]{1,0:T(8,128)(2,1)S(1)} %collective-permute-done.16.refs_1_), channel_id=1, source_target_pairs={{0,16},{8,24},{16,0},{24,8},{1,17},{9,25},{17,1},{25,9},{2,18},{10... | collective-permute-start | bytes 1179656 | tf_op jit(solution)/shard_map/ppermute | solution.py:24
  155.5 16.1 %collective-permute-start.21 = (bf16[512,384]{1,0:T(8,128)(2,1)S(1)}, bf16[512,384]{1,0:T(8,128)(2,1)S(1)}, u32[]{:S(2)}, u32[]{:S(2)}) collective-permute-start(bf16[512,384]{1,0:T(8,128)(2,1)S(1)} %collective-permute-done.19.refs_5_), channel_id=1, source_target_pairs={{0,8},{8,0},{16,24},{24,16},{1,9},{9,1},{17,25},{25,17},{2,10},{10... | collective-permute-start | bytes 1179656 | tf_op jit(solution)/shard_map/ppermute | solution.py:24
  174.7 5.1 %collective-permute-start.22 = (bf16[3,128,128]{2,1,0:T(8,128)(2,1)S(1)}, bf16[3,128,128]{2,1,0:T(8,128)(2,1)S(1)}, u32[]{:S(2)}, u32[]{:S(2)}) collective-permute-start(bf16[3,128,128]{2,1,0:T(8,128)(2,1)S(1)} %get-tuple-element.41), channel_id=1, source_target_pairs={{0,8},{8,0},{16,24},{24,16},{1,9},{9,1},{17,25},{25,17},{2,10},{10... | collective-permute-start | bytes 294920 | tf_op jit(solution)/shard_map/ppermute | solution.py:24
  176.2 6.4 %collective-permute-start.23 = (bf16[3,128,128]{2,1,0:T(8,128)(2,1)S(1)}, bf16[3,128,128]{2,1,0:T(8,128)(2,1)S(1)}, u32[]{:S(2)}, u32[]{:S(2)}) collective-permute-start(bf16[3,128,128]{2,1,0:T(8,128)(2,1)S(1)} %get-tuple-element.41), channel_id=1, source_target_pairs={{0,16},{8,24},{16,0},{24,8},{1,17},{9,25},{17,1},{25,9},{2,18},{10... | collective-permute-start | bytes 294920 | tf_op jit(solution)/shard_map/ppermute | solution.py:24
  176.7 5.8 %collective-permute-start.24 = (bf16[3,128,128]{2,1,0:T(8,128)(2,1)S(1)}, bf16[3,128,128]{2,1,0:T(8,128)(2,1)S(1)}, u32[]{:S(2)}, u32[]{:S(2)}) collective-permute-start(bf16[3,128,128]{2,1,0:T(8,128)(2,1)S(1)} %get-tuple-element.41), channel_id=1, source_target_pairs={{0,24},{8,16},{16,8},{24,0},{1,25},{9,17},{17,9},{25,1},{2,26},{10... | collective-permute-start | bytes 294920 | tf_op jit(solution)/shard_map/ppermute | solution.py:24
  185.1 16.9 %all-to-all-start = ((bf16[8,64,384]{2,1,0:T(8,128)(2,1)}), bf16[8,64,384]{2,1,0:T(8,128)(2,1)S(1)}, u32[]{:S(2)}, u32[]{:S(2)}) async-start(bf16[8,64,384]{2,1,0:T(8,128)(2,1)} %bitcast.4), calls=%async_computation | async-start | bytes 786432 | tf_op jit(solution)/shard_map/all_to_all | solution.py:301

commit v3 on v2

--- a/solution.py
+++ b/solution.py
@@ -10,7 +10,9 @@
 
 DK = 128
 CAP = 64
-LAST_HEADS = 3
+LAST_HEADS = 2
+PIECES = (True, True)
+EARLY = (True, False)
 LIMIT = 24 << 20
 VMEM = pl.BlockSpec(memory_space=pltpu.VMEM)
 SMEM = pl.BlockSpec(memory_space=pltpu.SMEM)
@@ -50,7 +52,8 @@
     slots = [(name * CAP + place).astype(jnp.float32) for name, place in zip(named, places)]
     level = levels[...].astype(jnp.float32)
     gates = level / (level[0:1, :] + level[1:2, :])
-    entries = jnp.concatenate(slots + [gates, jnp.zeros((4, count), jnp.float32)], axis=0)
+    turned = [c.astype(jnp.float32) for c in crossed]
+    entries = jnp.concatenate(slots + [gates] + turned + [jnp.zeros((2, count), jnp.float32)], axis=0)
     table[...] = entries.T
 
 
@@ -85,11 +88,22 @@
     return total
 
 
-def kv_kernel(here, x, *refs, masks):
+def early_kernel(here, x, *refs, masks):
     n = len(masks[0])
-    k_out, v_out, t_out = refs[2 * n :]
-    k_out[...] = project(x, here[0], refs[:n], masks[0]).astype(bf16)
-    v_out[...] = project(x, here[0], refs[n : 2 * n], masks[1]).astype(bf16)
+    k_out, v_out = refs[2 * n :]
+    k_out[...] = project(x, here[0], refs[:n], masks[0])
+    v_out[...] = project(x, here[0], refs[n : 2 * n], masks[1])
+
+
+def kv_kernel(here, x, *refs, masks, early):
+    n = len(masks[0])
+    partial = refs[2 * n : 2 * n + early]
+    k_out, v_out, t_out = refs[2 * n + early :]
+    for s, out in enumerate((k_out, v_out)):
+        total = project(x, here[0], refs[s * n : (s + 1) * n], masks[s])
+        if early:
+            total = total + partial[s][...]
+        out[...] = total.astype(bf16)
     for h in range(t_out.shape[0]):
         cols = slice(h * DK, (h + 1) * DK)
         t_out[h] = contract(k_out[:, cols], v_out[:, cols], 0, 0).astype(bf16)
@@ -115,9 +129,13 @@
         out[:, pl.ds(at, cols)] = contract(x[...], quarter[...], 1, 0).astype(bf16)
 
 
-def attend_kernel(here, q_all, k, v, *refs, first):
-    *states, out = refs
+def attend_kernel(here, q_all, k, v, *refs, first, others):
+    states, outs = refs[:others], refs[others:]
     length = k.shape[0]
+    if len(outs) > 1:
+        *outs, out = outs
+    else:
+        (out,), outs = outs, []
     step = length // 2
     row = lax.broadcasted_iota(jnp.int32, (step, step), 0)
     col = lax.broadcasted_iota(jnp.int32, (step, step), 1)
@@ -143,20 +161,22 @@
             reads = reads + contract(q, high, 1, 0) + contract(q, low, 1, 0)
             scale = lax.rsqrt(jnp.mean(reads * reads, axis=-1, keepdims=True) + 1e-06)
             out[rows, cols] = (reads * scale).astype(bf16)
-
-
-def combine_kernel(table, part, *refs):
-    *prior, out = refs
+    for k, piece in enumerate(outs):
+        piece[...] = out[pl.ds(pl.multiple_of((here[1] ^ k) * CAP, CAP), CAP), :]
+
+
+def combine_kernel(table, *refs, parts, at):
+    pieces, prior, out = refs[:parts], refs[parts:-1], refs[-1]
     count = table.shape[0]
-    at = 0
     for done in prior:
-        out[:, : done.shape[1]] = done[...]
-        at = done.shape[1]
+        out[:, :at] = done[...]
+    part = jnp.concatenate([p[...] for p in pieces], axis=0)
     index = lax.broadcasted_iota(jnp.int32, (count, part.shape[0]), 1).astype(jnp.float32)
+    column = 4 if parts > 1 else 0
     mixed = None
     for j in range(2):
-        pick = jnp.where(index == table[:, j : j + 1], 1.0, 0.0).astype(bf16)
-        term = table[:, 2 + j : 3 + j] * contract(pick, part[...], 1, 0)
+        pick = jnp.where(index == table[:, column + j : column + j + 1], 1.0, 0.0).astype(bf16)
+        term = table[:, 2 + j : 3 + j] * contract(pick, part, 1, 0)
         mixed = term if mixed is None else mixed + term
     out[:, at:] = mixed.astype(bf16)
 
@@ -270,26 +290,42 @@
     out = None
     for c, (first, heads) in enumerate(chunks):
         cols = heads * DK
+        k_pieces, v_pieces = weights[c]
+        near = groups // 2 + 1 if EARLY[c] else 0
+        partial = []
+        if near:
+            partial = call(
+                functools.partial(early_kernel, masks=[m[:near] for m in masks]),
+                [shape((length, cols), jnp.float32)] * 2,
+                [SMEM] + [VMEM] * (1 + 2 * near),
+                here,
+                arrived,
+                *k_pieces[:near],
+                *v_pieces[:near],
+                flops=3 * length * model * cols,
+            )
         keys, values, total = call(
-            functools.partial(kv_kernel, masks=masks),
+            functools.partial(kv_kernel, masks=[m[near:] for m in masks], early=len(partial)),
             [
                 shape((length, cols), bf16),
                 shape((length, cols), bf16),
                 shape((heads, DK, DK), bf16),
             ],
-            [SMEM, VMEM] + [VMEM] * (2 * groups),
+            [SMEM] + [VMEM] * (1 + 2 * (groups - near) + len(partial)),
             here,
             arrived,
-            *weights[c][0],
-            *weights[c][1],
+            *k_pieces[near:],
+            *v_pieces[near:],
+            *partial,
             flops=4 * length * model * cols,
         )
         states = []
         for m in range(1, groups):
             states.append(swap(total, "seq", m))
+        pieces = experts if PIECES[c] else 1
         normed = call(
-            functools.partial(attend_kernel, first=first),
-            shape((length, cols), bf16),
+            functools.partial(attend_kernel, first=first, others=len(states)),
+            [shape((length // pieces, cols), bf16)] * pieces,
             [SMEM] + [VMEM] * (3 + len(states)),
             here,
             queries,
@@ -297,18 +333,25 @@
             values,
             *states,
             flops=4 * length * length * cols,
+            scratch=[pltpu.VMEM((length, cols), bf16)] if pieces > 1 else [],
         )
-        back = lax.all_to_all(
-            normed.reshape(experts, CAP, cols), "mem", split_axis=0, concat_axis=0, tiled=True
-        )
-        back = back.reshape(length, cols)
+        if pieces > 1:
+            back = [normed[0]]
+            for k in range(1, experts):
+                back.append(swap(normed[k], "mem", k))
+        else:
+            back = [
+                lax.all_to_all(
+                    normed[0].reshape(experts, CAP, cols), "mem", split_axis=0, concat_axis=0, tiled=True
+                ).reshape(length, cols)
+            ]
         prior = [] if out is None else [out]
         out = call(
-            combine_kernel,
+            functools.partial(combine_kernel, parts=len(back), at=first * DK),
             shape((count, first * DK + cols), bf16),
-            [VMEM] * (2 + len(prior)),
+            [VMEM] * (1 + len(back) + len(prior)),
             table,
-            back,
+            *back,
             *prior,
             last=c + 1 == len(chunks),
         )

time: 204 us -> 184 us (0.902)
  waiting for transfers between devices: 118 us -> 97.2 us
  starting transfers between devices: 57.6 us -> 60.7 us
  Pallas kernels: 27.2 us -> 24.9 us
    ppermute x34 -> x48, starting transfers between devices: 38.8 us -> 60.7 us  [swap(): lax.ppermute(array, axis, [(i, i ^ mask) for i in range(lax.axis_size(axi...]
    all_to_all x2 -> x0, starting transfers between devices: 18.8 us -> none  [on_device(): lax.all_to_all(normed.reshape(experts, CAP, cols), 'mem', split_axis=0, c...]
    all_to_all x2 -> x0, waiting for transfers between devices: 11.9 us -> none  [on_device(): lax.all_to_all(normed.reshape(experts, CAP, cols), 'mem', split_axis=0, c...]
    ppermute x34 -> x48, waiting for transfers between devices: 106 us -> 97.2 us  [swap(): lax.ppermute(array, axis, [(i, i ^ mask) for i in range(lax.axis_size(axi...]
    pallas_call x13 -> x14, Pallas kernels: 27.2 us -> 24.9 us  [call(): pl.pallas_call(kernel, out_shape=outs if last else jax.tree.map(lambda s:...]
  transfers between devices with their start and end apart: 36 -> 48, of which waited for: 21 -> 16; matrix products, arithmetic and copies ran while one was open for 0% -> 0% of each run, Pallas kernels for 10% -> 12%
where the time goes in v3:
time: 184 us; the launch traced here: 183 us
  waiting for transfers between devices  97.2 us (53%)
  starting transfers between devices  60.7 us (33%)
  Pallas kernels  24.9 us (14%)
    ppermute x48, waiting for transfers between devices, swap(): lax.ppermute(array, axis, [(i, i ^ mask) for i in range(lax.axis_size(axi...  97.2 us
    ppermute x48, starting transfers between devices, swap(): lax.ppermute(array, axis, [(i, i ^ mask) for i in range(lax.axis_size(axi...  60.7 us
    pallas_call x14, Pallas kernels, call(): pl.pallas_call(kernel, out_shape=outs if last else jax.tree.map(lambda s:...  24.9 us
  transfers between devices with their start and end apart: 48, of which 16 were waited for; matrix products, arithmetic and copies ran while one was open for 0% of the time, Pallas kernels for 12%

profile of v3, /device:TPU:0, one launch (start us, length us, event | category | flops | bytes accessed | tf_op | source)
XLA Modules:
  0.0 183.1 jit_solution(8516263632303053810)
XLA Ops:
  0.1 1.5 shard_map.66
  1.6 3.1 %collective-permute-start.10 = (bf16[512,128]{1,0:T(8,128)(2,1)S(1)}, bf16[512,128]{1,0:T(8,128)(2,1)S(1)}, u32[]{:S(2)}, u32[]{:S(2)}) collective-permute-start(bf16[512,128]{1,0:T(8,128)(2,1)S(1)} %get-tuple-element.54.refs_4_), channel_id=1, source_target_pairs={{0,16},{8,24},{16,0},{24,8},{1,17},{9,25},{17,1},{25,9},{2,18},{10... | collective-permute-start | bytes 393224 | tf_op jit(solution)/shard_map/ppermute | solution.py:26
  4.7 2.3 %shard_map.64 = (f32[256,8]{1,0:T(8,128)S(1)}, bf16[64,2048]{1,0:T(8,128)(2,1)S(1)}, bf16[64,2048]{1,0:T(8,128)(2,1)S(1)}, bf16[64,2048]{1,0:T(8,128)(2,1)S(1)},...) custom-call(s32[2]{0:T(128)S(1)} %pad_add_fusion.here, ...), custom_call_target="tpu_custom_call" | custom-call | flops 536870912 | bytes 1048576 | tf_op jit(solution)/shard_map/pallas_call | solution.py:189
  7.0 1.6 collective-permute-start.7
  8.6 0.5 collective-permute-start.11
  9.1 1.6 collective-permute-start.1
  11.2 2.3 %collective-permute-done.7.refs_1_ = bf16[512,128]{1,0:T(8,128)(2,1)S(1)} collective-permute-done((bf16[512,128]{1,0:T(8,128)(2,1)S(1)}, bf16[512,128]{1,0:T(8,128)(2,1)S(1)}, u32[]{:S(2)}, u32[]{:S(2)}) %collective-permute-start.7) | collective-permute-done | bytes 131104 | tf_op jit(solution)/shard_map/ppermute | solution.py:26
  13.7 2.1 %collective-permute-done.11.refs_6_ = bf16[512,128]{1,0:T(8,128)(2,1)S(1)} collective-permute-done((bf16[512,128]{1,0:T(8,128)(2,1)S(1)}, bf16[512,128]{1,0:T(8,128)(2,1)S(1)}, u32[]{:S(2)}, u32[]{:S(2)}) %collective-permute-start.11) | collective-permute-done | bytes 131104 | tf_op jit(solution)/shard_map/ppermute | solution.py:26
  15.8 2.6 %collective-permute-start.3 = (bf16[64,2048]{1,0:T(8,128)(2,1)S(1)}, bf16[64,2048]{1,0:T(8,128)(2,1)S(1)}, u32[]{:S(2)}, u32[]{:S(2)}) collective-permute-start(bf16[64,2048]{1,0:T(8,128)(2,1)S(1)} %get-tuple-element.49), channel_id=1, source_target_pairs={{0,4},{1,5},{2,6},{3,7},{4,0},{5,1},{6,2},{7,3},{8,12},{9,13},{10,... | collective-permute-start | bytes 786440 | tf_op jit(solution)/shard_map/ppermute | solution.py:26
  18.4 2.8 %collective-permute-start.5 = (bf16[64,2048]{1,0:T(8,128)(2,1)S(1)}, bf16[64,2048]{1,0:T(8,128)(2,1)S(1)}, u32[]{:S(2)}, u32[]{:S(2)}) collective-permute-start(bf16[64,2048]{1,0:T(8,128)(2,1)S(1)} %get-tuple-element.51), channel_id=1, source_target_pairs={{0,6},{1,7},{2,4},{3,5},{4,2},{5,3},{6,0},{7,1},{8,14},{9,15},{10,... | collective-permute-start | bytes 786440 | tf_op jit(solution)/shard_map/ppermute | solution.py:26
  21.2 0.9 collective-permute-start.6
  22.1 6.1 %collective-permute-done.2.refs_3_ = bf16[64,2048]{1,0:T(8,128)(2,1)S(1)} collective-permute-done((bf16[64,2048]{1,0:T(8,128)(2,1)S(1)}, bf16[64,2048]{1,0:T(8,128)(2,1)S(1)}, u32[]{:S(2)}, u32[]{:S(2)}) %collective-permute-start.2) | collective-permute-done | bytes 262176 | tf_op jit(solution)/shard_map/ppermute | solution.py:26
  28.2 1.5 collective-permute-start.12
  29.7 18.6 %collective-permute-done.3.refs_4_ = bf16[64,2048]{1,0:T(8,128)(2,1)S(1)} collective-permute-done((bf16[64,2048]{1,0:T(8,128)(2,1)S(1)}, bf16[64,2048]{1,0:T(8,128)(2,1)S(1)}, u32[]{:S(2)}, u32[]{:S(2)}) %collective-permute-start.3) | collective-permute-done | bytes 262176 | tf_op jit(solution)/shard_map/ppermute | solution.py:26
  48.6 1.6 shard_map.69
  50.2 1.1 collective-permute-done.4.refs_5_
  51.2 1.5 collective-permute-start.16
  52.7 0.8 collective-permute-start.19
  53.5 1.2 collective-permute-start.17
  54.8 0.5 collective-permute-start.20
  55.3 0.7 shard_map.67.refs_0_
  56.0 8.6 %collective-permute-start.14 = (bf16[2048,256]{1,0:T(8,128)(2,1)S(1)}, bf16[2048,256]{1,0:T(8,128)(2,1)S(1)}, u32[]{:S(2)}, u32[]{:S(2)}) collective-permute-start(bf16[2048,256]{1,0:T(8,128)(2,1)S(1)} %shard_map.67.refs_0_), channel_id=1, source_target_pairs={{0,2},{1,3},{2,0},{3,1},{4,6},{5,7},{6,4},{7,5},{8,10},{9,11},{10,... | collective-permute-start | bytes 3145736 | tf_op jit(solution)/shard_map/ppermute | solution.py:26
  64.7 1.9 %shard_map.72 = (bf16[512,768]{1,0:T(8,128)(2,1)S(1)}, bf16[512,768]{1,0:T(8,128)(2,1)S(1)}) custom-call(s32[2]{0:T(128)S(1)} %pad_add_fusion.here, bf16[512,1024]{1,0:T(8,128)(2,1)} %refs_0_.5, bf16[1,512,1024]{2,1,0:T(8,128)(2,1)} %refs_1_.5, bf16[1,512,1024]{2,1,0:T(8,128)(2,1)} %refs_2_.5), custom_call_target="tpu_custom_call" | custom-call | flops 1 | bytes 1048576 | tf_op jit(solution)/shard_map/pallas_call | solution.py:189
  66.6 1.5 collective-permute-start.32
  68.6 1.5 collective-permute-start.18
  70.1 0.5 collective-permute-start.36
  70.6 23.5 %collective-permute-done.18.refs_3_ = bf16[512,256]{1,0:T(8,128)(2,1)S(1)} collective-permute-done((bf16[512,256]{1,0:T(8,128)(2,1)S(1)}, bf16[512,256]{1,0:T(8,128)(2,1)S(1)}, u32[]{:S(2)}, u32[]{:S(2)}) %collective-permute-start.18) | collective-permute-done | bytes 262176 | tf_op jit(solution)/shard_map/ppermute | solution.py:26
  94.1 0.6 collective-permute-start.21
  94.7 7.2 %collective-permute-done.21.refs_7_ = bf16[512,256]{1,0:T(8,128)(2,1)S(1)} collective-permute-done((bf16[512,256]{1,0:T(8,128)(2,1)S(1)}, bf16[512,256]{1,0:T(8,128)(2,1)S(1)}, u32[]{:S(2)}, u32[]{:S(2)}) %collective-permute-start.21) | collective-permute-done | bytes 262176 | tf_op jit(solution)/shard_map/ppermute | solution.py:26
  101.9 0.7 collective-permute-start.37
  102.6 0.6 collective-permute-start.33
  103.2 1.2 collective-permute-start.35
  104.5 6.5 %collective-permute-done.36.refs_2_ = bf16[512,768]{1,0:T(8,128)(2,1)S(1)} collective-permute-done((bf16[512,768]{1,0:T(8,128)(2,1)S(1)}, bf16[512,768]{1,0:T(8,128)(2,1)S(1)}, u32[]{:S(2)}, u32[]{:S(2)}) %collective-permute-start.36) | collective-permute-done | bytes 786464 | tf_op jit(solution)/shard_map/ppermute | solution.py:26
  111.5 0.7 shard_map.65.x
  112.2 2.1 %shard_map.70 = (bf16[512,256]{1,0:T(8,128)(2,1)S(1)}, bf16[512,256]{1,0:T(8,128)(2,1)S(1)}, bf16[2,128,128]{2,1,0:T(8,128)(2,1)S(1)}) custom-call(s32[2]{0:T(128)S(1)} %pad_add_fusion.here, bf16[512,2048]{1,0:T(8,128)(2,1)S(1)} %shard_map.65.x, bf16[512,256]{1,0:T(8,128)(2,1)S(1)} %get-tuple-element.55.refs_0_, ...), custom_call_target="tpu_custom_call" | custom-call | flops 1073741824 | bytes 1048576 | tf_op jit(solution)/shard_map/pallas_call | solution.py:189
  114.3 8.1 %collective-permute-done.37.refs_5_ = bf16[512,768]{1,0:T(8,128)(2,1)S(1)} collective-permute-done((bf16[512,768]{1,0:T(8,128)(2,1)S(1)}, bf16[512,768]{1,0:T(8,128)(2,1)S(1)}, u32[]{:S(2)}, u32[]{:S(2)}) %collective-permute-start.37) | collective-permute-done | bytes 786464 | tf_op jit(solution)/shard_map/ppermute | solution.py:26
  122.3 0.7 collective-permute-start.22
  123.1 3.2 %shard_map.73 = (f32[512,768]{1,0:T(8,128)S(1)}, f32[512,768]{1,0:T(8,128)S(1)}) custom-call(s32[2]{0:T(128)S(1)} %pad_add_fusion.here, bf16[512,2048]{1,0:T(8,128)(2,1)S(1)} %shard_map.65.x, bf16[512,768]{1,0:T(8,128)(2,1)S(1)} %get-tuple-element.68.refs_0_, bf16[512,768]{1,0:T(8,128)(2,1)S(1)} %collective-permute-done.32.refs_1_, ...), custom_call_target="tpu_custom_call" | custom-call | flops 2415919104 | bytes 1048576 | tf_op jit(solution)/shard_map/pallas_call | solution.py:189
  126.3 0.6 collective-permute-start.23
  126.9 9.0 %collective-permute-done.35.refs_1_ = bf16[512,768]{1,0:T(8,128)(2,1)S(1)} collective-permute-done((bf16[512,768]{1,0:T(8,128)(2,1)S(1)}, bf16[512,768]{1,0:T(8,128)(2,1)S(1)}, u32[]{:S(2)}, u32[]{:S(2)}) %collective-permute-start.35) | collective-permute-done | bytes 786464 | tf_op jit(solution)/shard_map/ppermute | solution.py:26
  135.9 1.9 %shard_map.74 = (bf16[512,768]{1,0:T(8,128)(2,1)S(1)}, bf16[512,768]{1,0:T(8,128)(2,1)S(1)}, bf16[6,128,128]{2,1,0:T(8,128)(2,1)S(1)}) custom-call(s32[2]{0:T(128)S(1)} %pad_add_fusion.here, bf16[512,2048]{1,0:T(8,128)(2,1)S(1)} %shard_map.65.x, bf16[512,768]{1,0:T(8,128)(2,1)S(1)} %collective-permute-done.33.refs_0_, ...), custom_call_target="tpu_custom_call" | custom-call | flops 3221225472 | bytes 1048576 | tf_op jit(solution)/shard_map/pallas_call | solution.py:189
  137.8 0.8 collective-permute-start.38
  138.6 0.6 collective-permute-start.39
  139.2 2.2 %collective-permute-start.40 = (bf16[6,128,128]{2,1,0:T(8,128)(2,1)S(1)}, bf16[6,128,128]{2,1,0:T(8,128)(2,1)S(1)}, u32[]{:S(2)}, u32[]{:S(2)}) collective-permute-start(bf16[6,128,128]{2,1,0:T(8,128)(2,1)S(1)} %get-tuple-element.74), channel_id=1, source_target_pairs={{0,24},{8,16},{16,8},{24,0},{1,25},{9,17},{17,9},{25,1},{2,26},{10... | collective-permute-start | bytes 589832 | tf_op jit(solution)/shard_map/ppermute | solution.py:26
  141.4 3.0 %shard_map.68.q_all = bf16[512,1024]{1,0:T(8,128)(2,1)S(1)} custom-call(s32[2]{0:T(128)S(1)} %pad_add_fusion.here, bf16[512,2048]{1,0:T(8,128)(2,1)S(1)} %shard_map.65.x, bf16[2048,256]{1,0:T(8,128)(2,1)S(1)} %shard_map.67.refs_0_, bf16[2048,256]{1,0:T(8,128)(2,1)S(1)} %collective-permute-done.13.refs_1_, ...), custom_call_target="tpu_custom_call" | custom-call | flops 2147483648 | bytes 1048576 | tf_op jit(solution)/shard_map/pallas_call | solution.py:189
  144.3 0.8 collective-permute-start.24
  145.1 1.2 collective-permute-done.39.refs_1_
  146.4 2.7 %shard_map.75 = (bf16[64,768]{1,0:T(8,128)(2,1)S(1)}, bf16[64,768]{1,0:T(8,128)(2,1)S(1)}, bf16[64,768]{1,0:T(8,128)(2,1)S(1)}, bf16[64,768]{1,0:T(8,128)(2,1)S(...) custom-call(s32[2]{0:T(128)S(1)} %pad_add_fusion.here, ...), custom_call_target="tpu_custom_call" | custom-call | flops 805306368 | bytes 1048576 | tf_op jit(solution)/shard_map/pallas_call | solution.py:189
  149.2 4.3 %collective-permute-start.42 = (bf16[64,768]{1,0:T(8,128)(2,1)S(1)}, bf16[64,768]{1,0:T(8,128)(2,1)S(1)}, u32[]{:S(2)}, u32[]{:S(2)}) collective-permute-start(bf16[64,768]{1,0:T(8,128)(2,1)S(1)} %get-tuple-element.77), channel_id=1, source_target_pairs={{0,2},{1,3},{2,0},{3,1},{4,6},{5,7},{6,4},{7,5},{8,10},{9,11},{10,... | collective-permute-start | bytes 294920 | tf_op jit(solution)/shard_map/ppermute | solution.py:26
  153.5 1.6 shard_map.71
  155.4 1.6 collective-permute-start.43
  157.0 1.5 collective-permute-start.44
  158.5 1.0 collective-permute-done.26.refs_2_
  159.6 2.7 %collective-permute-start.46 = (bf16[64,768]{1,0:T(8,128)(2,1)S(1)}, bf16[64,768]{1,0:T(8,128)(2,1)S(1)}, u32[]{:S(2)}, u32[]{:S(2)}) collective-permute-start(bf16[64,768]{1,0:T(8,128)(2,1)S(1)} %get-tuple-element.81), channel_id=1, source_target_pairs={{0,6},{1,7},{2,4},{3,5},{4,2},{5,3},{6,0},{7,1},{8,14},{9,15},{10,... | collective-permute-start | bytes 294920 | tf_op jit(solution)/shard_map/ppermute | solution.py:26
  162.3 1.5 collective-permute-start.47
  163.8 2.6 %collective-permute-start.28 = (bf16[64,256]{1,0:T(8,128)(2,1)S(1)}, bf16[64,256]{1,0:T(8,128)(2,1)S(1)}, u32[]{:S(2)}, u32[]{:S(2)}) collective-permute-start(bf16[64,256]{1,0:T(8,128)(2,1)S(1)} %get-tuple-element.64), channel_id=1, source_target_pairs={{0,4},{1,5},{2,6},{3,7},{4,0},{5,1},{6,2},{7,3},{8,12},{9,13},{10,... | collective-permute-start | bytes 98312 | tf_op jit(solution)/shard_map/ppermute | solution.py:26
  166.4 7.2 %collective-permute-done.45.refs_5_ = bf16[64,768]{1,0:T(8,128)(2,1)S(1)} collective-permute-done((bf16[64,768]{1,0:T(8,128)(2,1)S(1)}, bf16[64,768]{1,0:T(8,128)(2,1)S(1)}, u32[]{:S(2)}, u32[]{:S(2)}) %collective-permute-start.45) | collective-permute-done | bytes 98336 | tf_op jit(solution)/shard_map/ppermute | solution.py:26
  173.6 3.1 %collective-permute-start.30 = (bf16[64,256]{1,0:T(8,128)(2,1)S(1)}, bf16[64,256]{1,0:T(8,128)(2,1)S(1)}, u32[]{:S(2)}, u32[]{:S(2)}) collective-permute-start(bf16[64,256]{1,0:T(8,128)(2,1)S(1)} %get-tuple-element.66), channel_id=1, source_target_pairs={{0,6},{1,7},{2,4},{3,5},{4,2},{5,3},{6,0},{7,1},{8,14},{9,15},{10,... | collective-permute-start | bytes 98312 | tf_op jit(solution)/shard_map/ppermute | solution.py:26
  176.7 1.2 collective-permute-start.31
  178.0 0.6 shard_map.76.refs_8_
  178.6 2.0 %collective-permute-done.28.refs_4_ = bf16[64,256]{1,0:T(8,128)(2,1)S(1)} collective-permute-done((bf16[64,256]{1,0:T(8,128)(2,1)S(1)}, bf16[64,256]{1,0:T(8,128)(2,1)S(1)}, u32[]{:S(2)}, u32[]{:S(2)}) %collective-permute-start.28) | collective-permute-done | bytes 32800 | tf_op jit(solution)/shard_map/ppermute | solution.py:26
  180.6 0.7 collective-permute-done.29.refs_5_
  181.3 0.7 collective-permute-done.31.refs_7_
  182.0 1.2 shard_map.77
  (53 shorter events, 2.8 us)
Async XLA Ops:
  0.1 4.6 %copy-start = (bf16[256,2048]{1,0:T(8,128)(2,1)S(1)}, bf16[256,2048]{1,0:T(8,128)(2,1)}, u32[]{:S(2)}) copy-start(bf16[256,2048]{1,0:T(8,128)(2,1)} %hidden.1) | copy-start | bytes 3145732
  0.1 4.6 %copy-start.1 = (s32[256,2]{0,1:T(2,128)S(1)}, s32[256,2]{0,1:T(2,128)}, u32[]{:S(2)}) copy-start(s32[256,2]{0,1:T(2,128)} %param.7) | copy-start | bytes 6148
  0.1 4.6 %copy-start.2 = (s32[256,2]{0,1:T(2,128)S(1)}, s32[256,2]{0,1:T(2,128)}, u32[]{:S(2)}) copy-start(s32[256,2]{0,1:T(2,128)} %param.8) | copy-start | bytes 6148
  1.6 9.1 %collective-permute-start.10 = (bf16[512,128]{1,0:T(8,128)(2,1)S(1)}, bf16[512,128]{1,0:T(8,128)(2,1)S(1)}, u32[]{:S(2)}, u32[]{:S(2)}) collective-permute-start(bf16[512,128]{1,0:T(8,128)(2,1)S(1)} %get-tuple-element.54.refs_4_), channel_id=1, source_target_pairs={{0,16},{8,24},{16,0},{24,8},{1,17},{9,25},{17,1},{25,9},{2,18},{10... | collective-permute-start | bytes 393224 | tf_op jit(solution)/shard_map/ppermute | solution.py:26
  7.0 11.4 %collective-permute-start = (bf16[64,2048]{1,0:T(8,128)(2,1)S(1)}, bf16[64,2048]{1,0:T(8,128)(2,1)S(1)}, u32[]{:S(2)}, u32[]{:S(2)}) collective-permute-start(bf16[64,2048]{1,0:T(8,128)(2,1)S(1)} %get-tuple-element.46), channel_id=1, source_target_pairs={{0,1},{1,0},{2,3},{3,2},{4,5},{5,4},{6,7},{7,6},{8,9},{9,8},{10,11... | collective-permute-start | bytes 786440 | tf_op jit(solution)/shard_map/ppermute | solution.py:26
  7.0 6.4 %collective-permute-start.7 = (bf16[512,128]{1,0:T(8,128)(2,1)S(1)}, bf16[512,128]{1,0:T(8,128)(2,1)S(1)}, u32[]{:S(2)}, u32[]{:S(2)}) collective-permute-start(bf16[512,128]{1,0:T(8,128)(2,1)S(1)} %get-tuple-element.53.refs_0_), channel_id=1, source_target_pairs={{0,8},{8,0},{16,24},{24,16},{1,9},{9,1},{17,25},{25,17},{2,10},{10... | collective-permute-start | bytes 393224 | tf_op jit(solution)/shard_map/ppermute | solution.py:26
  8.6 7.1 %collective-permute-start.11 = (bf16[512,128]{1,0:T(8,128)(2,1)S(1)}, bf16[512,128]{1,0:T(8,128)(2,1)S(1)}, u32[]{:S(2)}, u32[]{:S(2)}) collective-permute-start(bf16[512,128]{1,0:T(8,128)(2,1)S(1)} %get-tuple-element.54.refs_4_), channel_id=1, source_target_pairs={{0,8},{8,0},{16,24},{24,16},{1,9},{9,1},{17,25},{25,17},{2,10},{10... | collective-permute-start | bytes 393224 | tf_op jit(solution)/shard_map/ppermute | solution.py:26
  9.1 12.1 %collective-permute-start.1 = (bf16[64,2048]{1,0:T(8,128)(2,1)S(1)}, bf16[64,2048]{1,0:T(8,128)(2,1)S(1)}, u32[]{:S(2)}, u32[]{:S(2)}) collective-permute-start(bf16[64,2048]{1,0:T(8,128)(2,1)S(1)} %get-tuple-element.47), channel_id=1, source_target_pairs={{0,2},{1,3},{2,0},{3,1},{4,6},{5,7},{6,4},{7,5},{8,10},{9,11},{10,... | collective-permute-start | bytes 786440 | tf_op jit(solution)/shard_map/ppermute | solution.py:26
  10.7 7.6 %collective-permute-start.8 = (bf16[512,128]{1,0:T(8,128)(2,1)S(1)}, bf16[512,128]{1,0:T(8,128)(2,1)S(1)}, u32[]{:S(2)}, u32[]{:S(2)}) collective-permute-start(bf16[512,128]{1,0:T(8,128)(2,1)S(1)} %get-tuple-element.53.refs_0_), channel_id=1, source_target_pairs={{0,16},{8,24},{16,0},{24,8},{1,17},{9,25},{17,1},{25,9},{2,18},{10... | collective-permute-start | bytes 393224 | tf_op jit(solution)/shard_map/ppermute | solution.py:26
  13.5 14.7 %collective-permute-start.2 = (bf16[64,2048]{1,0:T(8,128)(2,1)S(1)}, bf16[64,2048]{1,0:T(8,128)(2,1)S(1)}, u32[]{:S(2)}, u32[]{:S(2)}) collective-permute-start(bf16[64,2048]{1,0:T(8,128)(2,1)S(1)} %get-tuple-element.48), channel_id=1, source_target_pairs={{0,3},{1,2},{2,1},{3,0},{4,7},{5,6},{6,5},{7,4},{8,11},{9,10},{10,... | collective-permute-start | bytes 786440 | tf_op jit(solution)/shard_map/ppermute | solution.py:26
  15.8 32.5 %collective-permute-start.3 = (bf16[64,2048]{1,0:T(8,128)(2,1)S(1)}, bf16[64,2048]{1,0:T(8,128)(2,1)S(1)}, u32[]{:S(2)}, u32[]{:S(2)}) collective-permute-start(bf16[64,2048]{1,0:T(8,128)(2,1)S(1)} %get-tuple-element.49), channel_id=1, source_target_pairs={{0,4},{1,5},{2,6},{3,7},{4,0},{5,1},{6,2},{7,3},{8,12},{9,13},{10,... | collective-permute-start | bytes 786440 | tf_op jit(solution)/shard_map/ppermute | solution.py:26
  18.4 32.9 %collective-permute-start.4 = (bf16[64,2048]{1,0:T(8,128)(2,1)S(1)}, bf16[64,2048]{1,0:T(8,128)(2,1)S(1)}, u32[]{:S(2)}, u32[]{:S(2)}) collective-permute-start(bf16[64,2048]{1,0:T(8,128)(2,1)S(1)} %get-tuple-element.50), channel_id=1, source_target_pairs={{0,5},{1,4},{2,7},{3,6},{4,1},{5,0},{6,3},{7,2},{8,13},{9,12},{10,... | collective-permute-start | bytes 786440 | tf_op jit(solution)/shard_map/ppermute | solution.py:26
  18.4 34.4 %collective-permute-start.5 = (bf16[64,2048]{1,0:T(8,128)(2,1)S(1)}, bf16[64,2048]{1,0:T(8,128)(2,1)S(1)}, u32[]{:S(2)}, u32[]{:S(2)}) collective-permute-start(bf16[64,2048]{1,0:T(8,128)(2,1)S(1)} %get-tuple-element.51), channel_id=1, source_target_pairs={{0,6},{1,7},{2,4},{3,5},{4,2},{5,3},{6,0},{7,1},{8,14},{9,15},{10,... | collective-permute-start | bytes 786440 | tf_op jit(solution)/shard_map/ppermute | solution.py:26
  21.2 34.8 %collective-permute-start.6 = (bf16[64,2048]{1,0:T(8,128)(2,1)S(1)}, bf16[64,2048]{1,0:T(8,128)(2,1)S(1)}, u32[]{:S(2)}, u32[]{:S(2)}) collective-permute-start(bf16[64,2048]{1,0:T(8,128)(2,1)S(1)} %get-tuple-element.52), channel_id=1, source_target_pairs={{0,7},{1,6},{2,5},{3,4},{4,3},{5,2},{6,1},{7,0},{8,15},{9,14},{10,... | collective-permute-start | bytes 786440 | tf_op jit(solution)/shard_map/ppermute | solution.py:26
  28.2 25.3 %collective-permute-start.12 = (bf16[512,128]{1,0:T(8,128)(2,1)S(1)}, bf16[512,128]{1,0:T(8,128)(2,1)S(1)}, u32[]{:S(2)}, u32[]{:S(2)}) collective-permute-start(bf16[512,128]{1,0:T(8,128)(2,1)S(1)} %collective-permute-done.10.refs_5_), channel_id=1, source_target_pairs={{0,8},{8,0},{16,24},{24,16},{1,9},{9,1},{17,25},{25,17},{2,10},{10... | collective-permute-start | bytes 393224 | tf_op jit(solution)/shard_map/ppermute | solution.py:26
  48.3 6.4 %collective-permute-start.9 = (bf16[512,128]{1,0:T(8,128)(2,1)S(1)}, bf16[512,128]{1,0:T(8,128)(2,1)S(1)}, u32[]{:S(2)}, u32[]{:S(2)}) collective-permute-start(bf16[512,128]{1,0:T(8,128)(2,1)S(1)} %collective-permute-done.7.refs_1_), channel_id=1, source_target_pairs={{0,16},{8,24},{16,0},{24,8},{1,17},{9,25},{17,1},{25,9},{2,18},{10... | collective-permute-start | bytes 393224 | tf_op jit(solution)/shard_map/ppermute | solution.py:26
  51.2 15.4 %collective-permute-start.16 = (bf16[512,256]{1,0:T(8,128)(2,1)S(1)}, bf16[512,256]{1,0:T(8,128)(2,1)S(1)}, u32[]{:S(2)}, u32[]{:S(2)}) collective-permute-start(bf16[512,256]{1,0:T(8,128)(2,1)S(1)} %get-tuple-element.55.refs_0_), channel_id=1, source_target_pairs={{0,8},{8,0},{16,24},{24,16},{1,9},{9,1},{17,25},{25,17},{2,10},{10... | collective-permute-start | bytes 786440 | tf_op jit(solution)/shard_map/ppermute | solution.py:26
  52.7 15.4 %collective-permute-start.19 = (bf16[512,256]{1,0:T(8,128)(2,1)S(1)}, bf16[512,256]{1,0:T(8,128)(2,1)S(1)}, u32[]{:S(2)}, u32[]{:S(2)}) collective-permute-start(bf16[512,256]{1,0:T(8,128)(2,1)S(1)} %get-tuple-element.56.refs_4_), channel_id=1, source_target_pairs={{0,16},{8,24},{16,0},{24,8},{1,17},{9,25},{17,1},{25,9},{2,18},{10... | collective-permute-start | bytes 786440 | tf_op jit(solution)/shard_map/ppermute | solution.py:26
  53.5 15.1 %collective-permute-start.17 = (bf16[512,256]{1,0:T(8,128)(2,1)S(1)}, bf16[512,256]{1,0:T(8,128)(2,1)S(1)}, u32[]{:S(2)}, u32[]{:S(2)}) collective-permute-start(bf16[512,256]{1,0:T(8,128)(2,1)S(1)} %get-tuple-element.55.refs_0_), channel_id=1, source_target_pairs={{0,16},{8,24},{16,0},{24,8},{1,17},{9,25},{17,1},{25,9},{2,18},{10... | collective-permute-start | bytes 786440 | tf_op jit(solution)/shard_map/ppermute | solution.py:26
  54.8 15.4 %collective-permute-start.20 = (bf16[512,256]{1,0:T(8,128)(2,1)S(1)}, bf16[512,256]{1,0:T(8,128)(2,1)S(1)}, u32[]{:S(2)}, u32[]{:S(2)}) collective-permute-start(bf16[512,256]{1,0:T(8,128)(2,1)S(1)} %get-tuple-element.56.refs_4_), channel_id=1, source_target_pairs={{0,8},{8,0},{16,24},{24,16},{1,9},{9,1},{17,25},{25,17},{2,10},{10... | collective-permute-start | bytes 786440 | tf_op jit(solution)/shard_map/ppermute | solution.py:26
  56.0 55.0 %collective-permute-start.14 = (bf16[2048,256]{1,0:T(8,128)(2,1)S(1)}, bf16[2048,256]{1,0:T(8,128)(2,1)S(1)}, u32[]{:S(2)}, u32[]{:S(2)}) collective-permute-start(bf16[2048,256]{1,0:T(8,128)(2,1)S(1)} %shard_map.67.refs_0_), channel_id=1, source_target_pairs={{0,2},{1,3},{2,0},{3,1},{4,6},{5,7},{6,4},{7,5},{8,10},{9,11},{10,... | collective-permute-start | bytes 3145736 | tf_op jit(solution)/shard_map/ppermute | solution.py:26
  66.6 36.0 %collective-permute-start.32 = (bf16[512,768]{1,0:T(8,128)(2,1)S(1)}, bf16[512,768]{1,0:T(8,128)(2,1)S(1)}, u32[]{:S(2)}, u32[]{:S(2)}) collective-permute-start(bf16[512,768]{1,0:T(8,128)(2,1)S(1)} %get-tuple-element.68.refs_0_), channel_id=1, source_target_pairs={{0,8},{8,0},{16,24},{24,16},{1,9},{9,1},{17,25},{25,17},{2,10},{10... | collective-permute-start | bytes 2359304 | tf_op jit(solution)/shard_map/ppermute | solution.py:26
  68.1 35.1 %collective-permute-start.34 = (bf16[512,768]{1,0:T(8,128)(2,1)S(1)}, bf16[512,768]{1,0:T(8,128)(2,1)S(1)}, u32[]{:S(2)}, u32[]{:S(2)}) collective-permute-start(bf16[512,768]{1,0:T(8,128)(2,1)S(1)} %get-tuple-element.69.refs_3_), channel_id=1, source_target_pairs={{0,16},{8,24},{16,0},{24,8},{1,17},{9,25},{17,1},{25,9},{2,18},{10... | collective-permute-start | bytes 2359304 | tf_op jit(solution)/shard_map/ppermute | solution.py:26
  68.6 25.5 %collective-permute-start.18 = (bf16[512,256]{1,0:T(8,128)(2,1)S(1)}, bf16[512,256]{1,0:T(8,128)(2,1)S(1)}, u32[]{:S(2)}, u32[]{:S(2)}) collective-permute-start(bf16[512,256]{1,0:T(8,128)(2,1)S(1)} %collective-permute-done.16.refs_1_), channel_id=1, source_target_pairs={{0,16},{8,24},{16,0},{24,8},{1,17},{9,25},{17,1},{25,9},{2,18},{10... | collective-permute-start | bytes 786440 | tf_op jit(solution)/shard_map/ppermute | solution.py:26
  70.1 40.8 %collective-permute-start.36 = (bf16[512,768]{1,0:T(8,128)(2,1)S(1)}, bf16[512,768]{1,0:T(8,128)(2,1)S(1)}, u32[]{:S(2)}, u32[]{:S(2)}) collective-permute-start(bf16[512,768]{1,0:T(8,128)(2,1)S(1)} %get-tuple-element.68.refs_0_), channel_id=1, source_target_pairs={{0,16},{8,24},{16,0},{24,8},{1,17},{9,25},{17,1},{25,9},{2,18},{10... | collective-permute-start | bytes 2359304 | tf_op jit(solution)/shard_map/ppermute | solution.py:26
  94.1 7.8 %collective-permute-start.21 = (bf16[512,256]{1,0:T(8,128)(2,1)S(1)}, bf16[512,256]{1,0:T(8,128)(2,1)S(1)}, u32[]{:S(2)}, u32[]{:S(2)}) collective-permute-start(bf16[512,256]{1,0:T(8,128)(2,1)S(1)} %collective-permute-done.19.refs_5_), channel_id=1, source_target_pairs={{0,8},{8,0},{16,24},{24,16},{1,9},{9,1},{17,25},{25,17},{2,10},{10... | collective-permute-start | bytes 786440 | tf_op jit(solution)/shard_map/ppermute | solution.py:26
  101.9 20.4 %collective-permute-start.37 = (bf16[512,768]{1,0:T(8,128)(2,1)S(1)}, bf16[512,768]{1,0:T(8,128)(2,1)S(1)}, u32[]{:S(2)}, u32[]{:S(2)}) collective-permute-start(bf16[512,768]{1,0:T(8,128)(2,1)S(1)} %get-tuple-element.69.refs_3_), channel_id=1, source_target_pairs={{0,8},{8,0},{16,24},{24,16},{1,9},{9,1},{17,25},{25,17},{2,10},{10... | collective-permute-start | bytes 2359304 | tf_op jit(solution)/shard_map/ppermute | solution.py:26
  102.6 23.6 %collective-permute-start.33 = (bf16[512,768]{1,0:T(8,128)(2,1)S(1)}, bf16[512,768]{1,0:T(8,128)(2,1)S(1)}, u32[]{:S(2)}, u32[]{:S(2)}) collective-permute-start(bf16[512,768]{1,0:T(8,128)(2,1)S(1)} %collective-permute-done.32.refs_1_), channel_id=1, source_target_pairs={{0,16},{8,24},{16,0},{24,8},{1,17},{9,25},{17,1},{25,9},{2,18},{10... | collective-permute-start | bytes 2359304 | tf_op jit(solution)/shard_map/ppermute | solution.py:26
  103.2 32.7 %collective-permute-start.35 = (bf16[512,768]{1,0:T(8,128)(2,1)S(1)}, bf16[512,768]{1,0:T(8,128)(2,1)S(1)}, u32[]{:S(2)}, u32[]{:S(2)}) collective-permute-start(bf16[512,768]{1,0:T(8,128)(2,1)S(1)} %collective-permute-done.34.refs_4_), channel_id=1, source_target_pairs={{0,8},{8,0},{16,24},{24,16},{1,9},{9,1},{17,25},{25,17},{2,10},{10... | collective-permute-start | bytes 2359304 | tf_op jit(solution)/shard_map/ppermute | solution.py:26
  111.0 27.6 %collective-permute-start.13 = (bf16[2048,256]{1,0:T(8,128)(2,1)S(1)}, bf16[2048,256]{1,0:T(8,128)(2,1)S(1)}, u32[]{:S(2)}, u32[]{:S(2)}) collective-permute-start(bf16[2048,256]{1,0:T(8,128)(2,1)S(1)} %shard_map.67.refs_0_), channel_id=1, source_target_pairs={{0,1},{1,0},{2,3},{3,2},{4,5},{5,4},{6,7},{7,6},{8,9},{9,8},{10,11... | collective-permute-start | bytes 3145736 | tf_op jit(solution)/shard_map/ppermute | solution.py:26
  111.0 28.2 %collective-permute-start.15 = (bf16[2048,256]{1,0:T(8,128)(2,1)S(1)}, bf16[2048,256]{1,0:T(8,128)(2,1)S(1)}, u32[]{:S(2)}, u32[]{:S(2)}) collective-permute-start(bf16[2048,256]{1,0:T(8,128)(2,1)S(1)} %collective-permute-done.14.refs_2_), channel_id=1, source_target_pairs={{0,1},{1,0},{2,3},{3,2},{4,5},{5,4},{6,7},{7,6},{8,9},{9,8},{10,11... | collective-permute-start | bytes 3145736 | tf_op jit(solution)/shard_map/ppermute | solution.py:26
  122.3 31.2 %collective-permute-start.22 = (bf16[2,128,128]{2,1,0:T(8,128)(2,1)S(1)}, bf16[2,128,128]{2,1,0:T(8,128)(2,1)S(1)}, u32[]{:S(2)}, u32[]{:S(2)}) collective-permute-start(bf16[2,128,128]{2,1,0:T(8,128)(2,1)S(1)} %get-tuple-element.59), channel_id=1, source_target_pairs={{0,8},{8,0},{16,24},{24,16},{1,9},{9,1},{17,25},{25,17},{2,10},{10... | collective-permute-start | bytes 196616 | tf_op jit(solution)/shard_map/ppermute | solution.py:26
  126.3 27.2 %collective-permute-start.23 = (bf16[2,128,128]{2,1,0:T(8,128)(2,1)S(1)}, bf16[2,128,128]{2,1,0:T(8,128)(2,1)S(1)}, u32[]{:S(2)}, u32[]{:S(2)}) collective-permute-start(bf16[2,128,128]{2,1,0:T(8,128)(2,1)S(1)} %get-tuple-element.59), channel_id=1, source_target_pairs={{0,16},{8,24},{16,0},{24,8},{1,17},{9,25},{17,1},{25,9},{2,18},{10... | collective-permute-start | bytes 196616 | tf_op jit(solution)/shard_map/ppermute | solution.py:26
  137.8 6.5 %collective-permute-start.38 = (bf16[6,128,128]{2,1,0:T(8,128)(2,1)S(1)}, bf16[6,128,128]{2,1,0:T(8,128)(2,1)S(1)}, u32[]{:S(2)}, u32[]{:S(2)}) collective-permute-start(bf16[6,128,128]{2,1,0:T(8,128)(2,1)S(1)} %get-tuple-element.74), channel_id=1, source_target_pairs={{0,8},{8,0},{16,24},{24,16},{1,9},{9,1},{17,25},{25,17},{2,10},{10... | collective-permute-start | bytes 589832 | tf_op jit(solution)/shard_map/ppermute | solution.py:26
  138.6 7.8 %collective-permute-start.39 = (bf16[6,128,128]{2,1,0:T(8,128)(2,1)S(1)}, bf16[6,128,128]{2,1,0:T(8,128)(2,1)S(1)}, u32[]{:S(2)}, u32[]{:S(2)}) collective-permute-start(bf16[6,128,128]{2,1,0:T(8,128)(2,1)S(1)} %get-tuple-element.74), channel_id=1, source_target_pairs={{0,16},{8,24},{16,0},{24,8},{1,17},{9,25},{17,1},{25,9},{2,18},{10... | collective-permute-start | bytes 589832 | tf_op jit(solution)/shard_map/ppermute | solution.py:26
  139.2 7.2 %collective-permute-start.40 = (bf16[6,128,128]{2,1,0:T(8,128)(2,1)S(1)}, bf16[6,128,128]{2,1,0:T(8,128)(2,1)S(1)}, u32[]{:S(2)}, u32[]{:S(2)}) collective-permute-start(bf16[6,128,128]{2,1,0:T(8,128)(2,1)S(1)} %get-tuple-element.74), channel_id=1, source_target_pairs={{0,24},{8,16},{16,8},{24,0},{1,25},{9,17},{17,9},{25,1},{2,26},{10... | collective-permute-start | bytes 589832 | tf_op jit(solution)/shard_map/ppermute | solution.py:26
  144.3 9.1 %collective-permute-start.24 = (bf16[2,128,128]{2,1,0:T(8,128)(2,1)S(1)}, bf16[2,128,128]{2,1,0:T(8,128)(2,1)S(1)}, u32[]{:S(2)}, u32[]{:S(2)}) collective-permute-start(bf16[2,128,128]{2,1,0:T(8,128)(2,1)S(1)} %get-tuple-element.59), channel_id=1, source_target_pairs={{0,24},{8,16},{16,8},{24,0},{1,25},{9,17},{17,9},{25,1},{2,26},{10... | collective-permute-start | bytes 196616 | tf_op jit(solution)/shard_map/ppermute | solution.py:26
  149.1 10.5 %collective-permute-start.41 = (bf16[64,768]{1,0:T(8,128)(2,1)S(1)}, bf16[64,768]{1,0:T(8,128)(2,1)S(1)}, u32[]{:S(2)}, u32[]{:S(2)}) collective-permute-start(bf16[64,768]{1,0:T(8,128)(2,1)S(1)} %get-tuple-element.76), channel_id=1, source_target_pairs={{0,1},{1,0},{2,3},{3,2},{4,5},{5,4},{6,7},{7,6},{8,9},{9,8},{10,11... | collective-permute-start | bytes 294920 | tf_op jit(solution)/shard_map/ppermute | solution.py:26
  149.2 13.1 %collective-permute-start.42 = (bf16[64,768]{1,0:T(8,128)(2,1)S(1)}, bf16[64,768]{1,0:T(8,128)(2,1)S(1)}, u32[]{:S(2)}, u32[]{:S(2)}) collective-permute-start(bf16[64,768]{1,0:T(8,128)(2,1)S(1)} %get-tuple-element.77), channel_id=1, source_target_pairs={{0,2},{1,3},{2,0},{3,1},{4,6},{5,7},{6,4},{7,5},{8,10},{9,11},{10,... | collective-permute-start | bytes 294920 | tf_op jit(solution)/shard_map/ppermute | solution.py:26
  155.1 1.9 %collective-permute-start.25 = (bf16[64,256]{1,0:T(8,128)(2,1)S(1)}, bf16[64,256]{1,0:T(8,128)(2,1)S(1)}, u32[]{:S(2)}, u32[]{:S(2)}) collective-permute-start(bf16[64,256]{1,0:T(8,128)(2,1)S(1)} %get-tuple-element.61), channel_id=1, source_target_pairs={{0,1},{1,0},{2,3},{3,2},{4,5},{5,4},{6,7},{7,6},{8,9},{9,8},{10,11... | collective-permute-start | bytes 98312 | tf_op jit(solution)/shard_map/ppermute | solution.py:26
  155.1 4.3 %collective-permute-start.26 = (bf16[64,256]{1,0:T(8,128)(2,1)S(1)}, bf16[64,256]{1,0:T(8,128)(2,1)S(1)}, u32[]{:S(2)}, u32[]{:S(2)}) collective-permute-start(bf16[64,256]{1,0:T(8,128)(2,1)S(1)} %get-tuple-element.62), channel_id=1, source_target_pairs={{0,2},{1,3},{2,0},{3,1},{4,6},{5,7},{6,4},{7,5},{8,10},{9,11},{10,... | collective-permute-start | bytes 98312 | tf_op jit(solution)/shard_map/ppermute | solution.py:26
  155.4 8.4 %collective-permute-start.43 = (bf16[64,768]{1,0:T(8,128)(2,1)S(1)}, bf16[64,768]{1,0:T(8,128)(2,1)S(1)}, u32[]{:S(2)}, u32[]{:S(2)}) collective-permute-start(bf16[64,768]{1,0:T(8,128)(2,1)S(1)} %get-tuple-element.78), channel_id=1, source_target_pairs={{0,3},{1,2},{2,1},{3,0},{4,7},{5,6},{6,5},{7,4},{8,11},{9,10},{10,... | collective-permute-start | bytes 294920 | tf_op jit(solution)/shard_map/ppermute | solution.py:26
  157.0 6.8 %collective-permute-start.44 = (bf16[64,768]{1,0:T(8,128)(2,1)S(1)}, bf16[64,768]{1,0:T(8,128)(2,1)S(1)}, u32[]{:S(2)}, u32[]{:S(2)}) collective-permute-start(bf16[64,768]{1,0:T(8,128)(2,1)S(1)} %get-tuple-element.79), channel_id=1, source_target_pairs={{0,4},{1,5},{2,6},{3,7},{4,0},{5,1},{6,2},{7,3},{8,12},{9,13},{10,... | collective-permute-start | bytes 294920 | tf_op jit(solution)/shard_map/ppermute | solution.py:26
  159.5 14.2 %collective-permute-start.45 = (bf16[64,768]{1,0:T(8,128)(2,1)S(1)}, bf16[64,768]{1,0:T(8,128)(2,1)S(1)}, u32[]{:S(2)}, u32[]{:S(2)}) collective-permute-start(bf16[64,768]{1,0:T(8,128)(2,1)S(1)} %get-tuple-element.80), channel_id=1, source_target_pairs={{0,5},{1,4},{2,7},{3,6},{4,1},{5,0},{6,3},{7,2},{8,13},{9,12},{10,... | collective-permute-start | bytes 294920 | tf_op jit(solution)/shard_map/ppermute | solution.py:26
  159.6 14.0 %collective-permute-start.46 = (bf16[64,768]{1,0:T(8,128)(2,1)S(1)}, bf16[64,768]{1,0:T(8,128)(2,1)S(1)}, u32[]{:S(2)}, u32[]{:S(2)}) collective-permute-start(bf16[64,768]{1,0:T(8,128)(2,1)S(1)} %get-tuple-element.81), channel_id=1, source_target_pairs={{0,6},{1,7},{2,4},{3,5},{4,2},{5,3},{6,0},{7,1},{8,14},{9,15},{10,... | collective-permute-start | bytes 294920 | tf_op jit(solution)/shard_map/ppermute | solution.py:26
  162.3 14.4 %collective-permute-start.47 = (bf16[64,768]{1,0:T(8,128)(2,1)S(1)}, bf16[64,768]{1,0:T(8,128)(2,1)S(1)}, u32[]{:S(2)}, u32[]{:S(2)}) collective-permute-start(bf16[64,768]{1,0:T(8,128)(2,1)S(1)} %get-tuple-element.82), channel_id=1, source_target_pairs={{0,7},{1,6},{2,5},{3,4},{4,3},{5,2},{6,1},{7,0},{8,15},{9,14},{10,... | collective-permute-start | bytes 294920 | tf_op jit(solution)/shard_map/ppermute | solution.py:26
  163.8 14.8 %collective-permute-start.27 = (bf16[64,256]{1,0:T(8,128)(2,1)S(1)}, bf16[64,256]{1,0:T(8,128)(2,1)S(1)}, u32[]{:S(2)}, u32[]{:S(2)}) collective-permute-start(bf16[64,256]{1,0:T(8,128)(2,1)S(1)} %get-tuple-element.63), channel_id=1, source_target_pairs={{0,3},{1,2},{2,1},{3,0},{4,7},{5,6},{6,5},{7,4},{8,11},{9,10},{10,... | collective-permute-start | bytes 98312 | tf_op jit(solution)/shard_map/ppermute | solution.py:26
  163.8 16.8 %collective-permute-start.28 = (bf16[64,256]{1,0:T(8,128)(2,1)S(1)}, bf16[64,256]{1,0:T(8,128)(2,1)S(1)}, u32[]{:S(2)}, u32[]{:S(2)}) collective-permute-start(bf16[64,256]{1,0:T(8,128)(2,1)S(1)} %get-tuple-element.64), channel_id=1, source_target_pairs={{0,4},{1,5},{2,6},{3,7},{4,0},{5,1},{6,2},{7,3},{8,12},{9,13},{10,... | collective-permute-start | bytes 98312 | tf_op jit(solution)/shard_map/ppermute | solution.py:26
  173.6 7.7 %collective-permute-start.29 = (bf16[64,256]{1,0:T(8,128)(2,1)S(1)}, bf16[64,256]{1,0:T(8,128)(2,1)S(1)}, u32[]{:S(2)}, u32[]{:S(2)}) collective-permute-start(bf16[64,256]{1,0:T(8,128)(2,1)S(1)} %get-tuple-element.65), channel_id=1, source_target_pairs={{0,5},{1,4},{2,7},{3,6},{4,1},{5,0},{6,3},{7,2},{8,13},{9,12},{10,... | collective-permute-start | bytes 98312 | tf_op jit(solution)/shard_map/ppermute | solution.py:26
  173.6 7.7 %collective-permute-start.30 = (bf16[64,256]{1,0:T(8,128)(2,1)S(1)}, bf16[64,256]{1,0:T(8,128)(2,1)S(1)}, u32[]{:S(2)}, u32[]{:S(2)}) collective-permute-start(bf16[64,256]{1,0:T(8,128)(2,1)S(1)} %get-tuple-element.66), channel_id=1, source_target_pairs={{0,6},{1,7},{2,4},{3,5},{4,2},{5,3},{6,0},{7,1},{8,14},{9,15},{10,... | collective-permute-start | bytes 98312 | tf_op jit(solution)/shard_map/ppermute | solution.py:26
  176.7 5.2 %collective-permute-start.31 = (bf16[64,256]{1,0:T(8,128)(2,1)S(1)}, bf16[64,256]{1,0:T(8,128)(2,1)S(1)}, u32[]{:S(2)}, u32[]{:S(2)}) collective-permute-start(bf16[64,256]{1,0:T(8,128)(2,1)S(1)} %get-tuple-element.67), channel_id=1, source_target_pairs={{0,7},{1,6},{2,5},{3,4},{4,3},{5,2},{6,1},{7,0},{8,15},{9,14},{10,... | collective-permute-start | bytes 98312 | tf_op jit(solution)/shard_map/ppermute | solution.py:26

commit v4 on v3

--- a/solution.py
+++ b/solution.py
@@ -11,7 +11,6 @@
 DK = 128
 CAP = 64
 LAST_HEADS = 2
-PIECES = (True, True)
 EARLY = (True, False)
 LIMIT = 24 << 20
 VMEM = pl.BlockSpec(memory_space=pltpu.VMEM)
@@ -49,11 +48,10 @@
         at = index + k * CAP
         pick = jnp.where((at == crossed[0]) | (at == crossed[1]), 1.0, 0.0).astype(bf16)
         sent[k][...] = contract(pick, hidden[...], 1, 0).astype(bf16)
-    slots = [(name * CAP + place).astype(jnp.float32) for name, place in zip(named, places)]
+    slots = [c.astype(jnp.float32) for c in crossed]
     level = levels[...].astype(jnp.float32)
     gates = level / (level[0:1, :] + level[1:2, :])
-    turned = [c.astype(jnp.float32) for c in crossed]
-    entries = jnp.concatenate(slots + [gates] + turned + [jnp.zeros((2, count), jnp.float32)], axis=0)
+    entries = jnp.concatenate(slots + [gates, jnp.zeros((4, count), jnp.float32)], axis=0)
     table[...] = entries.T
 
 
@@ -121,46 +119,59 @@
         at_col += cols
 
 
-def query_kernel(here, x, *refs):
+def near_query_kernel(x, *refs):
     *quarters, out = refs
     for k, quarter in enumerate(quarters):
         cols = quarter.shape[1]
+        out[:, k * cols : (k + 1) * cols] = contract(x[...], quarter[...], 1, 0).astype(bf16)
+
+
+def query_kernel(here, x, near, *refs):
+    *quarters, out = refs
+    cols = quarters[0].shape[1]
+    known = near.shape[1] // cols
+    for k in range(known + len(quarters)):
         at = pl.multiple_of(((here[1] & 3) ^ k) * cols, cols)
-        out[:, pl.ds(at, cols)] = contract(x[...], quarter[...], 1, 0).astype(bf16)
-
-
-def attend_kernel(here, q_all, k, v, *refs, first, others):
-    states, outs = refs[:others], refs[others:]
-    length = k.shape[0]
-    if len(outs) > 1:
-        *outs, out = outs
-    else:
-        (out,), outs = outs, []
-    step = length // 2
+        if k < known:
+            out[:, pl.ds(at, cols)] = near[:, k * cols : (k + 1) * cols]
+        else:
+            out[:, pl.ds(at, cols)] = contract(x[...], quarters[k - known][...], 1, 0).astype(bf16)
+
+
+def local_kernel(q_all, k, v, reads, *, first):
+    step = k.shape[0] // 2
     row = lax.broadcasted_iota(jnp.int32, (step, step), 0)
     col = lax.broadcasted_iota(jnp.int32, (step, step), 1)
     causal = row >= col
+    for head in range(k.shape[1] // DK):
+        cols = slice(head * DK, (head + 1) * DK)
+        q_cols = slice((first + head) * DK, (first + head + 1) * DK)
+        for b in range(2):
+            rows = slice(b * step, (b + 1) * step)
+            q = q_all[rows, q_cols]
+            scores = jnp.where(causal, contract(q, k[rows, cols], 1, 1), 0.0).astype(bf16)
+            total = contract(scores, v[rows, cols], 1, 0)
+            for e in range(b):
+                before = slice(e * step, (e + 1) * step)
+                scores = contract(q, k[before, cols], 1, 1).astype(bf16)
+                total = total + contract(scores, v[before, cols], 1, 0)
+            reads[rows, cols] = total
+
+
+def attend_kernel(here, q_all, reads, *refs, first, others):
+    states, outs, out = refs[:others], refs[others:-1], refs[-1]
     for head in range(states[0].shape[0]):
         cols = slice(head * DK, (head + 1) * DK)
-        q_cols = slice((first + head) * DK, (first + head + 1) * DK)
+        q = q_all[:, (first + head) * DK : (first + head + 1) * DK]
         state = jnp.zeros((DK, DK), jnp.float32)
         for m, other in enumerate(states, 1):
             earlier = (here[0] ^ m) < here[0]
             state = state + jnp.where(earlier, other[head].astype(jnp.float32), 0.0)
         high = state.astype(bf16)
         low = (state - high.astype(jnp.float32)).astype(bf16)
-        for b in range(2):
-            rows = slice(b * step, (b + 1) * step)
-            q = q_all[rows, q_cols]
-            scores = jnp.where(causal, contract(q, k[rows, cols], 1, 1), 0.0).astype(bf16)
-            reads = contract(scores, v[rows, cols], 1, 0)
-            for e in range(b):
-                before = slice(e * step, (e + 1) * step)
-                scores = contract(q, k[before, cols], 1, 1).astype(bf16)
-                reads = reads + contract(scores, v[before, cols], 1, 0)
-            reads = reads + contract(q, high, 1, 0) + contract(q, low, 1, 0)
-            scale = lax.rsqrt(jnp.mean(reads * reads, axis=-1, keepdims=True) + 1e-06)
-            out[rows, cols] = (reads * scale).astype(bf16)
+        total = reads[:, cols] + contract(q, high, 1, 0) + contract(q, low, 1, 0)
+        scale = lax.rsqrt(jnp.mean(total * total, axis=-1, keepdims=True) + 1e-06)
+        out[:, cols] = (total * scale).astype(bf16)
     for k, piece in enumerate(outs):
         piece[...] = out[pl.ds(pl.multiple_of((here[1] ^ k) * CAP, CAP), CAP), :]
 
@@ -172,10 +183,9 @@
         out[:, :at] = done[...]
     part = jnp.concatenate([p[...] for p in pieces], axis=0)
     index = lax.broadcasted_iota(jnp.int32, (count, part.shape[0]), 1).astype(jnp.float32)
-    column = 4 if parts > 1 else 0
     mixed = None
     for j in range(2):
-        pick = jnp.where(index == table[:, column + j : column + j + 1], 1.0, 0.0).astype(bf16)
+        pick = jnp.where(index == table[:, j : j + 1], 1.0, 0.0).astype(bf16)
         term = table[:, 2 + j : 3 + j] * contract(pick, part, 1, 0)
         mixed = term if mixed is None else mixed + term
     out[:, at:] = mixed.astype(bf16)
@@ -274,17 +284,25 @@
     quarter1 = swap(mine, "mem", 1)
     quarter2 = swap(mine, "mem", 2)
     quarter3 = swap(quarter2, "mem", 1)
+    near_queries = call(
+        near_query_kernel,
+        shape((length, 2 * quarter), bf16),
+        [VMEM] * 3,
+        arrived,
+        mine,
+        quarter1,
+        flops=length * model * width,
+    )
     queries = call(
         query_kernel,
         shape((length, width), bf16),
-        [SMEM] + [VMEM] * 5,
+        [SMEM] + [VMEM] * 4,
         here,
         arrived,
-        mine,
-        quarter1,
+        near_queries,
         quarter2,
         quarter3,
-        flops=2 * length * model * width,
+        flops=length * model * width,
     )
 
     out = None
@@ -322,29 +340,29 @@
         states = []
         for m in range(1, groups):
             states.append(swap(total, "seq", m))
-        pieces = experts if PIECES[c] else 1
-        normed = call(
-            functools.partial(attend_kernel, first=first, others=len(states)),
-            [shape((length // pieces, cols), bf16)] * pieces,
-            [SMEM] + [VMEM] * (3 + len(states)),
-            here,
+        reads = call(
+            functools.partial(local_kernel, first=first),
+            shape((length, cols), jnp.float32),
+            [VMEM] * 3,
             queries,
             keys,
             values,
+            flops=3 * length * length * cols,
+        )
+        normed = call(
+            functools.partial(attend_kernel, first=first, others=len(states)),
+            [shape((CAP, cols), bf16)] * experts,
+            [SMEM] + [VMEM] * (2 + len(states)),
+            here,
+            queries,
+            reads,
             *states,
-            flops=4 * length * length * cols,
-            scratch=[pltpu.VMEM((length, cols), bf16)] if pieces > 1 else [],
-        )
-        if pieces > 1:
-            back = [normed[0]]
-            for k in range(1, experts):
-                back.append(swap(normed[k], "mem", k))
-        else:
-            back = [
-                lax.all_to_all(
-                    normed[0].reshape(experts, CAP, cols), "mem", split_axis=0, concat_axis=0, tiled=True
-                ).reshape(length, cols)
-            ]
+            flops=4 * length * DK * cols,
+            scratch=[pltpu.VMEM((length, cols), bf16)],
+        )
+        back = [normed[0]]
+        for k in range(1, experts):
+            back.append(swap(normed[k], "mem", k))
         prior = [] if out is None else [out]
         out = call(
             functools.partial(combine_kernel, parts=len(back), at=first * DK),

time: 184 us -> 187 us (1.016)
  local copies, waits for them, and re-layouts: 0.01 us -> 2.59 us
    unnamed x6, local copies, waits for them, and re-layouts: 0.01 us -> 2.59 us
    pallas_call x14 -> x17, Pallas kernels: 24.9 us -> 26.6 us  [call(): pl.pallas_call(kernel, out_shape=outs if last else jax.tree.map(lambda s:...]
where the time goes in v4:
time: 187 us; the launch traced here: 186 us
  waiting for transfers between devices  95.4 us (51%)
  starting transfers between devices  61.4 us (33%)
  Pallas kernels  26.6 us (14%)
  local copies, waits for them, and re-layouts  2.59 us (1%)
    ppermute x48, waiting for transfers between devices, swap(): lax.ppermute(array, axis, [(i, i ^ mask) for i in range(lax.axis_size(axi...  95.4 us
    ppermute x48, starting transfers between devices, swap(): lax.ppermute(array, axis, [(i, i ^ mask) for i in range(lax.axis_size(axi...  61.4 us
    pallas_call x17, Pallas kernels, call(): pl.pallas_call(kernel, out_shape=outs if last else jax.tree.map(lambda s:...  26.6 us
  transfers between devices with their start and end apart: 48, of which 16 were waited for; matrix products, arithmetic and copies ran while one was open for 0% of the time, Pallas kernels for 12%

profile of v4, /device:TPU:0, one launch (start us, length us, event | category | flops | bytes accessed | tf_op | source)
XLA Modules:
  0.0 186.3 jit_solution(11130863971423299580)
XLA Ops:
  0.1 1.2 copy-done
  1.3 0.7 copy-done.1
  2.0 0.7 copy-done.2
  2.7 2.3 %shard_map.64 = (f32[256,8]{1,0:T(8,128)S(1)}, bf16[64,2048]{1,0:T(8,128)(2,1)S(1)}, bf16[64,2048]{1,0:T(8,128)(2,1)S(1)}, bf16[64,2048]{1,0:T(8,128)(2,1)S(1)},...) custom-call(s32[2]{0:T(128)S(1)} %pad_add_fusion.here, ...), custom_call_target="tpu_custom_call" | custom-call | flops 536870912 | bytes 1048576 | tf_op jit(solution)/shard_map/pallas_call | solution.py:199
  5.5 1.5 shard_map.66
  7.0 2.6 %collective-permute-start.10 = (bf16[512,128]{1,0:T(8,128)(2,1)S(1)}, bf16[512,128]{1,0:T(8,128)(2,1)S(1)}, u32[]{:S(2)}, u32[]{:S(2)}) collective-permute-start(bf16[512,128]{1,0:T(8,128)(2,1)S(1)} %get-tuple-element.54.refs_4_), channel_id=1, source_target_pairs={{0,16},{8,24},{16,0},{24,8},{1,17},{9,25},{17,1},{25,9},{2,18},{10... | collective-permute-start | bytes 393224 | tf_op jit(solution)/shard_map/ppermute | solution.py:25
  9.6 1.5 collective-permute-start.7
  11.7 2.0 %collective-permute-done.10.refs_5_ = bf16[512,128]{1,0:T(8,128)(2,1)S(1)} collective-permute-done((bf16[512,128]{1,0:T(8,128)(2,1)S(1)}, bf16[512,128]{1,0:T(8,128)(2,1)S(1)}, u32[]{:S(2)}, u32[]{:S(2)}) %collective-permute-start.10) | collective-permute-done | bytes 131104 | tf_op jit(solution)/shard_map/ppermute | solution.py:25
  13.8 1.9 %collective-permute-start.1 = (bf16[64,2048]{1,0:T(8,128)(2,1)S(1)}, bf16[64,2048]{1,0:T(8,128)(2,1)S(1)}, u32[]{:S(2)}, u32[]{:S(2)}) collective-permute-start(bf16[64,2048]{1,0:T(8,128)(2,1)S(1)} %get-tuple-element.47), channel_id=1, source_target_pairs={{0,2},{1,3},{2,0},{3,1},{4,6},{5,7},{6,4},{7,5},{8,10},{9,11},{10,... | collective-permute-start | bytes 786440 | tf_op jit(solution)/shard_map/ppermute | solution.py:25
  16.0 2.1 %collective-permute-done.11.refs_6_ = bf16[512,128]{1,0:T(8,128)(2,1)S(1)} collective-permute-done((bf16[512,128]{1,0:T(8,128)(2,1)S(1)}, bf16[512,128]{1,0:T(8,128)(2,1)S(1)}, u32[]{:S(2)}, u32[]{:S(2)}) %collective-permute-start.11) | collective-permute-done | bytes 131104 | tf_op jit(solution)/shard_map/ppermute | solution.py:25
  18.1 2.6 %collective-permute-start.3 = (bf16[64,2048]{1,0:T(8,128)(2,1)S(1)}, bf16[64,2048]{1,0:T(8,128)(2,1)S(1)}, u32[]{:S(2)}, u32[]{:S(2)}) collective-permute-start(bf16[64,2048]{1,0:T(8,128)(2,1)S(1)} %get-tuple-element.49), channel_id=1, source_target_pairs={{0,4},{1,5},{2,6},{3,7},{4,0},{5,1},{6,2},{7,3},{8,12},{9,13},{10,... | collective-permute-start | bytes 786440 | tf_op jit(solution)/shard_map/ppermute | solution.py:25
  20.7 2.6 %collective-permute-start.5 = (bf16[64,2048]{1,0:T(8,128)(2,1)S(1)}, bf16[64,2048]{1,0:T(8,128)(2,1)S(1)}, u32[]{:S(2)}, u32[]{:S(2)}) collective-permute-start(bf16[64,2048]{1,0:T(8,128)(2,1)S(1)} %get-tuple-element.51), channel_id=1, source_target_pairs={{0,6},{1,7},{2,4},{3,5},{4,2},{5,3},{6,0},{7,1},{8,14},{9,15},{10,... | collective-permute-start | bytes 786440 | tf_op jit(solution)/shard_map/ppermute | solution.py:25
  23.3 8.1 %collective-permute-done.1.refs_2_ = bf16[64,2048]{1,0:T(8,128)(2,1)S(1)} collective-permute-done((bf16[64,2048]{1,0:T(8,128)(2,1)S(1)}, bf16[64,2048]{1,0:T(8,128)(2,1)S(1)}, u32[]{:S(2)}, u32[]{:S(2)}) %collective-permute-start.1) | collective-permute-done | bytes 262176 | tf_op jit(solution)/shard_map/ppermute | solution.py:25
  31.3 3.5 %collective-permute-done.2.refs_3_ = bf16[64,2048]{1,0:T(8,128)(2,1)S(1)} collective-permute-done((bf16[64,2048]{1,0:T(8,128)(2,1)S(1)}, bf16[64,2048]{1,0:T(8,128)(2,1)S(1)}, u32[]{:S(2)}, u32[]{:S(2)}) %collective-permute-start.2) | collective-permute-done | bytes 262176 | tf_op jit(solution)/shard_map/ppermute | solution.py:25
  34.8 1.1 collective-permute-start.12
  35.9 2.2 %collective-permute-start.9 = (bf16[512,128]{1,0:T(8,128)(2,1)S(1)}, bf16[512,128]{1,0:T(8,128)(2,1)S(1)}, u32[]{:S(2)}, u32[]{:S(2)}) collective-permute-start(bf16[512,128]{1,0:T(8,128)(2,1)S(1)} %collective-permute-done.7.refs_1_), channel_id=1, source_target_pairs={{0,16},{8,24},{16,0},{24,8},{1,17},{9,25},{17,1},{25,9},{2,18},{10... | collective-permute-start | bytes 393224 | tf_op jit(solution)/shard_map/ppermute | solution.py:25
  38.1 1.6 shard_map.70
  39.7 14.0 %collective-permute-done.4.refs_5_ = bf16[64,2048]{1,0:T(8,128)(2,1)S(1)} collective-permute-done((bf16[64,2048]{1,0:T(8,128)(2,1)S(1)}, bf16[64,2048]{1,0:T(8,128)(2,1)S(1)}, u32[]{:S(2)}, u32[]{:S(2)}) %collective-permute-start.4) | collective-permute-done | bytes 262176 | tf_op jit(solution)/shard_map/ppermute | solution.py:25
  53.6 1.5 collective-permute-start.16
  55.7 1.5 collective-permute-start.17
  57.7 0.7 shard_map.67.refs_0_
  58.5 8.5 %collective-permute-start.14 = (bf16[2048,256]{1,0:T(8,128)(2,1)S(1)}, bf16[2048,256]{1,0:T(8,128)(2,1)S(1)}, u32[]{:S(2)}, u32[]{:S(2)}) collective-permute-start(bf16[2048,256]{1,0:T(8,128)(2,1)S(1)} %shard_map.67.refs_0_), channel_id=1, source_target_pairs={{0,2},{1,3},{2,0},{3,1},{4,6},{5,7},{6,4},{7,5},{8,10},{9,11},{10,... | collective-permute-start | bytes 3145736 | tf_op jit(solution)/shard_map/ppermute | solution.py:25
  67.0 1.9 %shard_map.74 = (bf16[512,768]{1,0:T(8,128)(2,1)S(1)}, bf16[512,768]{1,0:T(8,128)(2,1)S(1)}) custom-call(s32[2]{0:T(128)S(1)} %pad_add_fusion.here, bf16[512,1024]{1,0:T(8,128)(2,1)} %refs_0_.5, bf16[1,512,1024]{2,1,0:T(8,128)(2,1)} %refs_1_.5, bf16[1,512,1024]{2,1,0:T(8,128)(2,1)} %refs_2_.5), custom_call_target="tpu_custom_call" | custom-call | flops 1 | bytes 1048576 | tf_op jit(solution)/shard_map/pallas_call | solution.py:199
  68.9 1.3 collective-permute-start.32
  70.2 0.7 collective-permute-start.34
  70.9 1.3 collective-permute-start.18
  72.2 0.7 collective-permute-start.36
  73.0 23.3 %collective-permute-done.18.refs_3_ = bf16[512,256]{1,0:T(8,128)(2,1)S(1)} collective-permute-done((bf16[512,256]{1,0:T(8,128)(2,1)S(1)}, bf16[512,256]{1,0:T(8,128)(2,1)S(1)}, u32[]{:S(2)}, u32[]{:S(2)}) %collective-permute-start.18) | collective-permute-done | bytes 262176 | tf_op jit(solution)/shard_map/ppermute | solution.py:25
  96.2 0.8 collective-permute-start.21
  97.0 6.4 %collective-permute-done.21.refs_7_ = bf16[512,256]{1,0:T(8,128)(2,1)S(1)} collective-permute-done((bf16[512,256]{1,0:T(8,128)(2,1)S(1)}, bf16[512,256]{1,0:T(8,128)(2,1)S(1)}, u32[]{:S(2)}, u32[]{:S(2)}) %collective-permute-start.21) | collective-permute-done | bytes 262176 | tf_op jit(solution)/shard_map/ppermute | solution.py:25
  103.4 1.3 collective-permute-start.37
  105.3 1.3 collective-permute-start.35
  106.7 6.4 %collective-permute-done.36.refs_2_ = bf16[512,768]{1,0:T(8,128)(2,1)S(1)} collective-permute-done((bf16[512,768]{1,0:T(8,128)(2,1)S(1)}, bf16[512,768]{1,0:T(8,128)(2,1)S(1)}, u32[]{:S(2)}, u32[]{:S(2)}) %collective-permute-start.36) | collective-permute-done | bytes 786464 | tf_op jit(solution)/shard_map/ppermute | solution.py:25
  113.6 0.7 shard_map.65.x
  114.3 2.1 %shard_map.71 = (bf16[512,256]{1,0:T(8,128)(2,1)S(1)}, bf16[512,256]{1,0:T(8,128)(2,1)S(1)}, bf16[2,128,128]{2,1,0:T(8,128)(2,1)S(1)}) custom-call(s32[2]{0:T(128)S(1)} %pad_add_fusion.here, bf16[512,2048]{1,0:T(8,128)(2,1)S(1)} %shard_map.65.x, bf16[512,256]{1,0:T(8,128)(2,1)S(1)} %get-tuple-element.55.refs_0_, ...), custom_call_target="tpu_custom_call" | custom-call | flops 1073741824 | bytes 1048576 | tf_op jit(solution)/shard_map/pallas_call | solution.py:199
  116.3 7.5 %collective-permute-done.37.refs_5_ = bf16[512,768]{1,0:T(8,128)(2,1)S(1)} collective-permute-done((bf16[512,768]{1,0:T(8,128)(2,1)S(1)}, bf16[512,768]{1,0:T(8,128)(2,1)S(1)}, u32[]{:S(2)}, u32[]{:S(2)}) %collective-permute-start.37) | collective-permute-done | bytes 786464 | tf_op jit(solution)/shard_map/ppermute | solution.py:25
  123.9 1.3 collective-permute-start.22
  125.2 3.2 %shard_map.75 = (f32[512,768]{1,0:T(8,128)S(1)}, f32[512,768]{1,0:T(8,128)S(1)}) custom-call(s32[2]{0:T(128)S(1)} %pad_add_fusion.here, bf16[512,2048]{1,0:T(8,128)(2,1)S(1)} %shard_map.65.x, bf16[512,768]{1,0:T(8,128)(2,1)S(1)} %get-tuple-element.68.refs_0_, bf16[512,768]{1,0:T(8,128)(2,1)S(1)} %collective-permute-done.32.refs_1_, ...), custom_call_target="tpu_custom_call" | custom-call | flops 2415919104 | bytes 1048576 | tf_op jit(solution)/shard_map/pallas_call | solution.py:199
  128.6 8.8 %collective-permute-done.35.refs_1_ = bf16[512,768]{1,0:T(8,128)(2,1)S(1)} collective-permute-done((bf16[512,768]{1,0:T(8,128)(2,1)S(1)}, bf16[512,768]{1,0:T(8,128)(2,1)S(1)}, u32[]{:S(2)}, u32[]{:S(2)}) %collective-permute-start.35) | collective-permute-done | bytes 786464 | tf_op jit(solution)/shard_map/ppermute | solution.py:25
  137.4 1.9 %shard_map.76 = (bf16[512,768]{1,0:T(8,128)(2,1)S(1)}, bf16[512,768]{1,0:T(8,128)(2,1)S(1)}, bf16[6,128,128]{2,1,0:T(8,128)(2,1)S(1)}) custom-call(s32[2]{0:T(128)S(1)} %pad_add_fusion.here, bf16[512,2048]{1,0:T(8,128)(2,1)S(1)} %shard_map.65.x, bf16[512,768]{1,0:T(8,128)(2,1)S(1)} %collective-permute-done.33.refs_0_, ...), custom_call_target="tpu_custom_call" | custom-call | flops 3221225472 | bytes 1048576 | tf_op jit(solution)/shard_map/pallas_call | solution.py:199
  139.3 1.4 collective-permute-start.38
  140.7 0.6 collective-permute-start.39
  141.3 1.6 collective-permute-start.40
  142.9 1.2 shard_map.68.near
  144.2 1.3 collective-permute-start.23
  145.4 1.8 shard_map.69.q_all
  147.2 2.5 %shard_map.77.reads = f32[512,768]{1,0:T(8,128)S(1)} custom-call(bf16[512,1024]{1,0:T(8,128)(2,1)S(1)} %shard_map.69.q_all, bf16[512,768]{1,0:T(8,128)(2,1)S(1)} %get-tuple-element.72.k, bf16[512,768]{1,0:T(8,128)(2,1)S(1)} %get-tuple-element.73.v), custom_call_target="tpu_custom_call" | custom-call | flops 603979776 | bytes 1048576 | tf_op jit(solution)/shard_map/pallas_call | solution.py:199
  149.8 1.8 collective-permute-start.24
  151.6 1.4 shard_map.78
  153.1 3.8 %collective-permute-start.42 = (bf16[64,768]{1,0:T(8,128)(2,1)S(1)}, bf16[64,768]{1,0:T(8,128)(2,1)S(1)}, u32[]{:S(2)}, u32[]{:S(2)}) collective-permute-start(bf16[64,768]{1,0:T(8,128)(2,1)S(1)} %get-tuple-element.77), channel_id=1, source_target_pairs={{0,2},{1,3},{2,0},{3,1},{4,6},{5,7},{6,4},{7,5},{8,10},{9,11},{10,... | collective-permute-start | bytes 294920 | tf_op jit(solution)/shard_map/ppermute | solution.py:25
  156.8 0.9 shard_map.72.reads
  157.7 1.0 shard_map.73
  159.3 1.4 collective-permute-start.43
  160.7 1.6 collective-permute-start.44
  162.3 0.9 collective-permute-done.26.refs_2_
  163.4 2.2 %collective-permute-start.46 = (bf16[64,768]{1,0:T(8,128)(2,1)S(1)}, bf16[64,768]{1,0:T(8,128)(2,1)S(1)}, u32[]{:S(2)}, u32[]{:S(2)}) collective-permute-start(bf16[64,768]{1,0:T(8,128)(2,1)S(1)} %get-tuple-element.81), channel_id=1, source_target_pairs={{0,6},{1,7},{2,4},{3,5},{4,2},{5,3},{6,0},{7,1},{8,14},{9,15},{10,... | collective-permute-start | bytes 294920 | tf_op jit(solution)/shard_map/ppermute | solution.py:25
  165.6 2.2 %collective-permute-start.47 = (bf16[64,768]{1,0:T(8,128)(2,1)S(1)}, bf16[64,768]{1,0:T(8,128)(2,1)S(1)}, u32[]{:S(2)}, u32[]{:S(2)}) collective-permute-start(bf16[64,768]{1,0:T(8,128)(2,1)S(1)} %get-tuple-element.82), channel_id=1, source_target_pairs={{0,7},{1,6},{2,5},{3,4},{4,3},{5,2},{6,1},{7,0},{8,15},{9,14},{10,... | collective-permute-start | bytes 294920 | tf_op jit(solution)/shard_map/ppermute | solution.py:25
  167.7 8.0 %collective-permute-done.44.refs_4_ = bf16[64,768]{1,0:T(8,128)(2,1)S(1)} collective-permute-done((bf16[64,768]{1,0:T(8,128)(2,1)S(1)}, bf16[64,768]{1,0:T(8,128)(2,1)S(1)}, u32[]{:S(2)}, u32[]{:S(2)}) %collective-permute-start.44) | collective-permute-done | bytes 98336 | tf_op jit(solution)/shard_map/ppermute | solution.py:25
  175.7 1.3 collective-permute-done.45.refs_5_
  177.0 2.3 %collective-permute-start.30 = (bf16[64,256]{1,0:T(8,128)(2,1)S(1)}, bf16[64,256]{1,0:T(8,128)(2,1)S(1)}, u32[]{:S(2)}, u32[]{:S(2)}) collective-permute-start(bf16[64,256]{1,0:T(8,128)(2,1)S(1)} %get-tuple-element.66), channel_id=1, source_target_pairs={{0,6},{1,7},{2,4},{3,5},{4,2},{5,3},{6,0},{7,1},{8,14},{9,15},{10,... | collective-permute-start | bytes 98312 | tf_op jit(solution)/shard_map/ppermute | solution.py:25
  179.3 2.6 %collective-permute-start.31 = (bf16[64,256]{1,0:T(8,128)(2,1)S(1)}, bf16[64,256]{1,0:T(8,128)(2,1)S(1)}, u32[]{:S(2)}, u32[]{:S(2)}) collective-permute-start(bf16[64,256]{1,0:T(8,128)(2,1)S(1)} %get-tuple-element.67), channel_id=1, source_target_pairs={{0,7},{1,6},{2,5},{3,4},{4,3},{5,2},{6,1},{7,0},{8,15},{9,14},{10,... | collective-permute-start | bytes 98312 | tf_op jit(solution)/shard_map/ppermute | solution.py:25
  181.9 0.6 shard_map.79.refs_8_
  182.5 2.6 %collective-permute-done.28.refs_4_ = bf16[64,256]{1,0:T(8,128)(2,1)S(1)} collective-permute-done((bf16[64,256]{1,0:T(8,128)(2,1)S(1)}, bf16[64,256]{1,0:T(8,128)(2,1)S(1)}, u32[]{:S(2)}, u32[]{:S(2)}) %collective-permute-start.28) | collective-permute-done | bytes 32800 | tf_op jit(solution)/shard_map/ppermute | solution.py:25
  185.1 1.2 shard_map.80
  (56 shorter events, 4.6 us)
Async XLA Ops:
  0.1 1.2 copy-start
  1.3 0.7 copy-start.1
  2.0 0.7 copy-start.2
  5.0 15.7 %collective-permute-start = (bf16[64,2048]{1,0:T(8,128)(2,1)S(1)}, bf16[64,2048]{1,0:T(8,128)(2,1)S(1)}, u32[]{:S(2)}, u32[]{:S(2)}) collective-permute-start(bf16[64,2048]{1,0:T(8,128)(2,1)S(1)} %get-tuple-element.46), channel_id=1, source_target_pairs={{0,1},{1,0},{2,3},{3,2},{4,5},{5,4},{6,7},{7,6},{8,9},{9,8},{10,11... | collective-permute-start | bytes 786440 | tf_op jit(solution)/shard_map/ppermute | solution.py:25
  7.0 6.7 %collective-permute-start.10 = (bf16[512,128]{1,0:T(8,128)(2,1)S(1)}, bf16[512,128]{1,0:T(8,128)(2,1)S(1)}, u32[]{:S(2)}, u32[]{:S(2)}) collective-permute-start(bf16[512,128]{1,0:T(8,128)(2,1)S(1)} %get-tuple-element.54.refs_4_), channel_id=1, source_target_pairs={{0,16},{8,24},{16,0},{24,8},{1,17},{9,25},{17,1},{25,9},{2,18},{10... | collective-permute-start | bytes 393224 | tf_op jit(solution)/shard_map/ppermute | solution.py:25
  9.6 6.4 %collective-permute-start.7 = (bf16[512,128]{1,0:T(8,128)(2,1)S(1)}, bf16[512,128]{1,0:T(8,128)(2,1)S(1)}, u32[]{:S(2)}, u32[]{:S(2)}) collective-permute-start(bf16[512,128]{1,0:T(8,128)(2,1)S(1)} %get-tuple-element.53.refs_0_), channel_id=1, source_target_pairs={{0,8},{8,0},{16,24},{24,16},{1,9},{9,1},{17,25},{25,17},{2,10},{10... | collective-permute-start | bytes 393224 | tf_op jit(solution)/shard_map/ppermute | solution.py:25
  11.1 6.9 %collective-permute-start.11 = (bf16[512,128]{1,0:T(8,128)(2,1)S(1)}, bf16[512,128]{1,0:T(8,128)(2,1)S(1)}, u32[]{:S(2)}, u32[]{:S(2)}) collective-permute-start(bf16[512,128]{1,0:T(8,128)(2,1)S(1)} %get-tuple-element.54.refs_4_), channel_id=1, source_target_pairs={{0,8},{8,0},{16,24},{24,16},{1,9},{9,1},{17,25},{25,17},{2,10},{10... | collective-permute-start | bytes 393224 | tf_op jit(solution)/shard_map/ppermute | solution.py:25
  11.7 9.0 %collective-permute-start.8 = (bf16[512,128]{1,0:T(8,128)(2,1)S(1)}, bf16[512,128]{1,0:T(8,128)(2,1)S(1)}, u32[]{:S(2)}, u32[]{:S(2)}) collective-permute-start(bf16[512,128]{1,0:T(8,128)(2,1)S(1)} %get-tuple-element.53.refs_0_), channel_id=1, source_target_pairs={{0,16},{8,24},{16,0},{24,8},{1,17},{9,25},{17,1},{25,9},{2,18},{10... | collective-permute-start | bytes 393224 | tf_op jit(solution)/shard_map/ppermute | solution.py:25
  13.8 17.5 %collective-permute-start.1 = (bf16[64,2048]{1,0:T(8,128)(2,1)S(1)}, bf16[64,2048]{1,0:T(8,128)(2,1)S(1)}, u32[]{:S(2)}, u32[]{:S(2)}) collective-permute-start(bf16[64,2048]{1,0:T(8,128)(2,1)S(1)} %get-tuple-element.47), channel_id=1, source_target_pairs={{0,2},{1,3},{2,0},{3,1},{4,6},{5,7},{6,4},{7,5},{8,10},{9,11},{10,... | collective-permute-start | bytes 786440 | tf_op jit(solution)/shard_map/ppermute | solution.py:25
  16.0 18.8 %collective-permute-start.2 = (bf16[64,2048]{1,0:T(8,128)(2,1)S(1)}, bf16[64,2048]{1,0:T(8,128)(2,1)S(1)}, u32[]{:S(2)}, u32[]{:S(2)}) collective-permute-start(bf16[64,2048]{1,0:T(8,128)(2,1)S(1)} %get-tuple-element.48), channel_id=1, source_target_pairs={{0,3},{1,2},{2,1},{3,0},{4,7},{5,6},{6,5},{7,4},{8,11},{9,10},{10,... | collective-permute-start | bytes 786440 | tf_op jit(solution)/shard_map/ppermute | solution.py:25
  18.1 17.8 %collective-permute-start.3 = (bf16[64,2048]{1,0:T(8,128)(2,1)S(1)}, bf16[64,2048]{1,0:T(8,128)(2,1)S(1)}, u32[]{:S(2)}, u32[]{:S(2)}) collective-permute-start(bf16[64,2048]{1,0:T(8,128)(2,1)S(1)} %get-tuple-element.49), channel_id=1, source_target_pairs={{0,4},{1,5},{2,6},{3,7},{4,0},{5,1},{6,2},{7,3},{8,12},{9,13},{10,... | collective-permute-start | bytes 786440 | tf_op jit(solution)/shard_map/ppermute | solution.py:25
  20.6 33.0 %collective-permute-start.4 = (bf16[64,2048]{1,0:T(8,128)(2,1)S(1)}, bf16[64,2048]{1,0:T(8,128)(2,1)S(1)}, u32[]{:S(2)}, u32[]{:S(2)}) collective-permute-start(bf16[64,2048]{1,0:T(8,128)(2,1)S(1)} %get-tuple-element.50), channel_id=1, source_target_pairs={{0,5},{1,4},{2,7},{3,6},{4,1},{5,0},{6,3},{7,2},{8,13},{9,12},{10,... | collective-permute-start | bytes 786440 | tf_op jit(solution)/shard_map/ppermute | solution.py:25
  20.7 34.5 %collective-permute-start.5 = (bf16[64,2048]{1,0:T(8,128)(2,1)S(1)}, bf16[64,2048]{1,0:T(8,128)(2,1)S(1)}, u32[]{:S(2)}, u32[]{:S(2)}) collective-permute-start(bf16[64,2048]{1,0:T(8,128)(2,1)S(1)} %get-tuple-element.51), channel_id=1, source_target_pairs={{0,6},{1,7},{2,4},{3,5},{4,2},{5,3},{6,0},{7,1},{8,14},{9,15},{10,... | collective-permute-start | bytes 786440 | tf_op jit(solution)/shard_map/ppermute | solution.py:25
  31.3 27.1 %collective-permute-start.6 = (bf16[64,2048]{1,0:T(8,128)(2,1)S(1)}, bf16[64,2048]{1,0:T(8,128)(2,1)S(1)}, u32[]{:S(2)}, u32[]{:S(2)}) collective-permute-start(bf16[64,2048]{1,0:T(8,128)(2,1)S(1)} %get-tuple-element.52), channel_id=1, source_target_pairs={{0,7},{1,6},{2,5},{3,4},{4,3},{5,2},{6,1},{7,0},{8,15},{9,14},{10,... | collective-permute-start | bytes 786440 | tf_op jit(solution)/shard_map/ppermute | solution.py:25
  34.8 20.8 %collective-permute-start.12 = (bf16[512,128]{1,0:T(8,128)(2,1)S(1)}, bf16[512,128]{1,0:T(8,128)(2,1)S(1)}, u32[]{:S(2)}, u32[]{:S(2)}) collective-permute-start(bf16[512,128]{1,0:T(8,128)(2,1)S(1)} %collective-permute-done.10.refs_5_), channel_id=1, source_target_pairs={{0,8},{8,0},{16,24},{24,16},{1,9},{9,1},{17,25},{25,17},{2,10},{10... | collective-permute-start | bytes 393224 | tf_op jit(solution)/shard_map/ppermute | solution.py:25
  35.9 21.3 %collective-permute-start.9 = (bf16[512,128]{1,0:T(8,128)(2,1)S(1)}, bf16[512,128]{1,0:T(8,128)(2,1)S(1)}, u32[]{:S(2)}, u32[]{:S(2)}) collective-permute-start(bf16[512,128]{1,0:T(8,128)(2,1)S(1)} %collective-permute-done.7.refs_1_), channel_id=1, source_target_pairs={{0,16},{8,24},{16,0},{24,8},{1,17},{9,25},{17,1},{25,9},{2,18},{10... | collective-permute-start | bytes 393224 | tf_op jit(solution)/shard_map/ppermute | solution.py:25
  53.6 15.2 %collective-permute-start.16 = (bf16[512,256]{1,0:T(8,128)(2,1)S(1)}, bf16[512,256]{1,0:T(8,128)(2,1)S(1)}, u32[]{:S(2)}, u32[]{:S(2)}) collective-permute-start(bf16[512,256]{1,0:T(8,128)(2,1)S(1)} %get-tuple-element.55.refs_0_), channel_id=1, source_target_pairs={{0,8},{8,0},{16,24},{24,16},{1,9},{9,1},{17,25},{25,17},{2,10},{10... | collective-permute-start | bytes 786440 | tf_op jit(solution)/shard_map/ppermute | solution.py:25
  55.1 15.0 %collective-permute-start.19 = (bf16[512,256]{1,0:T(8,128)(2,1)S(1)}, bf16[512,256]{1,0:T(8,128)(2,1)S(1)}, u32[]{:S(2)}, u32[]{:S(2)}) collective-permute-start(bf16[512,256]{1,0:T(8,128)(2,1)S(1)} %get-tuple-element.56.refs_4_), channel_id=1, source_target_pairs={{0,16},{8,24},{16,0},{24,8},{1,17},{9,25},{17,1},{25,9},{2,18},{10... | collective-permute-start | bytes 786440 | tf_op jit(solution)/shard_map/ppermute | solution.py:25
  55.7 15.3 %collective-permute-start.17 = (bf16[512,256]{1,0:T(8,128)(2,1)S(1)}, bf16[512,256]{1,0:T(8,128)(2,1)S(1)}, u32[]{:S(2)}, u32[]{:S(2)}) collective-permute-start(bf16[512,256]{1,0:T(8,128)(2,1)S(1)} %get-tuple-element.55.refs_0_), channel_id=1, source_target_pairs={{0,16},{8,24},{16,0},{24,8},{1,17},{9,25},{17,1},{25,9},{2,18},{10... | collective-permute-start | bytes 786440 | tf_op jit(solution)/shard_map/ppermute | solution.py:25
  57.2 15.0 %collective-permute-start.20 = (bf16[512,256]{1,0:T(8,128)(2,1)S(1)}, bf16[512,256]{1,0:T(8,128)(2,1)S(1)}, u32[]{:S(2)}, u32[]{:S(2)}) collective-permute-start(bf16[512,256]{1,0:T(8,128)(2,1)S(1)} %get-tuple-element.56.refs_4_), channel_id=1, source_target_pairs={{0,8},{8,0},{16,24},{24,16},{1,9},{9,1},{17,25},{25,17},{2,10},{10... | collective-permute-start | bytes 786440 | tf_op jit(solution)/shard_map/ppermute | solution.py:25
  58.5 54.6 %collective-permute-start.14 = (bf16[2048,256]{1,0:T(8,128)(2,1)S(1)}, bf16[2048,256]{1,0:T(8,128)(2,1)S(1)}, u32[]{:S(2)}, u32[]{:S(2)}) collective-permute-start(bf16[2048,256]{1,0:T(8,128)(2,1)S(1)} %shard_map.67.refs_0_), channel_id=1, source_target_pairs={{0,2},{1,3},{2,0},{3,1},{4,6},{5,7},{6,4},{7,5},{8,10},{9,11},{10,... | collective-permute-start | bytes 3145736 | tf_op jit(solution)/shard_map/ppermute | solution.py:25
  68.9 35.9 %collective-permute-start.32 = (bf16[512,768]{1,0:T(8,128)(2,1)S(1)}, bf16[512,768]{1,0:T(8,128)(2,1)S(1)}, u32[]{:S(2)}, u32[]{:S(2)}) collective-permute-start(bf16[512,768]{1,0:T(8,128)(2,1)S(1)} %get-tuple-element.68.refs_0_), channel_id=1, source_target_pairs={{0,8},{8,0},{16,24},{24,16},{1,9},{9,1},{17,25},{25,17},{2,10},{10... | collective-permute-start | bytes 2359304 | tf_op jit(solution)/shard_map/ppermute | solution.py:25
  70.2 35.1 %collective-permute-start.34 = (bf16[512,768]{1,0:T(8,128)(2,1)S(1)}, bf16[512,768]{1,0:T(8,128)(2,1)S(1)}, u32[]{:S(2)}, u32[]{:S(2)}) collective-permute-start(bf16[512,768]{1,0:T(8,128)(2,1)S(1)} %get-tuple-element.69.refs_3_), channel_id=1, source_target_pairs={{0,16},{8,24},{16,0},{24,8},{1,17},{9,25},{17,1},{25,9},{2,18},{10... | collective-permute-start | bytes 2359304 | tf_op jit(solution)/shard_map/ppermute | solution.py:25
  70.9 25.3 %collective-permute-start.18 = (bf16[512,256]{1,0:T(8,128)(2,1)S(1)}, bf16[512,256]{1,0:T(8,128)(2,1)S(1)}, u32[]{:S(2)}, u32[]{:S(2)}) collective-permute-start(bf16[512,256]{1,0:T(8,128)(2,1)S(1)} %collective-permute-done.16.refs_1_), channel_id=1, source_target_pairs={{0,16},{8,24},{16,0},{24,8},{1,17},{9,25},{17,1},{25,9},{2,18},{10... | collective-permute-start | bytes 786440 | tf_op jit(solution)/shard_map/ppermute | solution.py:25
  72.2 40.9 %collective-permute-start.36 = (bf16[512,768]{1,0:T(8,128)(2,1)S(1)}, bf16[512,768]{1,0:T(8,128)(2,1)S(1)}, u32[]{:S(2)}, u32[]{:S(2)}) collective-permute-start(bf16[512,768]{1,0:T(8,128)(2,1)S(1)} %get-tuple-element.68.refs_0_), channel_id=1, source_target_pairs={{0,16},{8,24},{16,0},{24,8},{1,17},{9,25},{17,1},{25,9},{2,18},{10... | collective-permute-start | bytes 2359304 | tf_op jit(solution)/shard_map/ppermute | solution.py:25
  96.2 7.2 %collective-permute-start.21 = (bf16[512,256]{1,0:T(8,128)(2,1)S(1)}, bf16[512,256]{1,0:T(8,128)(2,1)S(1)}, u32[]{:S(2)}, u32[]{:S(2)}) collective-permute-start(bf16[512,256]{1,0:T(8,128)(2,1)S(1)} %collective-permute-done.19.refs_5_), channel_id=1, source_target_pairs={{0,8},{8,0},{16,24},{24,16},{1,9},{9,1},{17,25},{25,17},{2,10},{10... | collective-permute-start | bytes 786440 | tf_op jit(solution)/shard_map/ppermute | solution.py:25
  103.4 20.4 %collective-permute-start.37 = (bf16[512,768]{1,0:T(8,128)(2,1)S(1)}, bf16[512,768]{1,0:T(8,128)(2,1)S(1)}, u32[]{:S(2)}, u32[]{:S(2)}) collective-permute-start(bf16[512,768]{1,0:T(8,128)(2,1)S(1)} %get-tuple-element.69.refs_3_), channel_id=1, source_target_pairs={{0,8},{8,0},{16,24},{24,16},{1,9},{9,1},{17,25},{25,17},{2,10},{10... | collective-permute-start | bytes 2359304 | tf_op jit(solution)/shard_map/ppermute | solution.py:25
  104.8 23.8 %collective-permute-start.33 = (bf16[512,768]{1,0:T(8,128)(2,1)S(1)}, bf16[512,768]{1,0:T(8,128)(2,1)S(1)}, u32[]{:S(2)}, u32[]{:S(2)}) collective-permute-start(bf16[512,768]{1,0:T(8,128)(2,1)S(1)} %collective-permute-done.32.refs_1_), channel_id=1, source_target_pairs={{0,16},{8,24},{16,0},{24,8},{1,17},{9,25},{17,1},{25,9},{2,18},{10... | collective-permute-start | bytes 2359304 | tf_op jit(solution)/shard_map/ppermute | solution.py:25
  105.3 32.1 %collective-permute-start.35 = (bf16[512,768]{1,0:T(8,128)(2,1)S(1)}, bf16[512,768]{1,0:T(8,128)(2,1)S(1)}, u32[]{:S(2)}, u32[]{:S(2)}) collective-permute-start(bf16[512,768]{1,0:T(8,128)(2,1)S(1)} %collective-permute-done.34.refs_4_), channel_id=1, source_target_pairs={{0,8},{8,0},{16,24},{24,16},{1,9},{9,1},{17,25},{25,17},{2,10},{10... | collective-permute-start | bytes 2359304 | tf_op jit(solution)/shard_map/ppermute | solution.py:25
  113.1 28.2 %collective-permute-start.13 = (bf16[2048,256]{1,0:T(8,128)(2,1)S(1)}, bf16[2048,256]{1,0:T(8,128)(2,1)S(1)}, u32[]{:S(2)}, u32[]{:S(2)}) collective-permute-start(bf16[2048,256]{1,0:T(8,128)(2,1)S(1)} %shard_map.67.refs_0_), channel_id=1, source_target_pairs={{0,1},{1,0},{2,3},{3,2},{4,5},{5,4},{6,7},{7,6},{8,9},{9,8},{10,11... | collective-permute-start | bytes 3145736 | tf_op jit(solution)/shard_map/ppermute | solution.py:25
  113.1 31.1 %collective-permute-start.15 = (bf16[2048,256]{1,0:T(8,128)(2,1)S(1)}, bf16[2048,256]{1,0:T(8,128)(2,1)S(1)}, u32[]{:S(2)}, u32[]{:S(2)}) collective-permute-start(bf16[2048,256]{1,0:T(8,128)(2,1)S(1)} %collective-permute-done.14.refs_0_), channel_id=1, source_target_pairs={{0,1},{1,0},{2,3},{3,2},{4,5},{5,4},{6,7},{7,6},{8,9},{9,8},{10,11... | collective-permute-start | bytes 3145736 | tf_op jit(solution)/shard_map/ppermute | solution.py:25
  123.9 33.8 %collective-permute-start.22 = (bf16[2,128,128]{2,1,0:T(8,128)(2,1)S(1)}, bf16[2,128,128]{2,1,0:T(8,128)(2,1)S(1)}, u32[]{:S(2)}, u32[]{:S(2)}) collective-permute-start(bf16[2,128,128]{2,1,0:T(8,128)(2,1)S(1)} %get-tuple-element.59), channel_id=1, source_target_pairs={{0,8},{8,0},{16,24},{24,16},{1,9},{9,1},{17,25},{25,17},{2,10},{10... | collective-permute-start | bytes 196616 | tf_op jit(solution)/shard_map/ppermute | solution.py:25
  139.3 10.4 %collective-permute-start.38 = (bf16[6,128,128]{2,1,0:T(8,128)(2,1)S(1)}, bf16[6,128,128]{2,1,0:T(8,128)(2,1)S(1)}, u32[]{:S(2)}, u32[]{:S(2)}) collective-permute-start(bf16[6,128,128]{2,1,0:T(8,128)(2,1)S(1)} %get-tuple-element.74), channel_id=1, source_target_pairs={{0,8},{8,0},{16,24},{24,16},{1,9},{9,1},{17,25},{25,17},{2,10},{10... | collective-permute-start | bytes 589832 | tf_op jit(solution)/shard_map/ppermute | solution.py:25
  140.7 10.9 %collective-permute-start.39 = (bf16[6,128,128]{2,1,0:T(8,128)(2,1)S(1)}, bf16[6,128,128]{2,1,0:T(8,128)(2,1)S(1)}, u32[]{:S(2)}, u32[]{:S(2)}) collective-permute-start(bf16[6,128,128]{2,1,0:T(8,128)(2,1)S(1)} %get-tuple-element.74), channel_id=1, source_target_pairs={{0,16},{8,24},{16,0},{24,8},{1,17},{9,25},{17,1},{25,9},{2,18},{10... | collective-permute-start | bytes 589832 | tf_op jit(solution)/shard_map/ppermute | solution.py:25
  141.3 10.3 %collective-permute-start.40 = (bf16[6,128,128]{2,1,0:T(8,128)(2,1)S(1)}, bf16[6,128,128]{2,1,0:T(8,128)(2,1)S(1)}, u32[]{:S(2)}, u32[]{:S(2)}) collective-permute-start(bf16[6,128,128]{2,1,0:T(8,128)(2,1)S(1)} %get-tuple-element.74), channel_id=1, source_target_pairs={{0,24},{8,16},{16,8},{24,0},{1,25},{9,17},{17,9},{25,1},{2,26},{10... | collective-permute-start | bytes 589832 | tf_op jit(solution)/shard_map/ppermute | solution.py:25
  144.2 13.5 %collective-permute-start.23 = (bf16[2,128,128]{2,1,0:T(8,128)(2,1)S(1)}, bf16[2,128,128]{2,1,0:T(8,128)(2,1)S(1)}, u32[]{:S(2)}, u32[]{:S(2)}) collective-permute-start(bf16[2,128,128]{2,1,0:T(8,128)(2,1)S(1)} %get-tuple-element.59), channel_id=1, source_target_pairs={{0,16},{8,24},{16,0},{24,8},{1,17},{9,25},{17,1},{25,9},{2,18},{10... | collective-permute-start | bytes 196616 | tf_op jit(solution)/shard_map/ppermute | solution.py:25
  149.8 8.0 %collective-permute-start.24 = (bf16[2,128,128]{2,1,0:T(8,128)(2,1)S(1)}, bf16[2,128,128]{2,1,0:T(8,128)(2,1)S(1)}, u32[]{:S(2)}, u32[]{:S(2)}) collective-permute-start(bf16[2,128,128]{2,1,0:T(8,128)(2,1)S(1)} %get-tuple-element.59), channel_id=1, source_target_pairs={{0,24},{8,16},{16,8},{24,0},{1,25},{9,17},{17,9},{25,1},{2,26},{10... | collective-permute-start | bytes 196616 | tf_op jit(solution)/shard_map/ppermute | solution.py:25
  153.0 10.4 %collective-permute-start.41 = (bf16[64,768]{1,0:T(8,128)(2,1)S(1)}, bf16[64,768]{1,0:T(8,128)(2,1)S(1)}, u32[]{:S(2)}, u32[]{:S(2)}) collective-permute-start(bf16[64,768]{1,0:T(8,128)(2,1)S(1)} %get-tuple-element.76), channel_id=1, source_target_pairs={{0,1},{1,0},{2,3},{3,2},{4,5},{5,4},{6,7},{7,6},{8,9},{9,8},{10,11... | collective-permute-start | bytes 294920 | tf_op jit(solution)/shard_map/ppermute | solution.py:25
  153.1 12.5 %collective-permute-start.42 = (bf16[64,768]{1,0:T(8,128)(2,1)S(1)}, bf16[64,768]{1,0:T(8,128)(2,1)S(1)}, u32[]{:S(2)}, u32[]{:S(2)}) collective-permute-start(bf16[64,768]{1,0:T(8,128)(2,1)S(1)} %get-tuple-element.77), channel_id=1, source_target_pairs={{0,2},{1,3},{2,0},{3,1},{4,6},{5,7},{6,4},{7,5},{8,10},{9,11},{10,... | collective-permute-start | bytes 294920 | tf_op jit(solution)/shard_map/ppermute | solution.py:25
  158.8 1.9 %collective-permute-start.25 = (bf16[64,256]{1,0:T(8,128)(2,1)S(1)}, bf16[64,256]{1,0:T(8,128)(2,1)S(1)}, u32[]{:S(2)}, u32[]{:S(2)}) collective-permute-start(bf16[64,256]{1,0:T(8,128)(2,1)S(1)} %get-tuple-element.61), channel_id=1, source_target_pairs={{0,1},{1,0},{2,3},{3,2},{4,5},{5,4},{6,7},{7,6},{8,9},{9,8},{10,11... | collective-permute-start | bytes 98312 | tf_op jit(solution)/shard_map/ppermute | solution.py:25
  159.0 4.3 %collective-permute-start.26 = (bf16[64,256]{1,0:T(8,128)(2,1)S(1)}, bf16[64,256]{1,0:T(8,128)(2,1)S(1)}, u32[]{:S(2)}, u32[]{:S(2)}) collective-permute-start(bf16[64,256]{1,0:T(8,128)(2,1)S(1)} %get-tuple-element.62), channel_id=1, source_target_pairs={{0,2},{1,3},{2,0},{3,1},{4,6},{5,7},{6,4},{7,5},{8,10},{9,11},{10,... | collective-permute-start | bytes 98312 | tf_op jit(solution)/shard_map/ppermute | solution.py:25
  159.3 8.5 %collective-permute-start.43 = (bf16[64,768]{1,0:T(8,128)(2,1)S(1)}, bf16[64,768]{1,0:T(8,128)(2,1)S(1)}, u32[]{:S(2)}, u32[]{:S(2)}) collective-permute-start(bf16[64,768]{1,0:T(8,128)(2,1)S(1)} %get-tuple-element.78), channel_id=1, source_target_pairs={{0,3},{1,2},{2,1},{3,0},{4,7},{5,6},{6,5},{7,4},{8,11},{9,10},{10,... | collective-permute-start | bytes 294920 | tf_op jit(solution)/shard_map/ppermute | solution.py:25
  160.7 15.0 %collective-permute-start.44 = (bf16[64,768]{1,0:T(8,128)(2,1)S(1)}, bf16[64,768]{1,0:T(8,128)(2,1)S(1)}, u32[]{:S(2)}, u32[]{:S(2)}) collective-permute-start(bf16[64,768]{1,0:T(8,128)(2,1)S(1)} %get-tuple-element.79), channel_id=1, source_target_pairs={{0,4},{1,5},{2,6},{3,7},{4,0},{5,1},{6,2},{7,3},{8,12},{9,13},{10,... | collective-permute-start | bytes 294920 | tf_op jit(solution)/shard_map/ppermute | solution.py:25
  163.2 13.7 %collective-permute-start.45 = (bf16[64,768]{1,0:T(8,128)(2,1)S(1)}, bf16[64,768]{1,0:T(8,128)(2,1)S(1)}, u32[]{:S(2)}, u32[]{:S(2)}) collective-permute-start(bf16[64,768]{1,0:T(8,128)(2,1)S(1)} %get-tuple-element.80), channel_id=1, source_target_pairs={{0,5},{1,4},{2,7},{3,6},{4,1},{5,0},{6,3},{7,2},{8,13},{9,12},{10,... | collective-permute-start | bytes 294920 | tf_op jit(solution)/shard_map/ppermute | solution.py:25
  163.4 13.6 %collective-permute-start.46 = (bf16[64,768]{1,0:T(8,128)(2,1)S(1)}, bf16[64,768]{1,0:T(8,128)(2,1)S(1)}, u32[]{:S(2)}, u32[]{:S(2)}) collective-permute-start(bf16[64,768]{1,0:T(8,128)(2,1)S(1)} %get-tuple-element.81), channel_id=1, source_target_pairs={{0,6},{1,7},{2,4},{3,5},{4,2},{5,3},{6,0},{7,1},{8,14},{9,15},{10,... | collective-permute-start | bytes 294920 | tf_op jit(solution)/shard_map/ppermute | solution.py:25
  165.6 13.7 %collective-permute-start.47 = (bf16[64,768]{1,0:T(8,128)(2,1)S(1)}, bf16[64,768]{1,0:T(8,128)(2,1)S(1)}, u32[]{:S(2)}, u32[]{:S(2)}) collective-permute-start(bf16[64,768]{1,0:T(8,128)(2,1)S(1)} %get-tuple-element.82), channel_id=1, source_target_pairs={{0,7},{1,6},{2,5},{3,4},{4,3},{5,2},{6,1},{7,0},{8,15},{9,14},{10,... | collective-permute-start | bytes 294920 | tf_op jit(solution)/shard_map/ppermute | solution.py:25
  167.7 14.8 %collective-permute-start.27 = (bf16[64,256]{1,0:T(8,128)(2,1)S(1)}, bf16[64,256]{1,0:T(8,128)(2,1)S(1)}, u32[]{:S(2)}, u32[]{:S(2)}) collective-permute-start(bf16[64,256]{1,0:T(8,128)(2,1)S(1)} %get-tuple-element.63), channel_id=1, source_target_pairs={{0,3},{1,2},{2,1},{3,0},{4,7},{5,6},{6,5},{7,4},{8,11},{9,10},{10,... | collective-permute-start | bytes 98312 | tf_op jit(solution)/shard_map/ppermute | solution.py:25
  175.7 9.4 %collective-permute-start.28 = (bf16[64,256]{1,0:T(8,128)(2,1)S(1)}, bf16[64,256]{1,0:T(8,128)(2,1)S(1)}, u32[]{:S(2)}, u32[]{:S(2)}) collective-permute-start(bf16[64,256]{1,0:T(8,128)(2,1)S(1)} %get-tuple-element.64), channel_id=1, source_target_pairs={{0,4},{1,5},{2,6},{3,7},{4,0},{5,1},{6,2},{7,3},{8,12},{9,13},{10,... | collective-permute-start | bytes 98312 | tf_op jit(solution)/shard_map/ppermute | solution.py:25
  177.0 8.1 %collective-permute-start.29 = (bf16[64,256]{1,0:T(8,128)(2,1)S(1)}, bf16[64,256]{1,0:T(8,128)(2,1)S(1)}, u32[]{:S(2)}, u32[]{:S(2)}) collective-permute-start(bf16[64,256]{1,0:T(8,128)(2,1)S(1)} %get-tuple-element.65), channel_id=1, source_target_pairs={{0,5},{1,4},{2,7},{3,6},{4,1},{5,0},{6,3},{7,2},{8,13},{9,12},{10,... | collective-permute-start | bytes 98312 | tf_op jit(solution)/shard_map/ppermute | solution.py:25
  177.0 8.1 %collective-permute-start.30 = (bf16[64,256]{1,0:T(8,128)(2,1)S(1)}, bf16[64,256]{1,0:T(8,128)(2,1)S(1)}, u32[]{:S(2)}, u32[]{:S(2)}) collective-permute-start(bf16[64,256]{1,0:T(8,128)(2,1)S(1)} %get-tuple-element.66), channel_id=1, source_target_pairs={{0,6},{1,7},{2,4},{3,5},{4,2},{5,3},{6,0},{7,1},{8,14},{9,15},{10,... | collective-permute-start | bytes 98312 | tf_op jit(solution)/shard_map/ppermute | solution.py:25
  179.3 5.8 %collective-permute-start.31 = (bf16[64,256]{1,0:T(8,128)(2,1)S(1)}, bf16[64,256]{1,0:T(8,128)(2,1)S(1)}, u32[]{:S(2)}, u32[]{:S(2)}) collective-permute-start(bf16[64,256]{1,0:T(8,128)(2,1)S(1)} %get-tuple-element.67), channel_id=1, source_target_pairs={{0,7},{1,6},{2,5},{3,4},{4,3},{5,2},{6,1},{7,0},{8,15},{9,14},{10,... | collective-permute-start | bytes 98312 | tf_op jit(solution)/shard_map/ppermute | solution.py:25
